TPU v7x, 256 devices: a whole 4x4x8 slice. The times are simulated.
256 devices in a mesh: rows: 32 (over z, x_lo, core), cols: 8 (over y, x_hi).
Axes of the slice: x: 4 (x_hi: 2, x_lo: 2; x = x_hi * 2 + x_lo), y: 4, z: 8, core: 2. Of those that a mesh axis runs over, the one named last changes fastest.
Arguments:
- kets: float32 [32, 16, 32], P('rows', 'cols'), may hold values from -3 to 3
- left_maps: float32 [2, 32, 16, 96, 384], P(None, 'rows', 'cols'), may hold values from -0.3125 to 0.3125
- right_maps: float32 [2, 32, 16, 96, 384], P(None, 'rows', 'cols'), may hold values from -0.3125 to 0.3125
- top_edge: float32 [16, 96, 384], P('cols'), may hold values from -6 to 6
- bottom_edge: float32 [16, 96, 384], P('cols'), may hold values from -6 to 6
- left_edge: float32 [32, 96, 384], P('rows'), may hold values from -6 to 6
- right_edge: float32 [32, 96, 384], P('rows'), may hold values from -6 to 6
- term_rows: int32 [16], replicated, may hold values from 0 to 31
- term_bonds: int32 [16], replicated, may hold values from 0 to 14
- term_ops: int32 [16], replicated, may hold values from 0 to 3
- operators: float32 [4, 16], replicated, may hold values from -6 to 6
Outputs:
- top_out: float32 [32, 16, 96, 384], P('rows', 'cols')
- bottom_out: float32 [32, 16, 96, 384], P('rows', 'cols')
- energies: float32 [16], replicated
Inputs may be any that keep to these rules, and one draw needn't show every extreme that they name: Term t acts on the bond between columns term_bonds[t] and term_bonds[t] + 1 of row term_rows[t].
All inputs are finite; a program needn't handle non-finite values.
Results may differ from a plain program's by a relative error of at most 0.0003.
Values sent between devices are 32-bit elements; how exact they have to be, the bound alone decides.
A program may use at most 64 MiB of HBM per device.

v0:
```python
import jax
import jax.numpy as jnp
from jax import lax
from jax.sharding import Mesh
from jax.sharding import PartitionSpec as P

D = 2
D2 = 4
PHYS = 2
CHI = 96
OPS = 4
TERMS = 16
ROWS = ("rows_0", "rows_1", "rows_2")
COLS = ("cols_0", "cols_1")
ROWS_COLS = ("rows_0", "rows_1", "rows_2", "cols_0", "cols_1")


EPSILON = 1e-06
PRECISION_HIGH = lax.Precision.HIGHEST


def shifted(value, axis, steps):
    count = lax.axis_size(axis)
    initial, last = (max(0, -steps), min(count, count - steps))
    return lax.ppermute(value, axis, [(source, source + steps) for source in range(initial, last)])


def over_axes(value, axes):
    for axis in axes:
        value = lax.psum(value, axis)
    return value


def product(pattern, former, latter):
    return jnp.einsum(
        pattern, former, latter, precision=PRECISION_HIGH, preferred_element_type=jnp.float32
    )


def normalize(values):
    return values / jnp.sqrt(jnp.mean(values * values) + EPSILON)


def select_at(values, position):
    return lax.dynamic_index_in_dim(values, position, 0, keepdims=False)


def pair_layers(ket_flat):
    tensor = ket_flat.reshape(PHYS, D, D, D, D)
    doubled = product("pabcd,pefgh->aebfcgdh", tensor, tensor)
    return doubled.reshape(D2, D2, D2, D2)


def open_layers(ket_flat):
    tensor = ket_flat.reshape(PHYS, D, D, D, D)
    doubled = product("pabcd,qefgh->pqaebfcgdh", tensor, tensor)
    return doubled.reshape(PHYS * PHYS, D2, D2, D2, D2)


def pair_diagonal():
    matched = jnp.arange(PHYS)[:, None] == jnp.arange(PHYS)[None, :]
    return jnp.where(matched, 1.0, 0.0).astype(jnp.float32).reshape(PHYS * PHYS)


def absorb_down(boundary, layers, left_map, right_map):
    above_col = boundary.reshape(CHI, D2, CHI)
    left_three = left_map.reshape(CHI, CHI, D2)
    right_three = right_map.reshape(CHI, CHI, D2)
    joined = product("aub,cbr->aurc", above_col, right_three)
    through = product("aurc,uldr->aldc", joined, layers)
    renewed = product("xal,aldc->xdc", left_three, through)
    return normalize(renewed.reshape(CHI, D2 * CHI))


def absorb_up(boundary, layers, left_map, right_map):
    below_col = boundary.reshape(CHI, D2, CHI)
    left_three = left_map.reshape(CHI, CHI, D2)
    right_three = right_map.reshape(CHI, CHI, D2)
    joined = product("adb,cbr->adrc", below_col, right_three)
    through = product("adrc,uldr->aluc", joined, layers)
    renewed = product("xal,aluc->xuc", left_three, through)
    return normalize(renewed.reshape(CHI, D2 * CHI))


def left_core(environ, layers, above_col, below_col):
    env_three = environ.reshape(CHI, D2, CHI)
    upper_three = above_col.reshape(CHI, D2, CHI)
    lower_three = below_col.reshape(CHI, D2, CHI)
    step_one = product("alb,aux->lbux", env_three, upper_three)
    step_two = product("lbux,uldr->bxdr", step_one, layers)
    return product("bxdr,bdy->xry", step_two, lower_three).reshape(CHI, D2 * CHI)


def right_core(environ, layers, above_col, below_col):
    env_three = environ.reshape(CHI, D2, CHI)
    upper_three = above_col.reshape(CHI, D2, CHI)
    lower_three = below_col.reshape(CHI, D2, CHI)
    step_one = product("xry,aux->ryau", env_three, upper_three)
    step_two = product("ryau,uldr->yald", step_one, layers)
    return product("yald,bdy->alb", step_two, lower_three).reshape(CHI, D2 * CHI)


def side_step(core_map, environ, ket_flat, layers, above_col, below_col, wanted):

    def with_open(unused):
        opened = lax.map(
            lambda single: core_map(environ, single, above_col, below_col), open_layers(ket_flat)
        )
        closed = jnp.sum(pair_diagonal()[:, None, None] * opened, axis=0)
        return (opened, normalize(closed))

    def without_open(unused):
        empty_open = jnp.zeros((PHYS * PHYS, CHI, D2 * CHI), jnp.float32)
        return (empty_open, normalize(core_map(environ, layers, above_col, below_col)))

    return lax.cond(wanted, with_open, without_open, 0)


def shards(
    kets,
    left_maps,
    right_maps,
    top_edge,
    bottom_edge,
    left_edge,
    right_edge,
    term_rows,
    term_bonds,
    term_ops,
    operators,
):
    row_count = lax.axis_size(ROWS)
    row_place = lax.axis_index(ROWS)
    col_count = lax.axis_size(COLS)
    col_place = lax.axis_index(COLS)
    local_rows = kets.shape[0]
    local_cols = kets.shape[1]
    layers = jax.vmap(jax.vmap(pair_layers))(kets)
    column_shape = (CHI, D2 * CHI)
    blank_column = jnp.zeros(column_shape, jnp.float32)

    def run_down(source, column):
        current = source
        current = absorb_down(
            current,
            select_at(layers[0], column),
            select_at(left_maps[0, 0], column),
            select_at(right_maps[0, 0], column),
        )
        columns_out = [current]
        return jnp.stack(columns_out)

    def run_up(source, column):
        columns_out = [None] * local_rows
        current = source
        for local_row in reversed(range(local_rows)):
            current = absorb_up(
                current,
                select_at(layers[local_row], column),
                select_at(left_maps[1, local_row], column),
                select_at(right_maps[1, local_row], column),
            )
            columns_out[local_row] = current
        return jnp.stack(columns_out)

    def pipe_step(step_number, carried):
        from_above, from_below, enter_top, leave_top, enter_bottom, leave_bottom = carried
        slot_top = step_number - row_place
        column_top = jnp.clip(slot_top, 0, local_cols - 1)
        source_top = jnp.where(row_place == 0, select_at(top_edge, column_top), from_above)

        def down_live(stores):
            renewed = run_down(source_top, column_top)
            entered = lax.dynamic_update_index_in_dim(stores[0], source_top, column_top, 0)
            left_now = lax.dynamic_update_index_in_dim(stores[1], renewed, column_top, 1)
            return (entered, left_now, renewed[local_rows - 1])

        def down_spare(stores):
            return (stores[0], stores[1], blank_column)

        live_top = (slot_top >= 0) & (slot_top < local_cols)
        enter_top, leave_top, send_down = lax.cond(
            live_top, down_live, down_spare, (enter_top, leave_top)
        )
        slot_bottom = step_number - (row_count - 1 - row_place)
        column_bottom = jnp.clip(slot_bottom, 0, local_cols - 1)
        source_bottom = jnp.where(
            row_place == row_count - 1, select_at(bottom_edge, column_bottom), from_below
        )

        def up_live(stores):
            renewed = run_up(source_bottom, column_bottom)
            entered = lax.dynamic_update_index_in_dim(stores[0], source_bottom, column_bottom, 0)
            left_now = lax.dynamic_update_index_in_dim(stores[1], renewed, column_bottom, 1)
            return (entered, left_now, renewed[0])

        def up_spare(stores):
            return (stores[0], stores[1], blank_column)

        live_bottom = (slot_bottom >= 0) & (slot_bottom < local_cols)
        enter_bottom, leave_bottom, send_up = lax.cond(
            live_bottom, up_live, up_spare, (enter_bottom, leave_bottom)
        )
        from_above = shifted(send_down, ROWS, 1)
        from_below = shifted(send_up, ROWS, -1)
        return (from_above, from_below, enter_top, leave_top, enter_bottom, leave_bottom)

    entry_shape = (local_cols,) + column_shape
    store_shape = (local_rows, local_cols) + column_shape
    initial = (
        blank_column,
        blank_column,
        jnp.zeros(entry_shape, jnp.float32),
        jnp.zeros(store_shape, jnp.float32),
        jnp.zeros(entry_shape, jnp.float32),
        jnp.zeros(store_shape, jnp.float32),
    )
    unused_above, unused_below, enter_top, leave_top, enter_bottom, leave_bottom = lax.fori_loop(
        0, row_count + local_cols - 1, pipe_step, initial
    )
    above = jnp.concatenate([enter_top[None], leave_top[:-1]], axis=0)
    below = jnp.concatenate([leave_bottom[1:], enter_bottom[None]], axis=0)
    global_rows = row_place * local_rows + jnp.arange(local_rows, dtype=jnp.int32)
    global_cols = col_place * local_cols + jnp.arange(local_cols, dtype=jnp.int32)
    row_match = term_rows[:, None] == global_rows[None, :]
    site_match = row_match[:, :, None] & (term_bonds[:, None, None] == global_cols[None, None, :])
    left_need = jnp.any(site_match, axis=0)
    right_need = jnp.any(
        row_match[:, :, None] & (term_bonds[:, None, None] == global_cols[None, None, :] - 1),
        axis=0,
    )
    rows_shape = (local_rows,) + column_shape
    edge_shape = (local_rows, PHYS * PHYS) + column_shape
    open_shape = (local_rows, local_cols, PHYS * PHYS) + column_shape

    def chain_step(section_number, carried):
        from_left, from_right, edge_in, left_opens, right_opens, edge_open = carried

        def left_live(stores):
            source = jnp.where(col_place == 0, left_edge, from_left)
            environ = source[0]
            row_open = []
            for column in range(local_cols):
                opened, environ = side_step(
                    left_core,
                    environ,
                    kets[0, column],
                    layers[0, column],
                    above[0, column],
                    below[0, column],
                    left_need[0, column],
                )
                row_open.append(opened)
            opened_rows = [jnp.stack(row_open)]
            sent_rows = [environ]
            return (jnp.stack(opened_rows), jnp.stack(sent_rows))

        def left_spare(stores):
            return (stores, jnp.zeros(rows_shape, jnp.float32))

        left_opens, sent_left = lax.cond(
            section_number == col_place, left_live, left_spare, left_opens
        )

        def right_live(stores):
            source = jnp.where(col_place == col_count - 1, right_edge, from_right)
            environ = source[0]
            row_open = [None] * local_cols
            for column in reversed(range(local_cols)):
                opened, environ = side_step(
                    right_core,
                    environ,
                    kets[0, column],
                    layers[0, column],
                    above[0, column],
                    below[0, column],
                    right_need[0, column],
                )
                row_open[column] = opened
            opened_rows = [jnp.stack(row_open)]
            sent_rows = [environ]
            kept_edge = stores[1]
            return (jnp.stack(opened_rows), kept_edge, jnp.stack(sent_rows))

        def right_spare(stores):
            return (stores[0], stores[1], jnp.zeros(rows_shape, jnp.float32))

        right_opens, edge_open, sent_right = lax.cond(
            section_number == col_count - 1 - col_place,
            right_live,
            right_spare,
            (right_opens, edge_open),
        )
        from_left = shifted(sent_left, COLS, 1)
        from_right = shifted(sent_right, COLS, -1)
        return (from_left, from_right, edge_in, left_opens, right_opens, edge_open)

    chain_start = (
        jnp.zeros(rows_shape, jnp.float32),
        jnp.zeros(rows_shape, jnp.float32),
        jnp.zeros(edge_shape, jnp.float32),
        jnp.zeros(open_shape, jnp.float32),
        jnp.zeros(open_shape, jnp.float32),
        jnp.zeros(edge_shape, jnp.float32),
    )
    unused_left, unused_right, unused_edge, left_opens, right_opens, edge_open = lax.fori_loop(
        0, col_count, chain_step, chain_start
    )
    edge_open = shifted(right_opens[:, 0], COLS, -1)
    partner = jnp.concatenate([right_opens[:, 1:], edge_open[:, None]], axis=1)
    flat_left = left_opens.reshape(local_rows * local_cols, PHYS * PHYS, -1)
    flat_right = partner.reshape(local_rows * local_cols, PHYS * PHYS, -1)
    density = product("kpz,kqz->kpq", flat_left, flat_right).reshape(local_rows * local_cols, -1)
    diagonal = pair_diagonal()
    weights = jnp.outer(diagonal, diagonal).reshape(-1)
    trace_value = jnp.sum(density * weights[None, :], axis=1)
    spread = jnp.sqrt(jnp.sum(density * density, axis=1))
    valid_bond = left_need.reshape(-1)
    denominator = jnp.where(valid_bond, jnp.maximum(jnp.abs(trace_value), 0.25 * spread), 1.0)
    scaled = density / denominator[:, None]
    chooser = jnp.where(site_match.reshape(TERMS, -1), 1.0, 0.0).astype(jnp.float32)
    chosen = jnp.dot(chooser, scaled, precision=PRECISION_HIGH, preferred_element_type=jnp.float32)
    op_match = jnp.where(
        term_ops[:, None] == jnp.arange(OPS, dtype=jnp.int32)[None, :], 1.0, 0.0
    ).astype(jnp.float32)
    picked = jnp.dot(
        op_match, operators, precision=PRECISION_HIGH, preferred_element_type=jnp.float32
    )
    term_share = jnp.sum(chosen * picked, axis=1)
    energies = over_axes(term_share, ROWS_COLS)
    return (leave_top, leave_bottom, energies)


def solution(mesh):
    torus = Mesh(
        mesh.devices.reshape(8, 2, 2, 4, 2), ("rows_0", "rows_1", "rows_2", "cols_0", "cols_1")
    )
    placed = (
        P(ROWS, COLS, None),
        P(None, ROWS, COLS, None, None),
        P(None, ROWS, COLS, None, None),
        P(COLS, None, None),
        P(COLS, None, None),
        P(ROWS, None, None),
        P(ROWS, None, None),
        P(),
        P(),
        P(),
        P(),
    )
    return jax.shard_map(
        shards,
        mesh=torus,
        in_specs=placed,
        out_specs=(P(ROWS, COLS, None, None), P(ROWS, COLS, None, None), P()),
        check_vma=False,
    )
```

profile of v0, /device:TPU:8, one launch (start us, length us, event | category | flops | bytes accessed | tf_op | source)
XLA Modules:
  0.0 1136.0 jit_solution(6941940179682645546)
XLA Ops:
  10.7 626.6 %while.90 = (s32[]{:T(128)}, f32[96,384]{1,0:T(8,128)S(1)}, f32[96,384]{1,0:T(8,128)}, f32[2,96,384]{2,1,0:T(8,128)S(1)}, f32[1,2,96,384]{3,2,1,0:T(8,128)}, /*i...) while((s32[]{:T(128)}, f32[96,384]{1,0:T(8,128)S(1)}, ...), condition=%wide.region_7.8_spmd, body=%wide.region_0.7_spmd.sunk | while | flops 736395264 | bytes 20592360 | solution.py:218
  71.3 15.6 %collective-permute-start = (f32[96,384]{1,0:T(8,128)}, f32[96,384]{1,0:T(8,128)S(1)}, u32[]{:S(2)}, u32[]{:S(2)}) collective-permute-start(f32[96,384]{1,0:T(8,128)} %get-tuple-element.1732), channel_id=1, source_target_pairs={{0,8},{8,16},{16,24},{24,32},{32,40},{40,48},{48,56},{56,64},{64,7... | collective-permute-start | bytes 442376 | tf_op jit(solution)/shard_map/while/body/eval_jaxpr/ppermute | solution.py:25
  100.7 14.1 %collective-permute-start = (f32[96,384]{1,0:T(8,128)}, f32[96,384]{1,0:T(8,128)S(1)}, u32[]{:S(2)}, u32[]{:S(2)}) collective-permute-start(f32[96,384]{1,0:T(8,128)} %get-tuple-element.1732), channel_id=1, source_target_pairs={{0,8},{8,16},{16,24},{24,32},{32,40},{40,48},{48,56},{56,64},{64,7... | collective-permute-start | bytes 442376 | tf_op jit(solution)/shard_map/while/body/eval_jaxpr/ppermute | solution.py:25
  128.5 13.4 %collective-permute-start = (f32[96,384]{1,0:T(8,128)}, f32[96,384]{1,0:T(8,128)S(1)}, u32[]{:S(2)}, u32[]{:S(2)}) collective-permute-start(f32[96,384]{1,0:T(8,128)} %get-tuple-element.1732), channel_id=1, source_target_pairs={{0,8},{8,16},{16,24},{24,32},{32,40},{40,48},{48,56},{56,64},{64,7... | collective-permute-start | bytes 442376 | tf_op jit(solution)/shard_map/while/body/eval_jaxpr/ppermute | solution.py:25
  429.3 166.8 %collective-permute-start = (f32[96,384]{1,0:T(8,128)}, f32[96,384]{1,0:T(8,128)S(1)}, u32[]{:S(2)}, u32[]{:S(2)}) collective-permute-start(f32[96,384]{1,0:T(8,128)} %get-tuple-element.1732), channel_id=1, source_target_pairs={{0,8},{8,16},{16,24},{24,32},{32,40},{40,48},{48,56},{56,64},{64,7... | collective-permute-start | bytes 442376 | tf_op jit(solution)/shard_map/while/body/eval_jaxpr/ppermute | solution.py:25
  639.7 389.9 %while.91 = (s32[]{:T(128)}, f32[1,96,384]{2,1,0:T(8,128)S(1)}, f32[1,96,384]{2,1,0:T(8,128)S(1)}, f32[1,2,4,96,384]{4,3,2,1,0:T(8,128)}, f32[1,2,4,96,384]{4,3,...) while((s32[]{:T(128)}, f32[1,96,384]{2,1,0:T(8,128)S(1)}, ...), condition=%wide.region_43.44_spmd, body=%wide.region_10.43_spmd.sunk | while | flops 1474342912 | bytes 33713392 | solution.py:306
  639.9 14.3 %conditional.14 = (f32[1,2,4,96,384]{4,3,2,1,0:T(8,128)}, f32[1,96,384]{2,1,0:T(8,128)}) conditional(s32[]{:T(128)} %convert_element_type.66, f32[1,2,4,96,384]{4,3,2,1,0:T(8,128)} %get-tuple-element.1977, (pred[1,2]{1,0:T(4,128)(4,1)S(1)}, s32[]{:T(128)}, f32[1,96,384]{1,2,0:T(8,128)S(1)}, f32[1,96,384]{2,1,0:T(8,128)S(1)}, ...), branch_computations={%region_11.11_spmd, %region_12.26_spmd} | conditional | flops 737171456 | bytes 16268730 | solution.py:261
  672.9 14.1 %conditional.14 = (f32[1,2,4,96,384]{4,3,2,1,0:T(8,128)}, f32[1,96,384]{2,1,0:T(8,128)}) conditional(s32[]{:T(128)} %convert_element_type.66, f32[1,2,4,96,384]{4,3,2,1,0:T(8,128)} %get-tuple-element.1977, (pred[1,2]{1,0:T(4,128)(4,1)S(1)}, s32[]{:T(128)}, f32[1,96,384]{1,2,0:T(8,128)S(1)}, f32[1,96,384]{2,1,0:T(8,128)S(1)}, ...), branch_computations={%region_11.11_spmd, %region_12.26_spmd} | conditional | flops 737171456 | bytes 16268730 | solution.py:261
  695.3 14.7 %collective-permute-start.3 = (f32[1,96,384]{2,1,0:T(8,128)}, f32[1,96,384]{2,1,0:T(8,128)S(1)}, u32[]{:S(2)}, u32[]{:S(2)}) collective-permute-start(f32[1,96,384]{2,1,0:T(8,128)} %get-tuple-element.1754), channel_id=1, source_target_pairs={{1,0},{2,1},{3,2},{4,3},{5,4},{6,5},{7,6},{9,8},{10,9},{11,10},{12... | collective-permute-start | bytes 442376 | tf_op jit(solution)/shard_map/while/body/eval_jaxpr/ppermute | solution.py:25
  714.1 20.2 %conditional.14 = (f32[1,2,4,96,384]{4,3,2,1,0:T(8,128)}, f32[1,96,384]{2,1,0:T(8,128)}) conditional(s32[]{:T(128)} %convert_element_type.66, f32[1,2,4,96,384]{4,3,2,1,0:T(8,128)} %get-tuple-element.1977, (pred[1,2]{1,0:T(4,128)(4,1)S(1)}, s32[]{:T(128)}, f32[1,96,384]{1,2,0:T(8,128)S(1)}, f32[1,96,384]{2,1,0:T(8,128)S(1)}, ...), branch_computations={%region_11.11_spmd, %region_12.26_spmd} | conditional | flops 737171456 | bytes 16268730 | solution.py:261
  744.3 13.3 %collective-permute-done.3 = f32[1,96,384]{2,1,0:T(8,128)S(1)} collective-permute-done((f32[1,96,384]{2,1,0:T(8,128)}, f32[1,96,384]{2,1,0:T(8,128)S(1)}, u32[]{:S(2)}, u32[]{:S(2)}) %collective-permute-start.3) | collective-permute-done | bytes 147488 | tf_op jit(solution)/shard_map/while/body/eval_jaxpr/ppermute | solution.py:25
  757.8 14.2 %conditional.14 = (f32[1,2,4,96,384]{4,3,2,1,0:T(8,128)}, f32[1,96,384]{2,1,0:T(8,128)}) conditional(s32[]{:T(128)} %convert_element_type.66, f32[1,2,4,96,384]{4,3,2,1,0:T(8,128)} %get-tuple-element.1977, (pred[1,2]{1,0:T(4,128)(4,1)S(1)}, s32[]{:T(128)}, f32[1,96,384]{1,2,0:T(8,128)S(1)}, f32[1,96,384]{2,1,0:T(8,128)S(1)}, ...), branch_computations={%region_11.11_spmd, %region_12.26_spmd} | conditional | flops 737171456 | bytes 16268730 | solution.py:261
  772.0 28.4 %collective-permute-start.2 = (f32[1,96,384]{2,1,0:T(8,128)}, f32[1,96,384]{2,1,0:T(8,128)S(1)}, u32[]{:S(2)}, u32[]{:S(2)}) collective-permute-start(f32[1,96,384]{2,1,0:T(8,128)} %get-tuple-element.1753), channel_id=1, source_target_pairs={{0,1},{1,2},{2,3},{3,4},{4,5},{5,6},{6,7},{8,9},{9,10},{10,11},{11... | collective-permute-start | bytes 442376 | tf_op jit(solution)/shard_map/while/body/eval_jaxpr/ppermute | solution.py:25
  804.0 19.1 %collective-permute-done.3 = f32[1,96,384]{2,1,0:T(8,128)S(1)} collective-permute-done((f32[1,96,384]{2,1,0:T(8,128)}, f32[1,96,384]{2,1,0:T(8,128)S(1)}, u32[]{:S(2)}, u32[]{:S(2)}) %collective-permute-start.3) | collective-permute-done | bytes 147488 | tf_op jit(solution)/shard_map/while/body/eval_jaxpr/ppermute | solution.py:25
  823.6 14.1 %conditional.14 = (f32[1,2,4,96,384]{4,3,2,1,0:T(8,128)}, f32[1,96,384]{2,1,0:T(8,128)}) conditional(s32[]{:T(128)} %convert_element_type.66, f32[1,2,4,96,384]{4,3,2,1,0:T(8,128)} %get-tuple-element.1977, (pred[1,2]{1,0:T(4,128)(4,1)S(1)}, s32[]{:T(128)}, f32[1,96,384]{1,2,0:T(8,128)S(1)}, f32[1,96,384]{2,1,0:T(8,128)S(1)}, ...), branch_computations={%region_11.11_spmd, %region_12.26_spmd} | conditional | flops 737171456 | bytes 16268730 | solution.py:261
  837.7 25.0 %collective-permute-start.2 = (f32[1,96,384]{2,1,0:T(8,128)}, f32[1,96,384]{2,1,0:T(8,128)S(1)}, u32[]{:S(2)}, u32[]{:S(2)}) collective-permute-start(f32[1,96,384]{2,1,0:T(8,128)} %get-tuple-element.1753), channel_id=1, source_target_pairs={{0,1},{1,2},{2,3},{3,4},{4,5},{5,6},{6,7},{8,9},{9,10},{10,11},{11... | collective-permute-start | bytes 442376 | tf_op jit(solution)/shard_map/while/body/eval_jaxpr/ppermute | solution.py:25
  866.6 32.4 %collective-permute-done.3 = f32[1,96,384]{2,1,0:T(8,128)S(1)} collective-permute-done((f32[1,96,384]{2,1,0:T(8,128)}, f32[1,96,384]{2,1,0:T(8,128)S(1)}, u32[]{:S(2)}, u32[]{:S(2)}) %collective-permute-start.3) | collective-permute-done | bytes 147488 | tf_op jit(solution)/shard_map/while/body/eval_jaxpr/ppermute | solution.py:25
  899.2 14.3 %conditional.14 = (f32[1,2,4,96,384]{4,3,2,1,0:T(8,128)}, f32[1,96,384]{2,1,0:T(8,128)}) conditional(s32[]{:T(128)} %convert_element_type.66, f32[1,2,4,96,384]{4,3,2,1,0:T(8,128)} %get-tuple-element.1977, (pred[1,2]{1,0:T(4,128)(4,1)S(1)}, s32[]{:T(128)}, f32[1,96,384]{1,2,0:T(8,128)S(1)}, f32[1,96,384]{2,1,0:T(8,128)S(1)}, ...), branch_computations={%region_11.11_spmd, %region_12.26_spmd} | conditional | flops 737171456 | bytes 16268730 | solution.py:261
  918.3 19.9 %conditional.15 = (f32[1,2,4,96,384]{4,3,2,1,0:T(8,128)}, f32[1,96,384]{2,1,0:T(8,128)}) conditional(s32[]{:T(128)} %convert_element_type.67, f32[1,2,4,96,384]{4,3,2,1,0:T(8,128)} %get-tuple-element.1978, (pred[1,2]{1,0:T(4,128)(4,1)S(1)}, s32[]{:T(128)}, f32[1,96,384]{1,2,0:T(8,128)S(1)}, f32[1,96,384]{2,1,0:T(8,128)S(1)}, ...), branch_computations={%region_27.27_spmd, %region_28.42_spmd} | conditional | flops 737171456 | bytes 16264634 | solution.py:288
  947.2 14.2 %conditional.14 = (f32[1,2,4,96,384]{4,3,2,1,0:T(8,128)}, f32[1,96,384]{2,1,0:T(8,128)}) conditional(s32[]{:T(128)} %convert_element_type.66, f32[1,2,4,96,384]{4,3,2,1,0:T(8,128)} %get-tuple-element.1977, (pred[1,2]{1,0:T(4,128)(4,1)S(1)}, s32[]{:T(128)}, f32[1,96,384]{1,2,0:T(8,128)S(1)}, f32[1,96,384]{2,1,0:T(8,128)S(1)}, ...), branch_computations={%region_11.11_spmd, %region_12.26_spmd} | conditional | flops 737171456 | bytes 16268730 | solution.py:261
  965.1 24.6 %collective-permute-start.3 = (f32[1,96,384]{2,1,0:T(8,128)}, f32[1,96,384]{2,1,0:T(8,128)S(1)}, u32[]{:S(2)}, u32[]{:S(2)}) collective-permute-start(f32[1,96,384]{2,1,0:T(8,128)} %get-tuple-element.1754), channel_id=1, source_target_pairs={{1,0},{2,1},{3,2},{4,3},{5,4},{6,5},{7,6},{9,8},{10,9},{11,10},{12... | collective-permute-start | bytes 442376 | tf_op jit(solution)/shard_map/while/body/eval_jaxpr/ppermute | solution.py:25
  993.1 14.1 %conditional.14 = (f32[1,2,4,96,384]{4,3,2,1,0:T(8,128)}, f32[1,96,384]{2,1,0:T(8,128)}) conditional(s32[]{:T(128)} %convert_element_type.66, f32[1,2,4,96,384]{4,3,2,1,0:T(8,128)} %get-tuple-element.1977, (pred[1,2]{1,0:T(4,128)(4,1)S(1)}, s32[]{:T(128)}, f32[1,96,384]{1,2,0:T(8,128)S(1)}, f32[1,96,384]{2,1,0:T(8,128)S(1)}, ...), branch_computations={%region_11.11_spmd, %region_12.26_spmd} | conditional | flops 737171456 | bytes 16268730 | solution.py:261
  1031.7 19.3 %collective-permute-start.4 = (f32[1,4,96,384]{3,2,1,0:T(8,128)}, f32[1,4,96,384]{3,2,1,0:T(8,128)S(1)}, u32[]{:S(2)}, u32[]{:S(2)}) collective-permute-start(f32[1,4,96,384]{3,2,1,0:T(8,128)} %get-tuple-element.1421), channel_id=1, source_target_pairs={{1,0},{2,1},{3,2},{4,3},{5,4},{6,5},{7,6},{9,8},{10,9},{11,10},{12... | collective-permute-start | bytes 1769480 | tf_op jit(solution)/shard_map/ppermute | solution.py:25
  1065.6 43.4 %psum.35 = f32[16]{0:T(128)S(1)} all-reduce(f32[16]{0:T(128)S(1)} %fusion.86), channel_id=1, replica_groups=mesh['rows_0'=8,'rows_1'=2,'rows_2'=2,'cols_0'=4,'cols_1'=2] {'rows_0'}, use_global_device_ids=true, to_apply=%region_47.48 | all-reduce | flops 16 | bytes 128 | tf_op jit(solution)/shard_map/psum | solution.py:30
  (483 shorter events, 710.9 us)
Async XLA Ops:
  42.4 15.2 %collective-permute-start.1 = (f32[96,384]{1,0:T(8,128)}, f32[96,384]{1,0:T(8,128)}, u32[]{:S(2)}, u32[]{:S(2)}) collective-permute-start(f32[96,384]{1,0:T(8,128)} %get-tuple-element.1733), channel_id=1, source_target_pairs={{8,0},{16,8},{24,16},{32,24},{40,32},{48,40},{56,48},{64,56},{72,6... | collective-permute-start | bytes 442376 | tf_op jit(solution)/shard_map/while/body/eval_jaxpr/ppermute | solution.py:25
  69.3 17.6 %collective-permute-start.1 = (f32[96,384]{1,0:T(8,128)}, f32[96,384]{1,0:T(8,128)}, u32[]{:S(2)}, u32[]{:S(2)}) collective-permute-start(f32[96,384]{1,0:T(8,128)} %get-tuple-element.1733), channel_id=1, source_target_pairs={{8,0},{16,8},{24,16},{32,24},{40,32},{48,40},{56,48},{64,56},{72,6... | collective-permute-start | bytes 442376 | tf_op jit(solution)/shard_map/while/body/eval_jaxpr/ppermute | solution.py:25
  71.3 16.8 %collective-permute-start = (f32[96,384]{1,0:T(8,128)}, f32[96,384]{1,0:T(8,128)S(1)}, u32[]{:S(2)}, u32[]{:S(2)}) collective-permute-start(f32[96,384]{1,0:T(8,128)} %get-tuple-element.1732), channel_id=1, source_target_pairs={{0,8},{8,16},{16,24},{24,32},{32,40},{40,48},{48,56},{56,64},{64,7... | collective-permute-start | bytes 442376 | tf_op jit(solution)/shard_map/while/body/eval_jaxpr/ppermute | solution.py:25
  98.7 16.1 %collective-permute-start.1 = (f32[96,384]{1,0:T(8,128)}, f32[96,384]{1,0:T(8,128)}, u32[]{:S(2)}, u32[]{:S(2)}) collective-permute-start(f32[96,384]{1,0:T(8,128)} %get-tuple-element.1733), channel_id=1, source_target_pairs={{8,0},{16,8},{24,16},{32,24},{40,32},{48,40},{56,48},{64,56},{72,6... | collective-permute-start | bytes 442376 | tf_op jit(solution)/shard_map/while/body/eval_jaxpr/ppermute | solution.py:25
  100.7 15.3 %collective-permute-start = (f32[96,384]{1,0:T(8,128)}, f32[96,384]{1,0:T(8,128)S(1)}, u32[]{:S(2)}, u32[]{:S(2)}) collective-permute-start(f32[96,384]{1,0:T(8,128)} %get-tuple-element.1732), channel_id=1, source_target_pairs={{0,8},{8,16},{16,24},{24,32},{32,40},{40,48},{48,56},{56,64},{64,7... | collective-permute-start | bytes 442376 | tf_op jit(solution)/shard_map/while/body/eval_jaxpr/ppermute | solution.py:25
  126.6 15.4 %collective-permute-start.1 = (f32[96,384]{1,0:T(8,128)}, f32[96,384]{1,0:T(8,128)}, u32[]{:S(2)}, u32[]{:S(2)}) collective-permute-start(f32[96,384]{1,0:T(8,128)} %get-tuple-element.1733), channel_id=1, source_target_pairs={{8,0},{16,8},{24,16},{32,24},{40,32},{48,40},{56,48},{64,56},{72,6... | collective-permute-start | bytes 442376 | tf_op jit(solution)/shard_map/while/body/eval_jaxpr/ppermute | solution.py:25
  128.5 14.6 %collective-permute-start = (f32[96,384]{1,0:T(8,128)}, f32[96,384]{1,0:T(8,128)S(1)}, u32[]{:S(2)}, u32[]{:S(2)}) collective-permute-start(f32[96,384]{1,0:T(8,128)} %get-tuple-element.1732), channel_id=1, source_target_pairs={{0,8},{8,16},{16,24},{24,32},{32,40},{40,48},{48,56},{56,64},{64,7... | collective-permute-start | bytes 442376 | tf_op jit(solution)/shard_map/while/body/eval_jaxpr/ppermute | solution.py:25
  154.7 14.5 %collective-permute-start.1 = (f32[96,384]{1,0:T(8,128)}, f32[96,384]{1,0:T(8,128)}, u32[]{:S(2)}, u32[]{:S(2)}) collective-permute-start(f32[96,384]{1,0:T(8,128)} %get-tuple-element.1733), channel_id=1, source_target_pairs={{8,0},{16,8},{24,16},{32,24},{40,32},{48,40},{56,48},{64,56},{72,6... | collective-permute-start | bytes 442376 | tf_op jit(solution)/shard_map/while/body/eval_jaxpr/ppermute | solution.py:25
  209.3 14.7 %collective-permute-start.1 = (f32[96,384]{1,0:T(8,128)}, f32[96,384]{1,0:T(8,128)}, u32[]{:S(2)}, u32[]{:S(2)}) collective-permute-start(f32[96,384]{1,0:T(8,128)} %get-tuple-element.1733), channel_id=1, source_target_pairs={{8,0},{16,8},{24,16},{32,24},{40,32},{48,40},{56,48},{64,56},{72,6... | collective-permute-start | bytes 442376 | tf_op jit(solution)/shard_map/while/body/eval_jaxpr/ppermute | solution.py:25
  318.6 14.7 %collective-permute-start.1 = (f32[96,384]{1,0:T(8,128)}, f32[96,384]{1,0:T(8,128)}, u32[]{:S(2)}, u32[]{:S(2)}) collective-permute-start(f32[96,384]{1,0:T(8,128)} %get-tuple-element.1733), channel_id=1, source_target_pairs={{8,0},{16,8},{24,16},{32,24},{40,32},{48,40},{56,48},{64,56},{72,6... | collective-permute-start | bytes 442376 | tf_op jit(solution)/shard_map/while/body/eval_jaxpr/ppermute | solution.py:25
  427.3 168.8 %collective-permute-start.1 = (f32[96,384]{1,0:T(8,128)}, f32[96,384]{1,0:T(8,128)}, u32[]{:S(2)}, u32[]{:S(2)}) collective-permute-start(f32[96,384]{1,0:T(8,128)} %get-tuple-element.1733), channel_id=1, source_target_pairs={{8,0},{16,8},{24,16},{32,24},{40,32},{48,40},{56,48},{64,56},{72,6... | collective-permute-start | bytes 442376 | tf_op jit(solution)/shard_map/while/body/eval_jaxpr/ppermute | solution.py:25
  429.3 168.0 %collective-permute-start = (f32[96,384]{1,0:T(8,128)}, f32[96,384]{1,0:T(8,128)S(1)}, u32[]{:S(2)}, u32[]{:S(2)}) collective-permute-start(f32[96,384]{1,0:T(8,128)} %get-tuple-element.1732), channel_id=1, source_target_pairs={{0,8},{8,16},{16,24},{24,32},{32,40},{40,48},{48,56},{56,64},{64,7... | collective-permute-start | bytes 442376 | tf_op jit(solution)/shard_map/while/body/eval_jaxpr/ppermute | solution.py:25
  687.0 23.0 %collective-permute-start.2 = (f32[1,96,384]{2,1,0:T(8,128)}, f32[1,96,384]{2,1,0:T(8,128)S(1)}, u32[]{:S(2)}, u32[]{:S(2)}) collective-permute-start(f32[1,96,384]{2,1,0:T(8,128)} %get-tuple-element.1753), channel_id=1, source_target_pairs={{0,1},{1,2},{2,3},{3,4},{4,5},{5,6},{6,7},{8,9},{9,10},{10,11},{11... | collective-permute-start | bytes 442376 | tf_op jit(solution)/shard_map/while/body/eval_jaxpr/ppermute | solution.py:25
  695.3 18.6 %collective-permute-start.3 = (f32[1,96,384]{2,1,0:T(8,128)}, f32[1,96,384]{2,1,0:T(8,128)S(1)}, u32[]{:S(2)}, u32[]{:S(2)}) collective-permute-start(f32[1,96,384]{2,1,0:T(8,128)} %get-tuple-element.1754), channel_id=1, source_target_pairs={{1,0},{2,1},{3,2},{4,3},{5,4},{6,5},{7,6},{9,8},{10,9},{11,10},{12... | collective-permute-start | bytes 442376 | tf_op jit(solution)/shard_map/while/body/eval_jaxpr/ppermute | solution.py:25
  742.3 15.2 %collective-permute-start.3 = (f32[1,96,384]{2,1,0:T(8,128)}, f32[1,96,384]{2,1,0:T(8,128)S(1)}, u32[]{:S(2)}, u32[]{:S(2)}) collective-permute-start(f32[1,96,384]{2,1,0:T(8,128)} %get-tuple-element.1754), channel_id=1, source_target_pairs={{1,0},{2,1},{3,2},{4,3},{5,4},{6,5},{7,6},{9,8},{10,9},{11,10},{12... | collective-permute-start | bytes 442376 | tf_op jit(solution)/shard_map/while/body/eval_jaxpr/ppermute | solution.py:25
  772.0 32.0 %collective-permute-start.2 = (f32[1,96,384]{2,1,0:T(8,128)}, f32[1,96,384]{2,1,0:T(8,128)S(1)}, u32[]{:S(2)}, u32[]{:S(2)}) collective-permute-start(f32[1,96,384]{2,1,0:T(8,128)} %get-tuple-element.1753), channel_id=1, source_target_pairs={{0,1},{1,2},{2,3},{3,4},{4,5},{5,6},{6,7},{8,9},{9,10},{10,11},{11... | collective-permute-start | bytes 442376 | tf_op jit(solution)/shard_map/while/body/eval_jaxpr/ppermute | solution.py:25
  802.1 21.1 %collective-permute-start.3 = (f32[1,96,384]{2,1,0:T(8,128)}, f32[1,96,384]{2,1,0:T(8,128)S(1)}, u32[]{:S(2)}, u32[]{:S(2)}) collective-permute-start(f32[1,96,384]{2,1,0:T(8,128)} %get-tuple-element.1754), channel_id=1, source_target_pairs={{1,0},{2,1},{3,2},{4,3},{5,4},{6,5},{7,6},{9,8},{10,9},{11,10},{12... | collective-permute-start | bytes 442376 | tf_op jit(solution)/shard_map/while/body/eval_jaxpr/ppermute | solution.py:25
  837.7 28.9 %collective-permute-start.2 = (f32[1,96,384]{2,1,0:T(8,128)}, f32[1,96,384]{2,1,0:T(8,128)S(1)}, u32[]{:S(2)}, u32[]{:S(2)}) collective-permute-start(f32[1,96,384]{2,1,0:T(8,128)} %get-tuple-element.1753), channel_id=1, source_target_pairs={{0,1},{1,2},{2,3},{3,4},{4,5},{5,6},{6,7},{8,9},{9,10},{10,11},{11... | collective-permute-start | bytes 442376 | tf_op jit(solution)/shard_map/while/body/eval_jaxpr/ppermute | solution.py:25
  864.7 34.4 %collective-permute-start.3 = (f32[1,96,384]{2,1,0:T(8,128)}, f32[1,96,384]{2,1,0:T(8,128)S(1)}, u32[]{:S(2)}, u32[]{:S(2)}) collective-permute-start(f32[1,96,384]{2,1,0:T(8,128)} %get-tuple-element.1754), channel_id=1, source_target_pairs={{1,0},{2,1},{3,2},{4,3},{5,4},{6,5},{7,6},{9,8},{10,9},{11,10},{12... | collective-permute-start | bytes 442376 | tf_op jit(solution)/shard_map/while/body/eval_jaxpr/ppermute | solution.py:25
  913.5 26.6 %collective-permute-start.2 = (f32[1,96,384]{2,1,0:T(8,128)}, f32[1,96,384]{2,1,0:T(8,128)S(1)}, u32[]{:S(2)}, u32[]{:S(2)}) collective-permute-start(f32[1,96,384]{2,1,0:T(8,128)} %get-tuple-element.1753), channel_id=1, source_target_pairs={{0,1},{1,2},{2,3},{3,4},{4,5},{5,6},{6,7},{8,9},{9,10},{10,11},{11... | collective-permute-start | bytes 442376 | tf_op jit(solution)/shard_map/while/body/eval_jaxpr/ppermute | solution.py:25
  961.5 28.2 %collective-permute-start.2 = (f32[1,96,384]{2,1,0:T(8,128)}, f32[1,96,384]{2,1,0:T(8,128)S(1)}, u32[]{:S(2)}, u32[]{:S(2)}) collective-permute-start(f32[1,96,384]{2,1,0:T(8,128)} %get-tuple-element.1753), channel_id=1, source_target_pairs={{0,1},{1,2},{2,3},{3,4},{4,5},{5,6},{6,7},{8,9},{9,10},{10,11},{11... | collective-permute-start | bytes 442376 | tf_op jit(solution)/shard_map/while/body/eval_jaxpr/ppermute | solution.py:25
  965.1 27.6 %collective-permute-start.3 = (f32[1,96,384]{2,1,0:T(8,128)}, f32[1,96,384]{2,1,0:T(8,128)S(1)}, u32[]{:S(2)}, u32[]{:S(2)}) collective-permute-start(f32[1,96,384]{2,1,0:T(8,128)} %get-tuple-element.1754), channel_id=1, source_target_pairs={{1,0},{2,1},{3,2},{4,3},{5,4},{6,5},{7,6},{9,8},{10,9},{11,10},{12... | collective-permute-start | bytes 442376 | tf_op jit(solution)/shard_map/while/body/eval_jaxpr/ppermute | solution.py:25
  1007.2 15.0 %collective-permute-start.2 = (f32[1,96,384]{2,1,0:T(8,128)}, f32[1,96,384]{2,1,0:T(8,128)S(1)}, u32[]{:S(2)}, u32[]{:S(2)}) collective-permute-start(f32[1,96,384]{2,1,0:T(8,128)} %get-tuple-element.1753), channel_id=1, source_target_pairs={{0,1},{1,2},{2,3},{3,4},{4,5},{5,6},{6,7},{8,9},{9,10},{10,11},{11... | collective-permute-start | bytes 442376 | tf_op jit(solution)/shard_map/while/body/eval_jaxpr/ppermute | solution.py:25
  1031.7 27.0 %collective-permute-start.4 = (f32[1,4,96,384]{3,2,1,0:T(8,128)}, f32[1,4,96,384]{3,2,1,0:T(8,128)S(1)}, u32[]{:S(2)}, u32[]{:S(2)}) collective-permute-start(f32[1,4,96,384]{3,2,1,0:T(8,128)} %get-tuple-element.1421), channel_id=1, source_target_pairs={{1,0},{2,1},{3,2},{4,3},{5,4},{6,5},{7,6},{9,8},{10,9},{11,10},{12... | collective-permute-start | bytes 1769480 | tf_op jit(solution)/shard_map/ppermute | solution.py:25
  (76 other events, 1721.6 us)
where the time goes:
time: 1160 us; the launch traced here: 1140 us
  starting transfers between devices  654 us (56%)
  loops' own time  132 us (11%)
  waiting for transfers between devices  131 us (11%)
  local copies, waits for them, and re-layouts  86.1 us (7%)
  blocking collectives  70.1 us (6%)
  matrix products  50.6 us (4%)
    ppermute x83, starting transfers between devices, shifted(): lax.ppermute(value, axis, [(source, source + steps) for source in range(i...  654 us
    ppermute x83, waiting for transfers between devices, shifted(): lax.ppermute(value, axis, [(source, source + steps) for source in range(i...  131 us
    another operation x8, loops' own time, chain_step(): lax.cond(section_number == col_place, left_live, left_spare, left_opens)  96.5 us
    psum x5, blocking collectives, over_axes(): value = lax.psum(value, axis)  70.1 us
    dot_general x26, matrix products, product(): jnp.einsum(pattern, former, latter, precision=PRECISION_HIGH, preferred_e...  50.2 us
    broadcast_in_dim x64, local copies, waits for them, and re-layouts, shards(): blank_column = jnp.zeros(column_shape, jnp.float32)  41.9 us
  transfers between devices with their start and end apart: 83, of which 42 were waited for; matrix products, arithmetic and copies ran while one was open for 6% of the time, Pallas kernels for 0%

commit v1 on v0

--- a/solution.py
+++ b/solution.py
@@ -1,6 +1,10 @@
+import functools
+
 import jax
 import jax.numpy as jnp
 from jax import lax
+from jax.experimental import pallas as pl
+from jax.experimental.pallas import tpu as pltpu
 from jax.sharding import Mesh
 from jax.sharding import PartitionSpec as P
 
@@ -8,15 +12,467 @@
 D2 = 4
 PHYS = 2
 CHI = 96
+WIDE = D2 * CHI
 OPS = 4
 TERMS = 16
+GROUP = 4
 ROWS = ("rows_0", "rows_1", "rows_2")
 COLS = ("cols_0", "cols_1")
 ROWS_COLS = ("rows_0", "rows_1", "rows_2", "cols_0", "cols_1")
-
+MESH = pl.DeviceIdType.MESH
 
 EPSILON = 1e-06
 PRECISION_HIGH = lax.Precision.HIGHEST
+F32 = jnp.float32
+BF16 = jnp.bfloat16
+
+
+def iota(shape, dim):
+    return lax.broadcasted_iota(jnp.int32, shape, dim)
+
+
+def halves(value):
+    high = value.astype(BF16)
+    low = (value - high.astype(F32)).astype(BF16)
+    return high, low
+
+
+def dot(left, right):
+    return jnp.dot(left, right, preferred_element_type=F32)
+
+
+def dot_nt(left, right):
+    return lax.dot_general(left, right, (((1,), (1,)), ((), ())), preferred_element_type=F32)
+
+
+def unpack(wide):
+    one, two, three = wide[:, 0:128], wide[:, 128:256], wide[:, 256:384]
+    lane = iota((CHI, 128), 1)
+    parts = (
+        one,
+        pltpu.roll(jnp.where(lane >= 96, one, two), 32, 1),
+        pltpu.roll(jnp.where(lane >= 64, two, three), 64, 1),
+        pltpu.roll(three, 96, 1),
+    )
+    return [jnp.where(lane < CHI, part, 0.0) for part in parts]
+
+
+def pack(tiles):
+    lane = iota((CHI, 128), 1)
+    first = tiles[0]
+    second = pltpu.roll(tiles[1], 96, 1)
+    third = pltpu.roll(tiles[2], 64, 1)
+    fourth = pltpu.roll(tiles[3], 32, 1)
+    return jnp.concatenate(
+        [
+            jnp.where(lane < 96, first, second),
+            jnp.where(lane < 64, second, third),
+            jnp.where(lane < 32, third, fourth),
+        ],
+        axis=1,
+    )
+
+
+def pick(mode, *choices):
+    value = choices[-1]
+    for index in range(len(choices) - 1):
+        value = jnp.where(mode == index, choices[index], value)
+    return value
+
+
+def layer_rows(ket, legs):
+    shape = (PHYS * 256, 32)
+    row, col = iota(shape, 0), iota(shape, 1)
+    digits = ((row >> 6) & 3, (row >> 4) & 3, (row >> 2) & 3, row & 3)
+    up, left, down, right = legs(*digits)
+    base = (row >> 8) * 16
+    ket_at = base + (up >> 1) * 8 + (left >> 1) * 4 + (down >> 1) * 2 + (right >> 1)
+    bra_at = base + (up & 1) * 8 + (left & 1) * 4 + (down & 1) * 2 + (right & 1)
+    take = functools.partial(jnp.dot, precision=PRECISION_HIGH, preferred_element_type=F32)
+    kets = take(jnp.where(col == ket_at, 1.0, 0.0), ket)
+    bras = take(jnp.where(col == bra_at, 1.0, 0.0), ket)
+    both = kets * bras
+    full = both[0:256] + both[256:512]
+    lane = iota((64, 128), 1)
+    at = [full[64 * m : 64 * (m + 1)] for m in range(4)]
+    return jnp.concatenate(
+        [
+            jnp.where(lane < 96, at[0], at[1]),
+            jnp.where(lane < 64, at[1], at[2]),
+            jnp.where(lane < 32, at[2], at[3]),
+        ],
+        axis=1,
+    )
+
+
+def thirds(value):
+    high = value.astype(BF16)
+    rest = value - high.astype(F32)
+    middle = rest.astype(BF16)
+    low = (rest - middle.astype(F32)).astype(BF16)
+    return high, middle, low
+
+
+def fold_first(spread, coeffs, folded, slot):
+    def body(index, carried):
+        total = None
+        for leg in range(4):
+            term = coeffs[pl.ds(index * 4 + leg, 1), :] * spread[leg]
+            total = term if total is None else total + term
+        high, middle, low = thirds(total)
+        rows = pl.ds(pl.multiple_of(index * CHI, CHI), CHI)
+        folded[slot, rows, 0:WIDE] = low
+        folded[slot, rows, WIDE : 2 * WIDE] = high
+        folded[slot, rows, 2 * WIDE : 3 * WIDE] = middle
+        return carried
+
+    lax.fori_loop(0, 16, body, 0)
+
+
+def padded(parts):
+    blank = jnp.zeros((32, parts[0].shape[1]), BF16)
+    return jnp.concatenate([piece for part in parts for piece in (part, blank)], axis=0)
+
+
+def apply_layer(state, scale, folded, second, third, slot, middle):
+    high, mid, low = thirds(state)
+    once = jnp.concatenate([high, mid], axis=1)
+    main = jnp.concatenate([once, once], axis=0)
+    fine = jnp.concatenate([high, low], axis=0)
+    for leg in range(4):
+        rows = slice(leg * WIDE, (leg + 1) * WIDE)
+        wide = dot(folded[slot, rows, WIDE : 3 * WIDE], main)
+        rest = dot(folded[slot, rows, 0 : 2 * WIDE], fine)
+        high, mid, low = thirds(wide[:, 0:128] + (wide[:, 128:256] + rest))
+        for index, part in enumerate((high, mid)):
+            middle[:, leg * 256 + index * 128 : leg * 256 + index * 128 + 128] = part
+        for index, part in enumerate((high, low)):
+            begin = 1024 + leg * 256 + index * 128
+            middle[:, begin : begin + 128] = part
+    wide = dot(middle[:, 0:1024], second[slot])
+    rest = dot(middle[:, 1024:2048], third[slot])
+    return (wide[:, 0:128] + (wide[:, 128:256] + rest)) * scale
+
+
+def nrm_scale(state):
+    total = jnp.sum(jnp.sum(state * state, axis=0, keepdims=True), axis=1, keepdims=True)
+    return lax.rsqrt(total * (1.0 / (CHI * WIDE)) + EPSILON)
+
+
+def boundary_kernel(
+    kets,
+    left_maps,
+    right_maps,
+    top_edge,
+    bottom_edge,
+    outs,
+    sides,
+    lefts,
+    rights,
+    ketses,
+    select_one,
+    select_two,
+    spread,
+    coeffs,
+    folded,
+    second,
+    third,
+    middle,
+    entered,
+    leaving,
+    state,
+    normed,
+    map_send,
+    map_recv,
+    hop_send,
+    hop_recv,
+    row_send,
+    out_recv,
+    side_recv,
+):
+    z = lax.axis_index("rows_0")
+    xl = lax.axis_index("rows_1")
+    core = lax.axis_index("rows_2")
+    y = lax.axis_index("cols_0")
+    xh = lax.axis_index("cols_1")
+    planes = lax.axis_size("rows_0")
+    mine = xl * 2 + core
+    col = xl
+    way = (core + z) % 2
+    place = xh * 2 + col
+    is_first = ((way == 0) & (z == 0)) | ((way == 1) & (z == planes - 1))
+    is_last = ((way == 0) & (z == planes - 1)) | ((way == 1) & (z == 0))
+    after_z = z + 1 - 2 * way
+    after = (jnp.clip(after_z, 0, planes - 1), xl, (way + after_z + 2) % 2, y, xh)
+
+    barrier = pltpu.get_barrier_semaphore()
+
+    def greet(device):
+        pl.semaphore_signal(barrier, inc=1, device_id=device, device_id_type=MESH)
+
+    for step in range(1, GROUP):
+        other = (mine + step) % GROUP
+        greet((z, other // 2, other % 2, y, xh))
+    for other in range(GROUP):
+        greet((z, other // 2, other % 2, y, 1 - xh))
+
+    for step in (1, planes - 1):
+        near = (z + step) % planes
+        greet((near, xl, (way + near) % 2, y, xh))
+
+    pl.semaphore_wait(barrier, 9)
+
+    def map_copies(step):
+        other = (mine + step) % GROUP
+        other_col = other // 2
+        other_way = (other % 2 + z) % 2
+        pairs = (
+            (left_maps.at[other_way, 0, other_col], lefts),
+            (right_maps.at[other_way, 0, other_col], rights),
+            (kets.at[other_col], ketses),
+        )
+        device = (z, other // 2, other % 2, y, xh)
+        return [
+            pltpu.make_async_remote_copy(
+                src_ref=source,
+                dst_ref=target.at[mine],
+                send_sem=map_send.at[step - 1, kind],
+                recv_sem=map_recv.at[mine, kind],
+                device_id=device,
+                device_id_type=MESH,
+            )
+            for kind, (source, target) in enumerate(pairs)
+        ]
+
+    own_pairs = (
+        (left_maps.at[way, 0, col], lefts),
+        (right_maps.at[way, 0, col], rights),
+        (kets.at[col], ketses),
+    )
+    for kind, (source, target) in enumerate(own_pairs):
+        pltpu.make_async_copy(source, target.at[mine], map_recv.at[mine, kind]).start()
+    for step in range(1, GROUP):
+        for copy in map_copies(step):
+            copy.start()
+
+    for leg in range(4):
+        row, lane = iota((WIDE, WIDE), 0), iota((WIDE, WIDE), 1)
+        within = lane
+        for _ in range(3):
+            within = jnp.where(within >= CHI, within - CHI, within)
+        select_one[:, leg * WIDE : (leg + 1) * WIDE] = jnp.where(
+            row == 4 * within + leg, 1.0, 0.0
+        ).astype(BF16)
+        row, lane = iota((256, WIDE), 0), iota((256, WIDE), 1)
+        inner = row & 127
+        select_two[leg * 256 : (leg + 1) * 256, :] = jnp.where(
+            (lane == 4 * inner + leg) & (inner < CHI), 1.0, 0.0
+        ).astype(BF16)
+
+    @pl.when(is_first & (way == 0))
+    def _():
+        entered[...] = top_edge[col]
+
+    @pl.when(is_first & (way == 1))
+    def _():
+        entered[...] = bottom_edge[col]
+
+    def row_at(number):
+        return number + way * (GROUP - 1 - 2 * number)
+
+    def legs(m, g, o, f):
+        return pick(way, m, o), f, pick(way, o, m), g
+
+    def prepare(number):
+        j = row_at(number)
+        for kind, target in enumerate((lefts, rights, ketses)):
+            pltpu.make_async_copy(target.at[j], target.at[j], map_recv.at[j, kind]).wait()
+        coeffs[...] = layer_rows(ketses[j], legs)
+        apart = dot(jnp.concatenate(thirds(lefts[j]), axis=0), select_one[...])
+        for leg in range(4):
+            lanes = slice(leg * WIDE, (leg + 1) * WIDE)
+            spread[leg] = apart[0:CHI, lanes] + (
+                apart[CHI : 2 * CHI, lanes] + apart[2 * CHI : 3 * CHI, lanes]
+            )
+        fold_first(spread, coeffs, folded, number)
+        high, mid, low = thirds(rights[j])
+        main = dot_nt(select_two[...], padded((high, mid)))
+        fine = dot_nt(select_two[...], padded((low,)))
+        second[number] = main.astype(BF16)
+        even = (iota((1024, 128), 0) & 128) == 0
+        third[number] = jnp.where(even, fine, main[:, 0:128]).astype(BF16)
+
+    def send_row(number, source, target_of, recv, xh_to, j, kind):
+        here = (j == mine) & (xh_to == xh)
+
+        @pl.when(here)
+        def _():
+            pltpu.make_async_copy(source, target_of, recv).start()
+
+        @pl.when(jnp.logical_not(here))
+        def _():
+            row_copy(number, source, target_of, recv, xh_to, j, kind).start()
+
+    def row_copy(number, source, target_of, recv, xh_to, j, kind):
+        return pltpu.make_async_remote_copy(
+            src_ref=source,
+            dst_ref=target_of,
+            send_sem=row_send.at[number, kind],
+            recv_sem=recv,
+            device_id=(z, j // 2, j % 2, y, xh_to),
+            device_id_type=MESH,
+        )
+
+    def side_args(number, xh_to, kind):
+        return (
+            number,
+            normed.at[number],
+            sides.at[way, place],
+            side_recv.at[way, place],
+            xh_to,
+            row_at(number),
+            kind,
+        )
+
+    def out_args(number):
+        return (
+            number,
+            normed.at[number + 1],
+            outs.at[way, col],
+            out_recv.at[way, col],
+            xh,
+            row_at(number),
+            2,
+        )
+
+    def advance(number):
+        @pl.when(number == 0)
+        def _():
+            @pl.when(jnp.logical_not(is_first))
+            def _():
+                pltpu.make_async_copy(entered, entered, hop_recv).wait()
+
+            for leg, tile in enumerate(unpack(entered[...])):
+                state[leg * CHI : (leg + 1) * CHI, :] = tile
+
+        current = state[...]
+        raw = is_first & (number == 0)
+        scale = jnp.where(raw, 1.0, nrm_scale(current))
+        renewed = apply_layer(current, scale, folded, second, third, number, middle)
+        state[...] = renewed
+
+        @pl.when(number == GROUP - 1)
+        def _():
+            leaving[...] = pack([renewed[leg * CHI : (leg + 1) * CHI] for leg in range(4)])
+
+            @pl.when(jnp.logical_not(is_last))
+            def _():
+                hop().start()
+
+        kept = pack([current[leg * CHI : (leg + 1) * CHI] for leg in range(4)])
+        normed[number] = kept * scale
+        send_row(*side_args(number, xh, 0))
+        send_row(*side_args(number, 1 - xh, 1))
+
+        @pl.when(number > 0)
+        def _():
+            send_row(*out_args(number - 1))
+
+    def hop():
+        return pltpu.make_async_remote_copy(
+            src_ref=leaving,
+            dst_ref=entered,
+            send_sem=hop_send,
+            recv_sem=hop_recv,
+            device_id=after,
+            device_id_type=MESH,
+        )
+
+    def task(index, carried):
+        early = is_first
+        is_prepare = (early & (index % 2 == 0)) | (jnp.logical_not(early) & (index < GROUP))
+
+        @pl.when(is_prepare)
+        def _():
+            prepare(jnp.where(early, index // 2, jnp.minimum(index, GROUP - 1)))
+
+        @pl.when(jnp.logical_not(is_prepare))
+        def _():
+            advance(jnp.where(early, index // 2, jnp.maximum(index - GROUP, 0)))
+
+        return carried
+
+    lax.fori_loop(0, 2 * GROUP, task, 0)
+
+    final = state[...]
+    normed[GROUP] = leaving[...] * nrm_scale(final)
+    send_row(*out_args(GROUP - 1))
+
+    for step in range(1, GROUP):
+        for copy in map_copies(step):
+            copy.wait_send()
+
+    @pl.when(jnp.logical_not(is_last))
+    def _():
+        hop().wait_send()
+
+    for number in range(GROUP):
+        row_copy(*side_args(number, 1 - xh, 1)).wait_send()
+
+        @pl.when(row_at(number) != mine)
+        def _():
+            row_copy(*side_args(number, xh, 0)).wait_send()
+            row_copy(*out_args(number)).wait_send()
+
+    for direction in range(2):
+        for column in range(2):
+            target = outs.at[direction, column]
+            pltpu.make_async_copy(target, target, out_recv.at[direction, column]).wait()
+        for column in range(4):
+            target = sides.at[direction, column]
+            pltpu.make_async_copy(target, target, side_recv.at[direction, column]).wait()
+
+
+def run_boundary(kets, left_maps, right_maps, top_edge, bottom_edge):
+    vmem = pl.BlockSpec(memory_space=pltpu.VMEM)
+    column = (CHI, WIDE)
+    return pl.pallas_call(
+        boundary_kernel,
+        out_shape=(
+            jax.ShapeDtypeStruct((2, 2) + column, F32),
+            jax.ShapeDtypeStruct((2, 4) + column, F32),
+        ),
+        in_specs=[vmem] * 5,
+        out_specs=(vmem, vmem),
+        scratch_shapes=[
+            pltpu.VMEM((GROUP,) + column, F32),
+            pltpu.VMEM((GROUP,) + column, F32),
+            pltpu.VMEM((GROUP, 32, 128), F32),
+            pltpu.VMEM((WIDE, 4 * WIDE), BF16),
+            pltpu.VMEM((1024, WIDE), BF16),
+            pltpu.VMEM((4,) + column, F32),
+            pltpu.VMEM((64, WIDE), F32),
+            pltpu.VMEM((GROUP, 16 * CHI, 3 * WIDE), BF16),
+            pltpu.VMEM((GROUP, 1024, 256), BF16),
+            pltpu.VMEM((GROUP, 1024, 128), BF16),
+            pltpu.VMEM((WIDE, 2048), BF16),
+            pltpu.VMEM(column, F32),
+            pltpu.VMEM(column, F32),
+            pltpu.VMEM((WIDE, 128), F32),
+            pltpu.VMEM((GROUP + 1,) + column, F32),
+            pltpu.SemaphoreType.DMA((GROUP - 1, 3)),
+            pltpu.SemaphoreType.DMA((GROUP, 3)),
+            pltpu.SemaphoreType.DMA,
+            pltpu.SemaphoreType.DMA,
+            pltpu.SemaphoreType.DMA((GROUP, 3)),
+            pltpu.SemaphoreType.DMA((2, 2)),
+            pltpu.SemaphoreType.DMA((2, 4)),
+        ],
+        compiler_params=pltpu.CompilerParams(
+            collective_id=0, has_side_effects=True, vmem_limit_bytes=48 * 1024 * 1024
+        ),
+        name="boundary",
+    )(kets, left_maps, right_maps, top_edge, bottom_edge)
 
 
 def shifted(value, axis, steps):
@@ -41,10 +497,6 @@
     return values / jnp.sqrt(jnp.mean(values * values) + EPSILON)
 
 
-def select_at(values, position):
-    return lax.dynamic_index_in_dim(values, position, 0, keepdims=False)
-
-
 def pair_layers(ket_flat):
     tensor = ket_flat.reshape(PHYS, D, D, D, D)
     doubled = product("pabcd,pefgh->aebfcgdh", tensor, tensor)
@@ -60,26 +512,6 @@
 def pair_diagonal():
     matched = jnp.arange(PHYS)[:, None] == jnp.arange(PHYS)[None, :]
     return jnp.where(matched, 1.0, 0.0).astype(jnp.float32).reshape(PHYS * PHYS)
-
-
-def absorb_down(boundary, layers, left_map, right_map):
-    above_col = boundary.reshape(CHI, D2, CHI)
-    left_three = left_map.reshape(CHI, CHI, D2)
-    right_three = right_map.reshape(CHI, CHI, D2)
-    joined = product("aub,cbr->aurc", above_col, right_three)
-    through = product("aurc,uldr->aldc", joined, layers)
-    renewed = product("xal,aldc->xdc", left_three, through)
-    return normalize(renewed.reshape(CHI, D2 * CHI))
-
-
-def absorb_up(boundary, layers, left_map, right_map):
-    below_col = boundary.reshape(CHI, D2, CHI)
-    left_three = left_map.reshape(CHI, CHI, D2)
-    right_three = right_map.reshape(CHI, CHI, D2)
-    joined = product("adb,cbr->adrc", below_col, right_three)
-    through = product("adrc,uldr->aluc", joined, layers)
-    renewed = product("xal,aluc->xuc", left_three, through)
-    return normalize(renewed.reshape(CHI, D2 * CHI))
 
 
 def left_core(environ, layers, above_col, below_col):
@@ -129,7 +561,6 @@
     term_ops,
     operators,
 ):
-    row_count = lax.axis_size(ROWS)
     row_place = lax.axis_index(ROWS)
     col_count = lax.axis_size(COLS)
     col_place = lax.axis_index(COLS)
@@ -137,89 +568,11 @@
     local_cols = kets.shape[1]
     layers = jax.vmap(jax.vmap(pair_layers))(kets)
     column_shape = (CHI, D2 * CHI)
-    blank_column = jnp.zeros(column_shape, jnp.float32)
-
-    def run_down(source, column):
-        current = source
-        current = absorb_down(
-            current,
-            select_at(layers[0], column),
-            select_at(left_maps[0, 0], column),
-            select_at(right_maps[0, 0], column),
-        )
-        columns_out = [current]
-        return jnp.stack(columns_out)
-
-    def run_up(source, column):
-        columns_out = [None] * local_rows
-        current = source
-        for local_row in reversed(range(local_rows)):
-            current = absorb_up(
-                current,
-                select_at(layers[local_row], column),
-                select_at(left_maps[1, local_row], column),
-                select_at(right_maps[1, local_row], column),
-            )
-            columns_out[local_row] = current
-        return jnp.stack(columns_out)
-
-    def pipe_step(step_number, carried):
-        from_above, from_below, enter_top, leave_top, enter_bottom, leave_bottom = carried
-        slot_top = step_number - row_place
-        column_top = jnp.clip(slot_top, 0, local_cols - 1)
-        source_top = jnp.where(row_place == 0, select_at(top_edge, column_top), from_above)
-
-        def down_live(stores):
-            renewed = run_down(source_top, column_top)
-            entered = lax.dynamic_update_index_in_dim(stores[0], source_top, column_top, 0)
-            left_now = lax.dynamic_update_index_in_dim(stores[1], renewed, column_top, 1)
-            return (entered, left_now, renewed[local_rows - 1])
-
-        def down_spare(stores):
-            return (stores[0], stores[1], blank_column)
-
-        live_top = (slot_top >= 0) & (slot_top < local_cols)
-        enter_top, leave_top, send_down = lax.cond(
-            live_top, down_live, down_spare, (enter_top, leave_top)
-        )
-        slot_bottom = step_number - (row_count - 1 - row_place)
-        column_bottom = jnp.clip(slot_bottom, 0, local_cols - 1)
-        source_bottom = jnp.where(
-            row_place == row_count - 1, select_at(bottom_edge, column_bottom), from_below
-        )
-
-        def up_live(stores):
-            renewed = run_up(source_bottom, column_bottom)
-            entered = lax.dynamic_update_index_in_dim(stores[0], source_bottom, column_bottom, 0)
-            left_now = lax.dynamic_update_index_in_dim(stores[1], renewed, column_bottom, 1)
-            return (entered, left_now, renewed[0])
-
-        def up_spare(stores):
-            return (stores[0], stores[1], blank_column)
-
-        live_bottom = (slot_bottom >= 0) & (slot_bottom < local_cols)
-        enter_bottom, leave_bottom, send_up = lax.cond(
-            live_bottom, up_live, up_spare, (enter_bottom, leave_bottom)
-        )
-        from_above = shifted(send_down, ROWS, 1)
-        from_below = shifted(send_up, ROWS, -1)
-        return (from_above, from_below, enter_top, leave_top, enter_bottom, leave_bottom)
-
-    entry_shape = (local_cols,) + column_shape
-    store_shape = (local_rows, local_cols) + column_shape
-    initial = (
-        blank_column,
-        blank_column,
-        jnp.zeros(entry_shape, jnp.float32),
-        jnp.zeros(store_shape, jnp.float32),
-        jnp.zeros(entry_shape, jnp.float32),
-        jnp.zeros(store_shape, jnp.float32),
-    )
-    unused_above, unused_below, enter_top, leave_top, enter_bottom, leave_bottom = lax.fori_loop(
-        0, row_count + local_cols - 1, pipe_step, initial
-    )
-    above = jnp.concatenate([enter_top[None], leave_top[:-1]], axis=0)
-    below = jnp.concatenate([leave_bottom[1:], enter_bottom[None]], axis=0)
+    spread_kets = jnp.broadcast_to(kets[0][:, :, None], (local_cols, 32, 128))
+    outs, sides = run_boundary(spread_kets, left_maps, right_maps, top_edge, bottom_edge)
+    leave_top, leave_bottom = outs[0][None], outs[1][None]
+    own = lax.dynamic_slice_in_dim(sides, lax.axis_index("cols_1") * 2, 2, 1)
+    above, below = own[0][None], own[1][None]
     global_rows = row_place * local_rows + jnp.arange(local_rows, dtype=jnp.int32)
     global_cols = col_place * local_cols + jnp.arange(local_cols, dtype=jnp.int32)
     row_match = term_rows[:, None] == global_rows[None, :]

time: 1160 us -> 654 us (0.56)
  the two profiles are of different devices: /device:TPU:8 before, /device:TPU:1 now
where the time goes in v1:
time: 654 us; the launch traced here: 641 us
  Pallas kernels  126 us (19%)
  loops' own time  123 us (19%)
  waiting for transfers between devices  119 us (18%)
  starting transfers between devices  94.8 us (14%)
  blocking collectives  59 us (9%)
  matrix products  58.3 us (9%)
  local copies, waits for them, and re-layouts  50.5 us (8%)
  other arithmetic  9.14 us (1%)
    pallas_call x1, Pallas kernels, run_boundary(): pl.pallas_call(boundary_kernel, out_shape=(jax.ShapeDtypeStruct((2, 2) +...  126 us
    ppermute x17, waiting for transfers between devices, shifted(): lax.ppermute(value, axis, [(source, source + steps) for source in range(i...  119 us
    another operation x8, loops' own time, chain_step(): lax.cond(section_number == col_place, left_live, left_spare, left_opens)  96.7 us
    ppermute x17, starting transfers between devices, shifted(): lax.ppermute(value, axis, [(source, source + steps) for source in range(i...  94.8 us
    psum x5, blocking collectives, over_axes(): value = lax.psum(value, axis)  59 us
    dot_general x32, matrix products, product(): jnp.einsum(pattern, former, latter, precision=PRECISION_HIGH, preferred_e...  57.8 us
    another operation x8, loops' own time, chain_step(): lax.cond(section_number == col_count - 1 - col_place, right_live, right_s...  15.1 us
    another operation x24, local copies, waits for them, and re-layouts  15.1 us
  transfers between devices with their start and end apart: 17, of which 10 were waited for; matrix products, arithmetic and copies ran while one was open for 7% of the time, Pallas kernels for 0%

profile of v1, /device:TPU:1, one launch (start us, length us, event | category | flops | bytes accessed | tf_op | source)
XLA Modules:
  0.0 640.7 jit_solution(3751945232549624709)
XLA Ops:
  8.0 125.8 %boundary.1 = (f32[2,2,96,384]{3,2,1,0:T(8,128)S(1)}, f32[2,4,96,384]{3,2,1,0:T(8,128)S(1)}) custom-call(f32[2,32,128]{2,1,0:T(8,128)S(1)} %broadcast_in_dim.94.kets, f32[2,1,2,96,384]{4,3,2,1,0:T(8,128)S(1)} %copy-done.1, f32[2,1,2,96,384]{4,3,2,1,0:T(8,128)S(1)} %copy-done.2, f32[2,96,384]{2,1,0:T(8,128)S(1)} %copy-done.3, f32[2,96,384]{2,1,0:T(8,128)S(1)} %copy-done.4), custom_call_target="tpu_custom_call" | custom-call | tf_op jit(solution)/shard_map/boundary/pallas_call | solution.py:439
  137.1 422.6 %while.66 = (s32[]{:T(128)}, f32[1,96,384]{2,1,0:T(8,128)S(1)}, f32[1,96,384]{2,1,0:T(8,128)}, f32[1,2,4,96,384]{4,3,2,1,0:T(8,128)}, f32[1,2,4,96,384]{4,3,2,1,...) while((s32[]{:T(128)}, f32[1,96,384]{2,1,0:T(8,128)S(1)}, ...), condition=%wide.region_35.36_spmd, body=%wide.region_2.35_spmd.sunk | while | flops 1474342912 | bytes 34500900 | solution.py:659
  137.4 44.5 %conditional.8 = (f32[1,2,4,96,384]{4,3,2,1,0:T(8,128)}, f32[1,96,384]{2,1,0:T(8,128)}) conditional(s32[]{:T(128)} %convert_element_type.46, f32[1,2,4,96,384]{4,3,2,1,0:T(8,128)} %get-tuple-element.1193, (pred[1,2]{1,0:T(4,128)(4,1)S(1)}, s32[]{:T(128)}, f32[1,96,384]{1,2,0:T(8,128)S(1)}, f32[1,96,384]{2,1,0:T(8,128)S(1)}, ...), branch_computations={%region_3.0_spmd, %region_4.18_spmd} | conditional | flops 737171456 | bytes 16072630 | solution.py:614
  140.4 29.2 %conditional = (f32[96,384]{1,0:T(8,128)S(1)}, f32[1,4,96,384]{3,2,1,0:T(8,128)}) conditional(s32[]{:T(128)} %bitcast.53, (f32[1,96,384]{1,2,0:T(8,128)S(1)}, f32[1,1,96,384]{3,2,1,0:T(8,128)S(1)}, f32[1,2,4,4,4,4]{2,5,3,4,1,0:T(4,128)}, f32[1,1,96,384]{3,2,1,0:T(8,128)S(1)}) %tuple.87, (f32[1,2,32]{2,1,0:T(2,128)S(1)}, f32[1,96,384]{1,2,0:T(8,128)S(1)}, ...), branch_computations={%region_5.5_spmd, %region_7.10_spmd} | conditional | flops 368419840 | bytes 5650565 | solution.py:548
  141.7 25.3 %while.62 = (s32[]{:T(128)}, f32[4,96,384]{2,1,0:T(8,128)}, f32[1,96,384]{1,2,0:T(8,128)S(1)}, f32[1,1,96,384]{3,2,1,0:T(8,128)S(1)}, f32[4,4,4,4,4]{1,4,2,3,0:T...) while((s32[]{:T(128)}, f32[4,96,384]{2,1,0:T(8,128)}, f32[1,96,384]{1,2,0:T(8,128)S(1)}, ...), condition=%wide.region_9.7_spmd, body=%wide.region_8.6_spmd.sunk | while | flops 368050176 | bytes 4457549 | solution.py:538
  198.4 14.2 %conditional.8 = (f32[1,2,4,96,384]{4,3,2,1,0:T(8,128)}, f32[1,96,384]{2,1,0:T(8,128)}) conditional(s32[]{:T(128)} %convert_element_type.46, f32[1,2,4,96,384]{4,3,2,1,0:T(8,128)} %get-tuple-element.1193, (pred[1,2]{1,0:T(4,128)(4,1)S(1)}, s32[]{:T(128)}, f32[1,96,384]{1,2,0:T(8,128)S(1)}, f32[1,96,384]{2,1,0:T(8,128)S(1)}, ...), branch_computations={%region_3.0_spmd, %region_4.18_spmd} | conditional | flops 737171456 | bytes 16072630 | solution.py:614
  212.7 10.4 %collective-permute-start = (f32[1,96,384]{2,1,0:T(8,128)}, f32[1,96,384]{2,1,0:T(8,128)S(1)}, u32[]{:S(2)}, u32[]{:S(2)}) collective-permute-start(f32[1,96,384]{2,1,0:T(8,128)} %get-tuple-element.1038), channel_id=1, source_target_pairs={{0,1},{1,2},{2,3},{3,4},{4,5},{5,6},{6,7},{8,9},{9,10},{10,11},{11... | collective-permute-start | bytes 442376 | tf_op jit(solution)/shard_map/while/body/eval_jaxpr/ppermute | solution.py:481
  236.7 14.1 %conditional.8 = (f32[1,2,4,96,384]{4,3,2,1,0:T(8,128)}, f32[1,96,384]{2,1,0:T(8,128)}) conditional(s32[]{:T(128)} %convert_element_type.46, f32[1,2,4,96,384]{4,3,2,1,0:T(8,128)} %get-tuple-element.1193, (pred[1,2]{1,0:T(4,128)(4,1)S(1)}, s32[]{:T(128)}, f32[1,96,384]{1,2,0:T(8,128)S(1)}, f32[1,96,384]{2,1,0:T(8,128)S(1)}, ...), branch_computations={%region_3.0_spmd, %region_4.18_spmd} | conditional | flops 737171456 | bytes 16072630 | solution.py:614
  260.5 11.1 %collective-permute-done.1 = f32[1,96,384]{2,1,0:T(8,128)S(1)} collective-permute-done((f32[1,96,384]{2,1,0:T(8,128)}, f32[1,96,384]{2,1,0:T(8,128)S(1)}, u32[]{:S(2)}, u32[]{:S(2)}) %collective-permute-start.1) | collective-permute-done | bytes 147488 | tf_op jit(solution)/shard_map/while/body/eval_jaxpr/ppermute | solution.py:481
  272.4 14.3 %conditional.8 = (f32[1,2,4,96,384]{4,3,2,1,0:T(8,128)}, f32[1,96,384]{2,1,0:T(8,128)}) conditional(s32[]{:T(128)} %convert_element_type.46, f32[1,2,4,96,384]{4,3,2,1,0:T(8,128)} %get-tuple-element.1193, (pred[1,2]{1,0:T(4,128)(4,1)S(1)}, s32[]{:T(128)}, f32[1,96,384]{1,2,0:T(8,128)S(1)}, f32[1,96,384]{2,1,0:T(8,128)S(1)}, ...), branch_computations={%region_3.0_spmd, %region_4.18_spmd} | conditional | flops 737171456 | bytes 16072630 | solution.py:614
  305.1 14.2 %conditional.8 = (f32[1,2,4,96,384]{4,3,2,1,0:T(8,128)}, f32[1,96,384]{2,1,0:T(8,128)}) conditional(s32[]{:T(128)} %convert_element_type.46, f32[1,2,4,96,384]{4,3,2,1,0:T(8,128)} %get-tuple-element.1193, (pred[1,2]{1,0:T(4,128)(4,1)S(1)}, s32[]{:T(128)}, f32[1,96,384]{1,2,0:T(8,128)S(1)}, f32[1,96,384]{2,1,0:T(8,128)S(1)}, ...), branch_computations={%region_3.0_spmd, %region_4.18_spmd} | conditional | flops 737171456 | bytes 16072630 | solution.py:614
  340.4 14.1 %conditional.8 = (f32[1,2,4,96,384]{4,3,2,1,0:T(8,128)}, f32[1,96,384]{2,1,0:T(8,128)}) conditional(s32[]{:T(128)} %convert_element_type.46, f32[1,2,4,96,384]{4,3,2,1,0:T(8,128)} %get-tuple-element.1193, (pred[1,2]{1,0:T(4,128)(4,1)S(1)}, s32[]{:T(128)}, f32[1,96,384]{1,2,0:T(8,128)S(1)}, f32[1,96,384]{2,1,0:T(8,128)S(1)}, ...), branch_computations={%region_3.0_spmd, %region_4.18_spmd} | conditional | flops 737171456 | bytes 16072630 | solution.py:614
  354.6 18.0 %collective-permute-start = (f32[1,96,384]{2,1,0:T(8,128)}, f32[1,96,384]{2,1,0:T(8,128)S(1)}, u32[]{:S(2)}, u32[]{:S(2)}) collective-permute-start(f32[1,96,384]{2,1,0:T(8,128)} %get-tuple-element.1038), channel_id=1, source_target_pairs={{0,1},{1,2},{2,3},{3,4},{4,5},{5,6},{6,7},{8,9},{9,10},{10,11},{11... | collective-permute-start | bytes 442376 | tf_op jit(solution)/shard_map/while/body/eval_jaxpr/ppermute | solution.py:481
  375.9 35.2 %collective-permute-done.1 = f32[1,96,384]{2,1,0:T(8,128)S(1)} collective-permute-done((f32[1,96,384]{2,1,0:T(8,128)}, f32[1,96,384]{2,1,0:T(8,128)S(1)}, u32[]{:S(2)}, u32[]{:S(2)}) %collective-permute-start.1) | collective-permute-done | bytes 147488 | tf_op jit(solution)/shard_map/while/body/eval_jaxpr/ppermute | solution.py:481
  412.0 14.3 %conditional.8 = (f32[1,2,4,96,384]{4,3,2,1,0:T(8,128)}, f32[1,96,384]{2,1,0:T(8,128)}) conditional(s32[]{:T(128)} %convert_element_type.46, f32[1,2,4,96,384]{4,3,2,1,0:T(8,128)} %get-tuple-element.1193, (pred[1,2]{1,0:T(4,128)(4,1)S(1)}, s32[]{:T(128)}, f32[1,96,384]{1,2,0:T(8,128)S(1)}, f32[1,96,384]{2,1,0:T(8,128)S(1)}, ...), branch_computations={%region_3.0_spmd, %region_4.18_spmd} | conditional | flops 737171456 | bytes 16072630 | solution.py:614
  426.3 25.8 %collective-permute-start = (f32[1,96,384]{2,1,0:T(8,128)}, f32[1,96,384]{2,1,0:T(8,128)S(1)}, u32[]{:S(2)}, u32[]{:S(2)}) collective-permute-start(f32[1,96,384]{2,1,0:T(8,128)} %get-tuple-element.1038), channel_id=1, source_target_pairs={{0,1},{1,2},{2,3},{3,4},{4,5},{5,6},{6,7},{8,9},{9,10},{10,11},{11... | collective-permute-start | bytes 442376 | tf_op jit(solution)/shard_map/while/body/eval_jaxpr/ppermute | solution.py:481
  455.2 26.3 %collective-permute-done.1 = f32[1,96,384]{2,1,0:T(8,128)S(1)} collective-permute-done((f32[1,96,384]{2,1,0:T(8,128)}, f32[1,96,384]{2,1,0:T(8,128)S(1)}, u32[]{:S(2)}, u32[]{:S(2)}) %collective-permute-start.1) | collective-permute-done | bytes 147488 | tf_op jit(solution)/shard_map/while/body/eval_jaxpr/ppermute | solution.py:481
  482.4 14.2 %conditional.8 = (f32[1,2,4,96,384]{4,3,2,1,0:T(8,128)}, f32[1,96,384]{2,1,0:T(8,128)}) conditional(s32[]{:T(128)} %convert_element_type.46, f32[1,2,4,96,384]{4,3,2,1,0:T(8,128)} %get-tuple-element.1193, (pred[1,2]{1,0:T(4,128)(4,1)S(1)}, s32[]{:T(128)}, f32[1,96,384]{1,2,0:T(8,128)S(1)}, f32[1,96,384]{2,1,0:T(8,128)S(1)}, ...), branch_computations={%region_3.0_spmd, %region_4.18_spmd} | conditional | flops 737171456 | bytes 16072630 | solution.py:614
  503.9 43.1 %conditional.9 = (f32[1,2,4,96,384]{4,3,2,1,0:T(8,128)}, f32[1,96,384]{2,1,0:T(8,128)}) conditional(s32[]{:T(128)} %convert_element_type.47, f32[1,2,4,96,384]{4,3,2,1,0:T(8,128)} %get-tuple-element.1194, (pred[1,2]{1,0:T(4,128)(4,1)S(1)}, s32[]{:T(128)}, f32[1,96,384]{1,2,0:T(8,128)S(1)}, f32[1,96,384]{2,1,0:T(8,128)}, ...), branch_computations={%region_19.19_spmd, %region_20.34_spmd} | conditional | flops 737171456 | bytes 16658386 | solution.py:641
  506.0 29.0 %conditional.2 = (f32[96,384]{1,0:T(8,128)S(1)}, f32[1,4,96,384]{3,2,1,0:T(8,128)}) conditional(s32[]{:T(128)} %bitcast.110, (f32[1,96,384]{1,2,0:T(8,128)S(1)}, f32[1,1,96,384]{3,2,1,0:T(8,128)S(1)}, f32[1,2,4,4,4,4]{2,4,5,3,1,0:T(4,128)}, f32[1,1,96,384]{3,2,1,0:T(8,128)S(1)}) %tuple.101, (f32[1,2,32]{2,1,0:T(2,128)S(1)}, ...), branch_computations={%region_21.21_spmd, %region_23.26_spmd} | conditional | flops 368419840 | bytes 5650565 | solution.py:548
  507.3 25.3 %while.64 = (s32[]{:T(128)}, f32[4,96,384]{2,1,0:T(8,128)}, f32[1,96,384]{1,2,0:T(8,128)S(1)}, f32[1,1,96,384]{3,2,1,0:T(8,128)S(1)}, f32[4,4,4,4,4]{1,3,4,2,0:T...) while((s32[]{:T(128)}, f32[4,96,384]{2,1,0:T(8,128)}, f32[1,96,384]{1,2,0:T(8,128)S(1)}, ...), condition=%wide.region_25.23_spmd, body=%wide.region_24.22_spmd.sunk | while | flops 368050176 | bytes 4457549 | solution.py:538
  581.1 15.0 %psum.35 = f32[16]{0:T(128)S(1)} all-reduce(f32[16]{0:T(128)S(1)} %fusion.72), channel_id=1, replica_groups=mesh['rows_0'=8,'rows_1'=2,'rows_2'=2,'cols_0'=4,'cols_1'=2] {'rows_0'}, use_global_device_ids=true, to_apply=%region_39.40 | all-reduce | flops 16 | bytes 128 | tf_op jit(solution)/shard_map/psum | solution.py:486
  596.1 17.1 %psum.36 = f32[16]{0:T(128)S(1)} all-reduce(f32[16]{0:T(128)S(1)} %psum.35), channel_id=1, replica_groups=mesh['rows_0'=8,'rows_1'=2,'rows_2'=2,'cols_0'=4,'cols_1'=2] {'rows_1'}, use_global_device_ids=true, to_apply=%region_40.41 | all-reduce | flops 16 | bytes 128 | tf_op jit(solution)/shard_map/psum | solution.py:486
  613.2 15.1 %psum.37 = f32[16]{0:T(128)S(1)} all-reduce(f32[16]{0:T(128)S(1)} %psum.36), channel_id=1, replica_groups=mesh['rows_0'=8,'rows_1'=2,'rows_2'=2,'cols_0'=4,'cols_1'=2] {'rows_2'}, use_global_device_ids=true, to_apply=%region_41.42 | all-reduce | flops 16 | bytes 128 | tf_op jit(solution)/shard_map/psum | solution.py:486
  (245 shorter events, 252.7 us)
Async XLA Ops:
  0.6 580.3 %copy-start = (f32[4,16]{1,0:T(4,128)S(1)}, f32[4,16]{1,0:T(4,128)}, u32[]{:S(2)}) copy-start(f32[4,16]{1,0:T(4,128)} %param.43) | copy-start | bytes 772
  0.7 133.2 %copy-start.10 = (s32[2]{0:T(128)}, s32[2]{0:T(128)S(1)}, u32[]{:S(2)}) copy-start(s32[2]{0:T(128)S(1)} %get-tuple-element.817) | copy-start | bytes 28
  6.0 128.0 %copy-start.12 = (pred[16]{0:T(512)(128)(4,1)}, pred[16]{0:T(512)(128)(4,1)S(1)}, u32[]{:S(2)}) copy-start(pred[16]{0:T(512)(128)(4,1)S(1)} %broadcast_compare_fusion) | copy-start | bytes 52
  8.0 125.9 %copy-start.8 = (s32[16]{0:T(128)S(1)}, s32[16]{0:T(128)}, u32[]{:S(2)}) copy-start(s32[16]{0:T(128)} %param.41) | copy-start | bytes 196
  181.8 9.4 %collective-permute-start = (f32[1,96,384]{2,1,0:T(8,128)}, f32[1,96,384]{2,1,0:T(8,128)S(1)}, u32[]{:S(2)}, u32[]{:S(2)}) collective-permute-start(f32[1,96,384]{2,1,0:T(8,128)} %get-tuple-element.1038), channel_id=1, source_target_pairs={{0,1},{1,2},{2,3},{3,4},{4,5},{5,6},{6,7},{8,9},{9,10},{10,11},{11... | collective-permute-start | bytes 442376 | tf_op jit(solution)/shard_map/while/body/eval_jaxpr/ppermute | solution.py:481
  189.9 7.6 %collective-permute-start.1 = (f32[1,96,384]{2,1,0:T(8,128)}, f32[1,96,384]{2,1,0:T(8,128)S(1)}, u32[]{:S(2)}, u32[]{:S(2)}) collective-permute-start(f32[1,96,384]{2,1,0:T(8,128)} %get-tuple-element.1039), channel_id=1, source_target_pairs={{1,0},{2,1},{3,2},{4,3},{5,4},{6,5},{7,6},{9,8},{10,9},{11,10},{12... | collective-permute-start | bytes 442376 | tf_op jit(solution)/shard_map/while/body/eval_jaxpr/ppermute | solution.py:481
  212.7 13.9 %collective-permute-start = (f32[1,96,384]{2,1,0:T(8,128)}, f32[1,96,384]{2,1,0:T(8,128)S(1)}, u32[]{:S(2)}, u32[]{:S(2)}) collective-permute-start(f32[1,96,384]{2,1,0:T(8,128)} %get-tuple-element.1038), channel_id=1, source_target_pairs={{0,1},{1,2},{2,3},{3,4},{4,5},{5,6},{6,7},{8,9},{9,10},{10,11},{11... | collective-permute-start | bytes 442376 | tf_op jit(solution)/shard_map/while/body/eval_jaxpr/ppermute | solution.py:481
  224.7 10.8 %collective-permute-start.1 = (f32[1,96,384]{2,1,0:T(8,128)}, f32[1,96,384]{2,1,0:T(8,128)S(1)}, u32[]{:S(2)}, u32[]{:S(2)}) collective-permute-start(f32[1,96,384]{2,1,0:T(8,128)} %get-tuple-element.1039), channel_id=1, source_target_pairs={{1,0},{2,1},{3,2},{4,3},{5,4},{6,5},{7,6},{9,8},{10,9},{11,10},{12... | collective-permute-start | bytes 442376 | tf_op jit(solution)/shard_map/while/body/eval_jaxpr/ppermute | solution.py:481
  250.8 9.6 %collective-permute-start = (f32[1,96,384]{2,1,0:T(8,128)}, f32[1,96,384]{2,1,0:T(8,128)S(1)}, u32[]{:S(2)}, u32[]{:S(2)}) collective-permute-start(f32[1,96,384]{2,1,0:T(8,128)} %get-tuple-element.1038), channel_id=1, source_target_pairs={{0,1},{1,2},{2,3},{3,4},{4,5},{5,6},{6,7},{8,9},{9,10},{10,11},{11... | collective-permute-start | bytes 442376 | tf_op jit(solution)/shard_map/while/body/eval_jaxpr/ppermute | solution.py:481
  259.2 12.4 %collective-permute-start.1 = (f32[1,96,384]{2,1,0:T(8,128)}, f32[1,96,384]{2,1,0:T(8,128)S(1)}, u32[]{:S(2)}, u32[]{:S(2)}) collective-permute-start(f32[1,96,384]{2,1,0:T(8,128)} %get-tuple-element.1039), channel_id=1, source_target_pairs={{1,0},{2,1},{3,2},{4,3},{5,4},{6,5},{7,6},{9,8},{10,9},{11,10},{12... | collective-permute-start | bytes 442376 | tf_op jit(solution)/shard_map/while/body/eval_jaxpr/ppermute | solution.py:481
  286.7 9.7 %collective-permute-start = (f32[1,96,384]{2,1,0:T(8,128)}, f32[1,96,384]{2,1,0:T(8,128)S(1)}, u32[]{:S(2)}, u32[]{:S(2)}) collective-permute-start(f32[1,96,384]{2,1,0:T(8,128)} %get-tuple-element.1038), channel_id=1, source_target_pairs={{0,1},{1,2},{2,3},{3,4},{4,5},{5,6},{6,7},{8,9},{9,10},{10,11},{11... | collective-permute-start | bytes 442376 | tf_op jit(solution)/shard_map/while/body/eval_jaxpr/ppermute | solution.py:481
  295.1 9.1 %collective-permute-start.1 = (f32[1,96,384]{2,1,0:T(8,128)}, f32[1,96,384]{2,1,0:T(8,128)S(1)}, u32[]{:S(2)}, u32[]{:S(2)}) collective-permute-start(f32[1,96,384]{2,1,0:T(8,128)} %get-tuple-element.1039), channel_id=1, source_target_pairs={{1,0},{2,1},{3,2},{4,3},{5,4},{6,5},{7,6},{9,8},{10,9},{11,10},{12... | collective-permute-start | bytes 442376 | tf_op jit(solution)/shard_map/while/body/eval_jaxpr/ppermute | solution.py:481
  319.3 11.3 %collective-permute-start = (f32[1,96,384]{2,1,0:T(8,128)}, f32[1,96,384]{2,1,0:T(8,128)S(1)}, u32[]{:S(2)}, u32[]{:S(2)}) collective-permute-start(f32[1,96,384]{2,1,0:T(8,128)} %get-tuple-element.1038), channel_id=1, source_target_pairs={{0,1},{1,2},{2,3},{3,4},{4,5},{5,6},{6,7},{8,9},{9,10},{10,11},{11... | collective-permute-start | bytes 442376 | tf_op jit(solution)/shard_map/while/body/eval_jaxpr/ppermute | solution.py:481
  329.3 10.0 %collective-permute-start.1 = (f32[1,96,384]{2,1,0:T(8,128)}, f32[1,96,384]{2,1,0:T(8,128)S(1)}, u32[]{:S(2)}, u32[]{:S(2)}) collective-permute-start(f32[1,96,384]{2,1,0:T(8,128)} %get-tuple-element.1039), channel_id=1, source_target_pairs={{1,0},{2,1},{3,2},{4,3},{5,4},{6,5},{7,6},{9,8},{10,9},{11,10},{12... | collective-permute-start | bytes 442376 | tf_op jit(solution)/shard_map/while/body/eval_jaxpr/ppermute | solution.py:481
  354.6 21.4 %collective-permute-start = (f32[1,96,384]{2,1,0:T(8,128)}, f32[1,96,384]{2,1,0:T(8,128)S(1)}, u32[]{:S(2)}, u32[]{:S(2)}) collective-permute-start(f32[1,96,384]{2,1,0:T(8,128)} %get-tuple-element.1038), channel_id=1, source_target_pairs={{0,1},{1,2},{2,3},{3,4},{4,5},{5,6},{6,7},{8,9},{9,10},{10,11},{11... | collective-permute-start | bytes 442376 | tf_op jit(solution)/shard_map/while/body/eval_jaxpr/ppermute | solution.py:481
  374.6 36.5 %collective-permute-start.1 = (f32[1,96,384]{2,1,0:T(8,128)}, f32[1,96,384]{2,1,0:T(8,128)S(1)}, u32[]{:S(2)}, u32[]{:S(2)}) collective-permute-start(f32[1,96,384]{2,1,0:T(8,128)} %get-tuple-element.1039), channel_id=1, source_target_pairs={{1,0},{2,1},{3,2},{4,3},{5,4},{6,5},{7,6},{9,8},{10,9},{11,10},{12... | collective-permute-start | bytes 442376 | tf_op jit(solution)/shard_map/while/body/eval_jaxpr/ppermute | solution.py:481
  426.3 28.9 %collective-permute-start = (f32[1,96,384]{2,1,0:T(8,128)}, f32[1,96,384]{2,1,0:T(8,128)S(1)}, u32[]{:S(2)}, u32[]{:S(2)}) collective-permute-start(f32[1,96,384]{2,1,0:T(8,128)} %get-tuple-element.1038), channel_id=1, source_target_pairs={{0,1},{1,2},{2,3},{3,4},{4,5},{5,6},{6,7},{8,9},{9,10},{10,11},{11... | collective-permute-start | bytes 442376 | tf_op jit(solution)/shard_map/while/body/eval_jaxpr/ppermute | solution.py:481
  453.9 27.6 %collective-permute-start.1 = (f32[1,96,384]{2,1,0:T(8,128)}, f32[1,96,384]{2,1,0:T(8,128)S(1)}, u32[]{:S(2)}, u32[]{:S(2)}) collective-permute-start(f32[1,96,384]{2,1,0:T(8,128)} %get-tuple-element.1039), channel_id=1, source_target_pairs={{1,0},{2,1},{3,2},{4,3},{5,4},{6,5},{7,6},{9,8},{10,9},{11,10},{12... | collective-permute-start | bytes 442376 | tf_op jit(solution)/shard_map/while/body/eval_jaxpr/ppermute | solution.py:481
  496.6 51.7 %collective-permute-start = (f32[1,96,384]{2,1,0:T(8,128)}, f32[1,96,384]{2,1,0:T(8,128)S(1)}, u32[]{:S(2)}, u32[]{:S(2)}) collective-permute-start(f32[1,96,384]{2,1,0:T(8,128)} %get-tuple-element.1038), channel_id=1, source_target_pairs={{0,1},{1,2},{2,3},{3,4},{4,5},{5,6},{6,7},{8,9},{9,10},{10,11},{11... | collective-permute-start | bytes 442376 | tf_op jit(solution)/shard_map/while/body/eval_jaxpr/ppermute | solution.py:481
  547.0 7.6 %collective-permute-start.1 = (f32[1,96,384]{2,1,0:T(8,128)}, f32[1,96,384]{2,1,0:T(8,128)S(1)}, u32[]{:S(2)}, u32[]{:S(2)}) collective-permute-start(f32[1,96,384]{2,1,0:T(8,128)} %get-tuple-element.1039), channel_id=1, source_target_pairs={{1,0},{2,1},{3,2},{4,3},{5,4},{6,5},{7,6},{9,8},{10,9},{11,10},{12... | collective-permute-start | bytes 442376 | tf_op jit(solution)/shard_map/while/body/eval_jaxpr/ppermute | solution.py:481
  561.9 12.3 %collective-permute-start.2 = (f32[1,4,96,384]{3,2,1,0:T(8,128)}, f32[1,4,96,384]{3,2,1,0:T(8,128)S(1)}, u32[]{:S(2)}, u32[]{:S(2)}) collective-permute-start(f32[1,4,96,384]{3,2,1,0:T(8,128)} %get-tuple-element.811), channel_id=1, source_target_pairs={{1,0},{2,1},{3,2},{4,3},{5,4},{6,5},{7,6},{9,8},{10,9},{11,10},{12... | collective-permute-start | bytes 1769480 | tf_op jit(solution)/shard_map/ppermute | solution.py:481
  574.5 6.2 copy-start.9
  574.5 6.2 copy-start.11
  574.5 6.4 copy-start.15
  (16 other events, 35.9 us)

commit v2 on v1

--- a/solution.py
+++ b/solution.py
@@ -167,6 +167,7 @@
     bottom_edge,
     outs,
     sides,
+    row_kets,
     lefts,
     rights,
     ketses,
@@ -189,6 +190,8 @@
     row_send,
     out_recv,
     side_recv,
+    ket_send,
+    ket_recv,
 ):
     z = lax.axis_index("rows_0")
     xl = lax.axis_index("rows_1")
@@ -196,6 +199,7 @@
     y = lax.axis_index("cols_0")
     xh = lax.axis_index("cols_1")
     planes = lax.axis_size("rows_0")
+    stations = lax.axis_size("cols_0")
     mine = xl * 2 + core
     col = xl
     way = (core + z) % 2
@@ -220,7 +224,11 @@
         near = (z + step) % planes
         greet((near, xl, (way + near) % 2, y, xh))
 
-    pl.semaphore_wait(barrier, 9)
+    for step in (1, stations - 1):
+        for other in range(GROUP):
+            greet((z, other // 2, other % 2, (y + step) % stations, xh))
+
+    pl.semaphore_wait(barrier, 17)
 
     def map_copies(step):
         other = (mine + step) % GROUP
@@ -255,6 +263,36 @@
         for copy in map_copies(step):
             copy.start()
 
+    def ket_across():
+        return pltpu.make_async_remote_copy(
+            src_ref=kets,
+            dst_ref=row_kets.at[pl.ds(2 * xh, 2)],
+            send_sem=ket_send.at[0],
+            recv_sem=ket_recv.at[xh],
+            device_id=(z, xl, core, y, 1 - xh),
+            device_id_type=MESH,
+        )
+
+    def ket_back():
+        return pltpu.make_async_remote_copy(
+            src_ref=kets.at[0],
+            dst_ref=row_kets.at[4],
+            send_sem=ket_send.at[1],
+            recv_sem=ket_recv.at[2],
+            device_id=(z, xl, core, jnp.maximum(y - 1, 0), xh),
+            device_id_type=MESH,
+        )
+
+    ket_across().start()
+    pltpu.make_async_copy(kets, row_kets.at[pl.ds(2 * xh, 2)], ket_recv.at[xh]).start()
+    sends_back = (xh == 0) & (y > 0)
+    extra = sends_back & (col == 0)
+    gets_back = (xh == 0) & (y < stations - 1)
+
+    @pl.when(sends_back)
+    def _():
+        ket_back().start()
+
     for leg in range(4):
         row, lane = iota((WIDE, WIDE), 0), iota((WIDE, WIDE), 1)
         within = lane
@@ -334,6 +372,17 @@
             kind,
         )
 
+    def back_copy(number):
+        j = row_at(number)
+        return pltpu.make_async_remote_copy(
+            src_ref=normed.at[number],
+            dst_ref=sides.at[way, 4],
+            send_sem=row_send.at[number, 3],
+            recv_sem=side_recv.at[way, 4],
+            device_id=(z, j // 2, j % 2, jnp.maximum(y - 1, 0), xh),
+            device_id_type=MESH,
+        )
+
     def out_args(number):
         return (
             number,
@@ -374,6 +423,10 @@
         send_row(*side_args(number, xh, 0))
         send_row(*side_args(number, 1 - xh, 1))
 
+        @pl.when(extra)
+        def _():
+            back_copy(number).start()
+
         @pl.when(number > 0)
         def _():
             send_row(*out_args(number - 1))
@@ -419,6 +472,10 @@
     for number in range(GROUP):
         row_copy(*side_args(number, 1 - xh, 1)).wait_send()
 
+        @pl.when(extra)
+        def _():
+            back_copy(number).wait_send()
+
         @pl.when(row_at(number) != mine)
         def _():
             row_copy(*side_args(number, xh, 0)).wait_send()
@@ -432,6 +489,24 @@
             target = sides.at[direction, column]
             pltpu.make_async_copy(target, target, side_recv.at[direction, column]).wait()
 
+        @pl.when(gets_back)
+        def _():
+            target = sides.at[direction, 4]
+            pltpu.make_async_copy(target, target, side_recv.at[direction, 4]).wait()
+
+    ket_across().wait_send()
+    for half in range(2):
+        target = row_kets.at[pl.ds(2 * half, 2)]
+        pltpu.make_async_copy(target, target, ket_recv.at[half]).wait()
+
+    @pl.when(sends_back)
+    def _():
+        ket_back().wait_send()
+
+    @pl.when(gets_back)
+    def _():
+        pltpu.make_async_copy(row_kets.at[4], row_kets.at[4], ket_recv.at[2]).wait()
+
 
 def run_boundary(kets, left_maps, right_maps, top_edge, bottom_edge):
     vmem = pl.BlockSpec(memory_space=pltpu.VMEM)
@@ -440,10 +515,11 @@
         boundary_kernel,
         out_shape=(
             jax.ShapeDtypeStruct((2, 2) + column, F32),
-            jax.ShapeDtypeStruct((2, 4) + column, F32),
+            jax.ShapeDtypeStruct((2, 5) + column, F32),
+            jax.ShapeDtypeStruct((5, 32, 128), F32),
         ),
         in_specs=[vmem] * 5,
-        out_specs=(vmem, vmem),
+        out_specs=(vmem, vmem, vmem),
         scratch_shapes=[
             pltpu.VMEM((GROUP,) + column, F32),
             pltpu.VMEM((GROUP,) + column, F32),
@@ -464,9 +540,11 @@
             pltpu.SemaphoreType.DMA((GROUP, 3)),
             pltpu.SemaphoreType.DMA,
             pltpu.SemaphoreType.DMA,
-            pltpu.SemaphoreType.DMA((GROUP, 3)),
+            pltpu.SemaphoreType.DMA((GROUP, 4)),
             pltpu.SemaphoreType.DMA((2, 2)),
-            pltpu.SemaphoreType.DMA((2, 4)),
+            pltpu.SemaphoreType.DMA((2, 5)),
+            pltpu.SemaphoreType.DMA((2,)),
+            pltpu.SemaphoreType.DMA((3,)),
         ],
         compiler_params=pltpu.CompilerParams(
             collective_id=0, has_side_effects=True, vmem_limit_bytes=48 * 1024 * 1024
@@ -475,77 +553,551 @@
     )(kets, left_maps, right_maps, top_edge, bottom_edge)
 
 
-def shifted(value, axis, steps):
-    count = lax.axis_size(axis)
-    initial, last = (max(0, -steps), min(count, count - steps))
-    return lax.ppermute(value, axis, [(source, source + steps) for source in range(initial, last)])
-
-
-def over_axes(value, axes):
-    for axis in axes:
-        value = lax.psum(value, axis)
-    return value
-
-
-def product(pattern, former, latter):
-    return jnp.einsum(
-        pattern, former, latter, precision=PRECISION_HIGH, preferred_element_type=jnp.float32
+def fold_pair(spread, coeffs, folded, slot):
+    def body(index, carried):
+        total = None
+        for leg in range(4):
+            term = coeffs[pl.ds(index * 4 + leg, 1), :] * spread[leg]
+            total = term if total is None else total + term
+        high, low = halves(total)
+        rows = pl.ds(pl.multiple_of(index * CHI, CHI), CHI)
+        folded[slot, rows, 0:WIDE] = high
+        folded[slot, rows, WIDE : 2 * WIDE] = low
+        return carried
+
+    lax.fori_loop(0, 16, body, 0)
+
+
+def apply_pair(state, scale, folded, second, slot, middle):
+    high, low = halves(state)
+    once = jnp.concatenate([high, low], axis=1)
+    twice = jnp.concatenate([once, once], axis=0)
+    for leg in range(4):
+        wide = dot(folded[slot, leg * WIDE : (leg + 1) * WIDE, :], twice)
+        high, low = halves(wide[:, 0:128] + wide[:, 128:256])
+        middle[:, leg * 256 : leg * 256 + 128] = high
+        middle[:, leg * 256 + 128 : leg * 256 + 256] = low
+    wide = dot(middle[...], second[slot])
+    return (wide[:, 0:128] + wide[:, 128:256]) * scale
+
+
+def environment_kernel(
+    sides,
+    row_kets,
+    left_edge,
+    right_edge,
+    from_left,
+    from_right,
+    select_one,
+    select_two,
+    spread,
+    coeffs,
+    folded,
+    second,
+    middle,
+    entered,
+    leaving,
+    state,
+    normed,
+    hop_send,
+    hop_recv,
+    over_send,
+    over_recv,
+):
+    z = lax.axis_index("rows_0")
+    xl = lax.axis_index("rows_1")
+    core = lax.axis_index("rows_2")
+    y = lax.axis_index("cols_0")
+    way = lax.axis_index("cols_1")
+    stations = lax.axis_size("cols_0")
+    is_first = ((way == 0) & (y == 0)) | ((way == 1) & (y == stations - 1))
+    is_last = ((way == 0) & (y == stations - 1)) | ((way == 1) & (y == 0))
+    after = (z, xl, core, jnp.clip(y + 1 - 2 * way, 0, stations - 1), way)
+
+    barrier = pltpu.get_barrier_semaphore()
+
+    def greet(y_to, way_to):
+        device = (z, xl, core, (y_to + stations) % stations, way_to)
+        pl.semaphore_signal(barrier, inc=1, device_id=device, device_id_type=MESH)
+
+    greet(y + 1, way)
+    greet(y - 1, way)
+    greet(y, 1 - way)
+    greet(y + 1 - 2 * way, 1 - way)
+    pl.semaphore_wait(barrier, 4)
+
+    @pl.when(way == 0)
+    def _():
+        row, lane = iota((2 * CHI, WIDE), 0), iota((2 * CHI, WIDE), 1)
+        row = jnp.where(row >= CHI, row - CHI, row)
+        for _ in range(3):
+            lane = jnp.where(lane >= CHI, lane - CHI, lane)
+        select_one[0 : 2 * CHI, 0:WIDE] = jnp.where(row == lane, 1.0, 0.0).astype(BF16)
+
+    @pl.when(way == 1)
+    def _():
+        for leg in range(4):
+            row, lane = iota((WIDE, WIDE), 0), iota((WIDE, WIDE), 1)
+            for _ in range(3):
+                lane = jnp.where(lane >= CHI, lane - CHI, lane)
+            select_one[:, leg * WIDE : (leg + 1) * WIDE] = jnp.where(
+                row == leg * CHI + lane, 1.0, 0.0
+            ).astype(BF16)
+            row, lane = iota((256, WIDE), 0), iota((256, WIDE), 1)
+            inner = row & 127
+            select_two[leg * 256 : (leg + 1) * 256, :] = jnp.where(
+                (lane == leg * CHI + inner) & (inner < CHI), 1.0, 0.0
+            ).astype(BF16)
+
+    @pl.when(is_first & (way == 0))
+    def _():
+        entered[...] = left_edge[0]
+
+    @pl.when(is_first & (way == 1))
+    def _():
+        entered[...] = right_edge[0]
+
+    def column_at(number):
+        return number + way * (3 - 2 * number)
+
+    def legs(m, g, o, f):
+        return f, pick(way, m, o), g, pick(way, o, m)
+
+    def prepare(number):
+        column = column_at(number)
+        coeffs[...] = layer_rows(row_kets[column], legs)
+        above = jnp.concatenate(halves(sides[0, column]), axis=0)
+
+        @pl.when(way == 0)
+        def _():
+            turned = lax.dot_general(
+                above,
+                select_one[0 : 2 * CHI, 0:WIDE],
+                (((0,), (0,)), ((), ())),
+                preferred_element_type=F32,
+            )
+            for leg in range(4):
+                spread[leg] = turned[leg * CHI : (leg + 1) * CHI]
+            for leg, tile in enumerate(unpack(sides[1, column])):
+                high, low = halves(tile)
+                both = jnp.concatenate(
+                    [jnp.concatenate([high, low], axis=1), jnp.zeros((32, 256), BF16)], axis=0
+                )
+                second[number, leg * 256 : leg * 256 + 128, :] = both
+                second[number, leg * 256 + 128 : leg * 256 + 256, :] = both
+
+        @pl.when(way == 1)
+        def _():
+            apart = dot(above, select_one[...])
+            for leg in range(4):
+                lanes = slice(leg * WIDE, (leg + 1) * WIDE)
+                spread[leg] = apart[0:CHI, lanes] + apart[CHI : 2 * CHI, lanes]
+            second[number] = dot_nt(select_two[...], padded(halves(sides[1, column]))).astype(BF16)
+
+        fold_pair(spread, coeffs, folded, number)
+
+    def hop():
+        return pltpu.make_async_remote_copy(
+            src_ref=leaving,
+            dst_ref=entered,
+            send_sem=hop_send,
+            recv_sem=hop_recv,
+            device_id=after,
+            device_id_type=MESH,
+        )
+
+    def over(number):
+        column = column_at(number)
+        wraps = column == 0
+        slot = jnp.where(wraps, 3, jnp.maximum(column - 1, 0))
+        y_to = jnp.where(wraps, jnp.maximum(y - 1, 0), y)
+        return pltpu.make_async_remote_copy(
+            src_ref=normed.at[number],
+            dst_ref=from_right.at[slot],
+            send_sem=over_send.at[number],
+            recv_sem=over_recv.at[slot],
+            device_id=(z, xl, core, y_to, 0),
+            device_id_type=MESH,
+        )
+
+    def sends_over(number):
+        return (way == 1) & ((y > 0) | (column_at(number) > 0))
+
+    def advance(number):
+        @pl.when(number == 0)
+        def _():
+            @pl.when(jnp.logical_not(is_first))
+            def _():
+                pltpu.make_async_copy(entered, entered, hop_recv).wait()
+
+            for leg, tile in enumerate(unpack(entered[...])):
+                state[leg * CHI : (leg + 1) * CHI, :] = tile
+
+        current = state[...]
+        raw = is_first & (number == 0)
+        scale = jnp.where(raw, 1.0, nrm_scale(current))
+
+        @pl.when(jnp.logical_not(is_last & (number >= 2)))
+        def _():
+            renewed = apply_pair(current, scale, folded, second, number, middle)
+            state[...] = renewed
+
+            @pl.when(number == 3)
+            def _():
+                leaving[...] = pack([renewed[leg * CHI : (leg + 1) * CHI] for leg in range(4)])
+                hop().start()
+
+        kept = pack([current[leg * CHI : (leg + 1) * CHI] for leg in range(4)]) * scale
+
+        @pl.when(way == 0)
+        def _():
+            from_left[number] = kept
+
+        @pl.when(sends_over(number))
+        def _():
+            normed[number] = kept
+            over(number).start()
+
+    def task(index, carried):
+        is_prepare = (is_first & (index % 2 == 0)) | (jnp.logical_not(is_first) & (index < 4))
+
+        @pl.when(is_prepare)
+        def _():
+            prepare(jnp.where(is_first, index // 2, jnp.minimum(index, 3)))
+
+        @pl.when(jnp.logical_not(is_prepare))
+        def _():
+            advance(jnp.where(is_first, index // 2, jnp.maximum(index - 4, 0)))
+
+        return carried
+
+    lax.fori_loop(0, 8, task, 0)
+
+    @pl.when(jnp.logical_not(is_last))
+    def _():
+        hop().wait_send()
+
+    for number in range(4):
+
+        @pl.when(sends_over(number))
+        def _():
+            over(number).wait_send()
+
+    @pl.when(way == 0)
+    def _():
+        for slot in range(3):
+            target = from_right.at[slot]
+            pltpu.make_async_copy(target, target, over_recv.at[slot]).wait()
+
+    @pl.when((way == 0) & (y < stations - 1))
+    def _():
+        target = from_right.at[3]
+        pltpu.make_async_copy(target, target, over_recv.at[3]).wait()
+
+
+def run_environment(sides, row_kets, left_edge, right_edge):
+    vmem = pl.BlockSpec(memory_space=pltpu.VMEM)
+    column = (CHI, WIDE)
+    return pl.pallas_call(
+        environment_kernel,
+        out_shape=(
+            jax.ShapeDtypeStruct((4,) + column, F32),
+            jax.ShapeDtypeStruct((4,) + column, F32),
+        ),
+        in_specs=[vmem] * 4,
+        out_specs=(vmem, vmem),
+        scratch_shapes=[
+            pltpu.VMEM((WIDE, 4 * WIDE), BF16),
+            pltpu.VMEM((1024, WIDE), BF16),
+            pltpu.VMEM((4,) + column, F32),
+            pltpu.VMEM((64, WIDE), F32),
+            pltpu.VMEM((4, 16 * CHI, 2 * WIDE), BF16),
+            pltpu.VMEM((4, 1024, 256), BF16),
+            pltpu.VMEM((WIDE, 1024), BF16),
+            pltpu.VMEM(column, F32),
+            pltpu.VMEM(column, F32),
+            pltpu.VMEM((WIDE, 128), F32),
+            pltpu.VMEM((4,) + column, F32),
+            pltpu.SemaphoreType.DMA,
+            pltpu.SemaphoreType.DMA,
+            pltpu.SemaphoreType.DMA((4,)),
+            pltpu.SemaphoreType.DMA((4,)),
+        ],
+        compiler_params=pltpu.CompilerParams(
+            collective_id=1, has_side_effects=True, vmem_limit_bytes=40 * 1024 * 1024
+        ),
+        name="environment",
+    )(sides, row_kets, left_edge, right_edge)
+
+
+def dot_general(left, right, dims):
+    return lax.dot_general(left, right, (dims, ((), ())), preferred_element_type=F32)
+
+
+def pad_rows(value):
+    return jnp.concatenate([value, jnp.zeros((32, value.shape[1]), value.dtype)], axis=0)
+
+
+def open_site(ket, legs_at, wide, opened):
+    def body(block, carried):
+        begin = pl.multiple_of(block * 8, 8)
+        half_done = {}
+        for bra in range(8):
+            u2, m2, d2 = bra >> 2, (bra >> 1) & 1, bra & 1
+            tiles = []
+            for top in range(8):
+                u, m, d = top >> 2, (top >> 1) & 1, top & 1
+                row = (2 * m + m2) * 4 + 2 * u + u2
+                lane = (2 * d + d2) * 128
+                tiles.append(wide[pl.ds(row * CHI + begin, 8), lane : lane + 128])
+            for state in range(2):
+                for out in range(2):
+                    total = None
+                    for top in range(8):
+                        at = state * 16 + legs_at(top >> 2, (top >> 1) & 1, top & 1, out)
+                        term = ket[at : at + 1, :] * tiles[top]
+                        total = term if total is None else total + term
+                    half_done[state, out, bra] = total
+        for state in range(2):
+            for out in range(2):
+                for other in range(2):
+                    for out2 in range(2):
+                        total = None
+                        for bra in range(8):
+                            at = other * 16 + legs_at(bra >> 2, (bra >> 1) & 1, bra & 1, out2)
+                            term = ket[at : at + 1, :] * half_done[state, out, bra]
+                            total = term if total is None else total + term
+                        row = (2 * out + out2) * CHI
+                        opened[state * 2 + other, pl.ds(row + begin, 8), :] = total
+        return carried
+
+    lax.fori_loop(0, CHI // 8, body, 0)
+
+
+def energy_kernel(
+    term_rows,
+    term_bonds,
+    term_ops,
+    operators,
+    sides,
+    row_kets,
+    from_left,
+    from_right,
+    shares,
+    wide,
+    opened,
+    closing,
+    density,
+):
+    way = lax.axis_index("cols_1")
+    row_here = (
+        lax.axis_index("rows_0") * GROUP + lax.axis_index("rows_1") * 2 + lax.axis_index("rows_2")
     )
-
-
-def normalize(values):
-    return values / jnp.sqrt(jnp.mean(values * values) + EPSILON)
-
-
-def pair_layers(ket_flat):
-    tensor = ket_flat.reshape(PHYS, D, D, D, D)
-    doubled = product("pabcd,pefgh->aebfcgdh", tensor, tensor)
-    return doubled.reshape(D2, D2, D2, D2)
-
-
-def open_layers(ket_flat):
-    tensor = ket_flat.reshape(PHYS, D, D, D, D)
-    doubled = product("pabcd,qefgh->pqaebfcgdh", tensor, tensor)
-    return doubled.reshape(PHYS * PHYS, D2, D2, D2, D2)
-
-
-def pair_diagonal():
-    matched = jnp.arange(PHYS)[:, None] == jnp.arange(PHYS)[None, :]
-    return jnp.where(matched, 1.0, 0.0).astype(jnp.float32).reshape(PHYS * PHYS)
-
-
-def left_core(environ, layers, above_col, below_col):
-    env_three = environ.reshape(CHI, D2, CHI)
-    upper_three = above_col.reshape(CHI, D2, CHI)
-    lower_three = below_col.reshape(CHI, D2, CHI)
-    step_one = product("alb,aux->lbux", env_three, upper_three)
-    step_two = product("lbux,uldr->bxdr", step_one, layers)
-    return product("bxdr,bdy->xry", step_two, lower_three).reshape(CHI, D2 * CHI)
-
-
-def right_core(environ, layers, above_col, below_col):
-    env_three = environ.reshape(CHI, D2, CHI)
-    upper_three = above_col.reshape(CHI, D2, CHI)
-    lower_three = below_col.reshape(CHI, D2, CHI)
-    step_one = product("xry,aux->ryau", env_three, upper_three)
-    step_two = product("ryau,uldr->yald", step_one, layers)
-    return product("yald,bdy->alb", step_two, lower_three).reshape(CHI, D2 * CHI)
-
-
-def side_step(core_map, environ, ket_flat, layers, above_col, below_col, wanted):
-
-    def with_open(unused):
-        opened = lax.map(
-            lambda single: core_map(environ, single, above_col, below_col), open_layers(ket_flat)
+    first = lax.axis_index("cols_0") * 4
+    shares[...] = jnp.zeros((8, 128), F32)
+
+    def hits(term, column):
+        here = (term_rows[term] == row_here) & (term_bonds[term] == first + column)
+        return here & (way == 0)
+
+    def column_body(column, carried):
+        count = 0
+        for term in range(TERMS):
+            count = count + jnp.where(hits(term, column), 1, 0)
+
+        @pl.when(count > 0)
+        def _():
+            high, low = halves(sides[0, column])
+            both = jnp.concatenate([high, low], axis=0)
+            state_high, state_low = halves(jnp.concatenate(unpack(from_left[column]), axis=1))
+            tn = ((0,), (0,))
+            joined = dot_general(
+                both, jnp.concatenate([state_high, state_high], axis=0), tn
+            ) + dot_general(both, jnp.concatenate([state_low, state_low], axis=0), tn)
+            below_high, below_low = halves(jnp.concatenate(unpack(sides[1, column]), axis=1))
+            main = jnp.concatenate([pad_rows(below_high), pad_rows(below_high)], axis=0)
+            fine = jnp.concatenate([pad_rows(below_low), pad_rows(below_low)], axis=0)
+            for leg in range(4):
+                part = jnp.concatenate(halves(joined[:, leg * 128 : (leg + 1) * 128]), axis=1)
+                wide[leg * WIDE : (leg + 1) * WIDE, :] = dot(part, main) + dot(part, fine)
+            open_site(
+                row_kets.at[column],
+                lambda u, m, d, out: u * 8 + m * 4 + d * 2 + out,
+                wide,
+                opened,
+            )
+
+            right = column + 1
+            above = jnp.concatenate(unpack(sides[0, right]), axis=0)
+            both = jnp.concatenate(halves(above), axis=1)
+            state_high, state_low = halves(jnp.concatenate(unpack(from_right[column]), axis=1))
+            state_high, state_low = pad_rows(state_high), pad_rows(state_low)
+            joined = dot(both, jnp.concatenate([state_high, state_high], axis=0)) + dot(
+                both, jnp.concatenate([state_low, state_low], axis=0)
+            )
+            below_high, below_low = halves(
+                jnp.concatenate([pad_rows(tile) for tile in unpack(sides[1, right])], axis=0)
+            )
+            main = jnp.concatenate([below_high, below_high], axis=1)
+            fine = jnp.concatenate([below_low, below_low], axis=1)
+            for leg in range(4):
+                part = jnp.concatenate(halves(joined[:, leg * 128 : (leg + 1) * 128]), axis=1)
+                wide[leg * WIDE : (leg + 1) * WIDE, :] = dot_nt(part, main) + dot_nt(part, fine)
+            open_site(
+                row_kets.at[right],
+                lambda u, m, d, out: u * 8 + out * 4 + d * 2 + m,
+                wide,
+                closing,
+            )
+
+            for pair in range(4):
+                for other in range(4):
+                    product = opened[pair] * closing[other]
+                    at = pair * 4 + other
+                    density[at : at + 1, :] = jnp.sum(product, axis=0, keepdims=True)
+            rho = jnp.sum(density[...], axis=1, keepdims=True)
+            index = iota((16, 1), 0)
+            diagonal = (index == 0) | (index == 3) | (index == 12) | (index == 15)
+            trace = jnp.sum(jnp.where(diagonal, rho, 0.0), axis=0, keepdims=True)
+            spread = jnp.sqrt(jnp.sum(rho * rho, axis=0, keepdims=True))
+            bottom = jnp.maximum(jnp.abs(trace), 0.25 * spread)
+
+            def term_body(term, kept):
+                @pl.when(hits(term, column))
+                def _():
+                    chosen = jnp.zeros((16, 1), F32)
+                    for entry in range(16):
+                        chosen = jnp.where(
+                            index == entry, operators[term_ops[term], entry], chosen
+                        )
+                    value = jnp.sum(chosen * rho, axis=0, keepdims=True) / bottom
+                    lane = iota((8, 128), 1)
+                    shares[...] = jnp.where(lane == term, value, shares[...])
+
+                return kept
+
+            lax.fori_loop(0, TERMS, term_body, 0)
+
+        return carried
+
+    lax.fori_loop(0, 4, column_body, 0)
+
+
+def run_energies(term_rows, term_bonds, term_ops, operators, sides, row_kets, lefts, rights):
+    vmem = pl.BlockSpec(memory_space=pltpu.VMEM)
+    smem = pl.BlockSpec(memory_space=pltpu.SMEM)
+    return pl.pallas_call(
+        energy_kernel,
+        out_shape=jax.ShapeDtypeStruct((8, 128), F32),
+        in_specs=[smem] * 4 + [vmem] * 4,
+        out_specs=vmem,
+        scratch_shapes=[
+            pltpu.VMEM((16 * CHI, 512), F32),
+            pltpu.VMEM((4, WIDE, 128), F32),
+            pltpu.VMEM((4, WIDE, 128), F32),
+            pltpu.VMEM((16, 128), F32),
+        ],
+        compiler_params=pltpu.CompilerParams(vmem_limit_bytes=32 * 1024 * 1024),
+        name="energies",
+    )(term_rows, term_bonds, term_ops, operators, sides, row_kets, lefts, rights)
+
+
+def sum_kernel(shares, total, planes_in, plane_in, partial, send_one, recv_one, send_two, recv_two):
+    z = lax.axis_index("rows_0")
+    xl = lax.axis_index("rows_1")
+    core = lax.axis_index("rows_2")
+    y = lax.axis_index("cols_0")
+    way = lax.axis_index("cols_1")
+    place = y * 4 + xl * 2 + core
+    barrier = pltpu.get_barrier_semaphore()
+
+    def greet(device):
+        pl.semaphore_signal(barrier, inc=1, device_id=device, device_id_type=MESH)
+
+    def along(step):
+        return ((z + step) % 8, xl, core, y, way)
+
+    def within(step):
+        other = (place * 2 + way + step) % 32
+        return (z, (other // 4) % 2, (other // 2) % 2, other // 8, other % 2)
+
+    for step in range(1, 8):
+        greet(along(step))
+    for step in range(1, 32):
+        greet(within(step))
+    pl.semaphore_wait(barrier, 38)
+
+    def first(step):
+        return pltpu.make_async_remote_copy(
+            src_ref=shares,
+            dst_ref=planes_in.at[z],
+            send_sem=send_one.at[step],
+            recv_sem=recv_one.at[z],
+            device_id=along(step),
+            device_id_type=MESH,
         )
-        closed = jnp.sum(pair_diagonal()[:, None, None] * opened, axis=0)
-        return (opened, normalize(closed))
-
-    def without_open(unused):
-        empty_open = jnp.zeros((PHYS * PHYS, CHI, D2 * CHI), jnp.float32)
-        return (empty_open, normalize(core_map(environ, layers, above_col, below_col)))
-
-    return lax.cond(wanted, with_open, without_open, 0)
+
+    def second(step):
+        return pltpu.make_async_remote_copy(
+            src_ref=partial,
+            dst_ref=plane_in.at[place],
+            send_sem=send_two.at[step],
+            recv_sem=recv_two.at[place],
+            device_id=within(step),
+            device_id_type=MESH,
+        )
+
+    @pl.when(way == 0)
+    def _():
+        for step in range(1, 8):
+            first(step).start()
+        pltpu.make_async_copy(shares, planes_in.at[z], recv_one.at[z]).start()
+        added = None
+        for plane in range(8):
+            target = planes_in.at[plane]
+            pltpu.make_async_copy(target, target, recv_one.at[plane]).wait()
+        for plane in range(8):
+            added = planes_in[plane] if added is None else added + planes_in[plane]
+        partial[...] = added
+        for step in range(1, 32):
+            second(step).start()
+        pltpu.make_async_copy(partial, plane_in.at[place], recv_two.at[place]).start()
+
+    for other in range(16):
+        target = plane_in.at[other]
+        pltpu.make_async_copy(target, target, recv_two.at[other]).wait()
+    added = None
+    for other in range(16):
+        added = plane_in[other] if added is None else added + plane_in[other]
+    total[...] = added
+
+    @pl.when(way == 0)
+    def _():
+        for step in range(1, 8):
+            first(step).wait_send()
+        for step in range(1, 32):
+            second(step).wait_send()
+
+
+def run_sum(shares):
+    vmem = pl.BlockSpec(memory_space=pltpu.VMEM)
+    return pl.pallas_call(
+        sum_kernel,
+        out_shape=jax.ShapeDtypeStruct((8, 128), F32),
+        in_specs=[vmem],
+        out_specs=vmem,
+        scratch_shapes=[
+            pltpu.VMEM((8, 8, 128), F32),
+            pltpu.VMEM((16, 8, 128), F32),
+            pltpu.VMEM((8, 128), F32),
+            pltpu.SemaphoreType.DMA((8,)),
+            pltpu.SemaphoreType.DMA((8,)),
+            pltpu.SemaphoreType.DMA((32,)),
+            pltpu.SemaphoreType.DMA((16,)),
+        ],
+        compiler_params=pltpu.CompilerParams(collective_id=2, has_side_effects=True),
+        name="shares_sum",
+    )(shares)
 
 
 def shards(
@@ -561,127 +1113,16 @@
     term_ops,
     operators,
 ):
-    row_place = lax.axis_index(ROWS)
-    col_count = lax.axis_size(COLS)
-    col_place = lax.axis_index(COLS)
-    local_rows = kets.shape[0]
-    local_cols = kets.shape[1]
-    layers = jax.vmap(jax.vmap(pair_layers))(kets)
-    column_shape = (CHI, D2 * CHI)
-    spread_kets = jnp.broadcast_to(kets[0][:, :, None], (local_cols, 32, 128))
-    outs, sides = run_boundary(spread_kets, left_maps, right_maps, top_edge, bottom_edge)
-    leave_top, leave_bottom = outs[0][None], outs[1][None]
-    own = lax.dynamic_slice_in_dim(sides, lax.axis_index("cols_1") * 2, 2, 1)
-    above, below = own[0][None], own[1][None]
-    global_rows = row_place * local_rows + jnp.arange(local_rows, dtype=jnp.int32)
-    global_cols = col_place * local_cols + jnp.arange(local_cols, dtype=jnp.int32)
-    row_match = term_rows[:, None] == global_rows[None, :]
-    site_match = row_match[:, :, None] & (term_bonds[:, None, None] == global_cols[None, None, :])
-    left_need = jnp.any(site_match, axis=0)
-    right_need = jnp.any(
-        row_match[:, :, None] & (term_bonds[:, None, None] == global_cols[None, None, :] - 1),
-        axis=0,
+    spread_kets = jnp.broadcast_to(kets[0][:, :, None], (kets.shape[1], 32, 128))
+    outs, sides, row_kets = run_boundary(
+        spread_kets, left_maps, right_maps, top_edge, bottom_edge
     )
-    rows_shape = (local_rows,) + column_shape
-    edge_shape = (local_rows, PHYS * PHYS) + column_shape
-    open_shape = (local_rows, local_cols, PHYS * PHYS) + column_shape
-
-    def chain_step(section_number, carried):
-        from_left, from_right, edge_in, left_opens, right_opens, edge_open = carried
-
-        def left_live(stores):
-            source = jnp.where(col_place == 0, left_edge, from_left)
-            environ = source[0]
-            row_open = []
-            for column in range(local_cols):
-                opened, environ = side_step(
-                    left_core,
-                    environ,
-                    kets[0, column],
-                    layers[0, column],
-                    above[0, column],
-                    below[0, column],
-                    left_need[0, column],
-                )
-                row_open.append(opened)
-            opened_rows = [jnp.stack(row_open)]
-            sent_rows = [environ]
-            return (jnp.stack(opened_rows), jnp.stack(sent_rows))
-
-        def left_spare(stores):
-            return (stores, jnp.zeros(rows_shape, jnp.float32))
-
-        left_opens, sent_left = lax.cond(
-            section_number == col_place, left_live, left_spare, left_opens
-        )
-
-        def right_live(stores):
-            source = jnp.where(col_place == col_count - 1, right_edge, from_right)
-            environ = source[0]
-            row_open = [None] * local_cols
-            for column in reversed(range(local_cols)):
-                opened, environ = side_step(
-                    right_core,
-                    environ,
-                    kets[0, column],
-                    layers[0, column],
-                    above[0, column],
-                    below[0, column],
-                    right_need[0, column],
-                )
-                row_open[column] = opened
-            opened_rows = [jnp.stack(row_open)]
-            sent_rows = [environ]
-            kept_edge = stores[1]
-            return (jnp.stack(opened_rows), kept_edge, jnp.stack(sent_rows))
-
-        def right_spare(stores):
-            return (stores[0], stores[1], jnp.zeros(rows_shape, jnp.float32))
-
-        right_opens, edge_open, sent_right = lax.cond(
-            section_number == col_count - 1 - col_place,
-            right_live,
-            right_spare,
-            (right_opens, edge_open),
-        )
-        from_left = shifted(sent_left, COLS, 1)
-        from_right = shifted(sent_right, COLS, -1)
-        return (from_left, from_right, edge_in, left_opens, right_opens, edge_open)
-
-    chain_start = (
-        jnp.zeros(rows_shape, jnp.float32),
-        jnp.zeros(rows_shape, jnp.float32),
-        jnp.zeros(edge_shape, jnp.float32),
-        jnp.zeros(open_shape, jnp.float32),
-        jnp.zeros(open_shape, jnp.float32),
-        jnp.zeros(edge_shape, jnp.float32),
+    lefts, rights = run_environment(sides, row_kets, left_edge, right_edge)
+    shares = run_energies(
+        term_rows, term_bonds, term_ops, operators, sides, row_kets, lefts, rights
     )
-    unused_left, unused_right, unused_edge, left_opens, right_opens, edge_open = lax.fori_loop(
-        0, col_count, chain_step, chain_start
-    )
-    edge_open = shifted(right_opens[:, 0], COLS, -1)
-    partner = jnp.concatenate([right_opens[:, 1:], edge_open[:, None]], axis=1)
-    flat_left = left_opens.reshape(local_rows * local_cols, PHYS * PHYS, -1)
-    flat_right = partner.reshape(local_rows * local_cols, PHYS * PHYS, -1)
-    density = product("kpz,kqz->kpq", flat_left, flat_right).reshape(local_rows * local_cols, -1)
-    diagonal = pair_diagonal()
-    weights = jnp.outer(diagonal, diagonal).reshape(-1)
-    trace_value = jnp.sum(density * weights[None, :], axis=1)
-    spread = jnp.sqrt(jnp.sum(density * density, axis=1))
-    valid_bond = left_need.reshape(-1)
-    denominator = jnp.where(valid_bond, jnp.maximum(jnp.abs(trace_value), 0.25 * spread), 1.0)
-    scaled = density / denominator[:, None]
-    chooser = jnp.where(site_match.reshape(TERMS, -1), 1.0, 0.0).astype(jnp.float32)
-    chosen = jnp.dot(chooser, scaled, precision=PRECISION_HIGH, preferred_element_type=jnp.float32)
-    op_match = jnp.where(
-        term_ops[:, None] == jnp.arange(OPS, dtype=jnp.int32)[None, :], 1.0, 0.0
-    ).astype(jnp.float32)
-    picked = jnp.dot(
-        op_match, operators, precision=PRECISION_HIGH, preferred_element_type=jnp.float32
-    )
-    term_share = jnp.sum(chosen * picked, axis=1)
-    energies = over_axes(term_share, ROWS_COLS)
-    return (leave_top, leave_bottom, energies)
+    energies = run_sum(shares)[0, :TERMS]
+    return (outs[0][None], outs[1][None], energies)
 
 
 def solution(mesh):

time: 654 us -> 210 us (0.32); the launches traced: 641 us -> 207 us
  loops' own time: 123 us -> 0 us
  waiting for transfers between devices: 119 us -> 0 us
  starting transfers between devices: 94.8 us -> 0 us
  Pallas kernels: 126 us -> 199 us
  blocking collectives: 59 us -> 0 us
  matrix products: 58.3 us -> 0 us
  local copies, waits for them, and re-layouts: 50.5 us -> 7.46 us
  other arithmetic: 9.14 us -> 0 us
    another operation x23 -> x0, loops' own time: 123 us -> none  [the longest x8 96.7 us: chain_step(): lax.cond(section_number == col_place, left_live, left_spare, left_opens)]
    ppermute x17 -> x0, waiting for transfers between devices: 119 us -> none  [shifted(): lax.ppermute(value, axis, [(source, source + steps) for source in range(i...]
    ppermute x17 -> x0, starting transfers between devices: 94.8 us -> none  [shifted(): lax.ppermute(value, axis, [(source, source + steps) for source in range(i...]
    pallas_call x0 -> x3, Pallas kernels: none -> 72.4 us  [the longest x1 52.8 us: run_environment(): pl.pallas_call(environment_kernel, out_shape=(jax.ShapeDtypeStruct((4,) +...]
    psum x5 -> x0, blocking collectives: 59 us -> none  [over_axes(): value = lax.psum(value, axis)]
    dot_general x34 -> x0, matrix products: 58.3 us -> none  [the longest x32 57.8 us: product(): jnp.einsum(pattern, former, latter, precision=PRECISION_HIGH, preferred_e...]
    another operation x26 -> x0, local copies, waits for them, and re-layouts: 16.8 us -> none
    while x20 -> x0, local copies, waits for them, and re-layouts: 9.03 us -> none
  transfers between devices with their start and end apart: 17 -> 0, of which waited for: 10 -> 0; matrix products, arithmetic and copies ran while one was open for 7% -> 0% of each run, Pallas kernels for 0% -> 0%
where the time goes in v2:
time: 210 us; the launch traced here: 207 us
  Pallas kernels  199 us (95%)
  local copies, waits for them, and re-layouts  7.46 us (4%)
    pallas_call x1, Pallas kernels, run_boundary(): pl.pallas_call(boundary_kernel, out_shape=(jax.ShapeDtypeStruct((2, 2) +...  127 us
    pallas_call x1, Pallas kernels, run_environment(): pl.pallas_call(environment_kernel, out_shape=(jax.ShapeDtypeStruct((4,) +...  52.8 us
    pallas_call x1, Pallas kernels, run_sum(): pl.pallas_call(sum_kernel, out_shape=jax.ShapeDtypeStruct((8, 128), F32),...  18.8 us
    unnamed x22, local copies, waits for them, and re-layouts  4.67 us

profile of v2, /device:TPU:1, one launch (start us, length us, event | category | flops | bytes accessed | tf_op | source)
XLA Modules:
  0.0 207.2 jit_solution(5669800126571930705)
XLA Ops:
  0.6 0.8 broadcast_in_dim.8.kets
  1.4 0.0 copy-start
  1.4 1.1 copy-done
  2.5 1.1 copy-done.1
  3.5 1.0 copy-done.2
  4.5 1.0 copy-done.3
  5.4 126.6 %boundary.1 = (f32[2,2,96,384]{3,2,1,0:T(8,128)S(1)}, f32[2,5,96,384]{3,2,1,0:T(8,128)S(1)}, f32[5,32,128]{2,1,0:T(8,128)S(1)}) custom-call(f32[2,32,128]{2,1,0:T(8,128)S(1)} %broadcast_in_dim.8.kets, f32[2,1,2,96,384]{4,3,2,1,0:T(8,128)S(1)} %copy-done, f32[2,1,2,96,384]{4,3,2,1,0:T(8,128)S(1)} %copy-done.1, f32[2,96,384]{2,1,0:T(8,128)S(1)} %copy-done.2, ...), custom_call_target="tpu_custom_call" | custom-call | tf_op jit(solution)/shard_map/boundary/pallas_call | solution.py:514
  132.1 0.0 copy-start.7
  132.1 0.0 copy-start.8
  132.1 0.0 copy-start.9
  132.1 0.0 copy-start.10
  132.1 0.9 fusion
  133.0 0.0 copy-done.4
  133.0 0.0 copy-done.5
  133.0 52.8 %environment.1 = (f32[4,96,384]{2,1,0:T(8,128)S(1)}, f32[4,96,384]{2,1,0:T(8,128)S(1)}) custom-call(f32[2,5,96,384]{3,2,1,0:T(8,128)S(1)} %get-tuple-element.9.sides, f32[5,32,128]{2,1,0:T(8,128)S(1)} %get-tuple-element.10.row_kets, f32[1,96,384]{2,1,0:T(8,128)S(1)} %copy-done.4, f32[1,96,384]{2,1,0:T(8,128)S(1)} %copy-done.5), custom_call_target="tpu_custom_call" | custom-call | tf_op jit(solution)/shard_map/environment/pallas_call | solution.py:801
  185.7 0.0 copy-done.7
  185.8 0.0 copy-done.8
  185.8 0.0 copy-done.9
  185.8 0.0 copy-done.10
  185.8 0.8 energies.1.shares
  186.6 0.0 copy-start.6
  186.6 0.6 copy-done.6
  187.2 18.8 %shares_sum.1 = f32[8,128]{1,0:T(8,128)} custom-call(f32[8,128]{1,0:T(8,128)} %copy-done.6), custom_call_target="tpu_custom_call" | custom-call | tf_op jit(solution)/shard_map/shares_sum/pallas_call | solution.py:1084
  206.0 1.2 slice_bitcast_fusion
  (5 shorter events, 0.0 us)
Async XLA Ops:
  1.4 1.1 copy-start
  2.4 1.1 copy-start.1
  3.5 1.0 copy-start.2
  4.5 1.0 copy-start.3
  5.4 127.5 %copy-start.4 = (f32[1,96,384]{2,1,0:T(8,128)S(1)}, f32[1,96,384]{2,1,0:T(8,128)}, u32[]{:S(2)}) copy-start(f32[1,96,384]{2,1,0:T(8,128)} %left_edge.1) | copy-start | bytes 442372
  5.4 127.5 %copy-start.5 = (f32[1,96,384]{2,1,0:T(8,128)S(1)}, f32[1,96,384]{2,1,0:T(8,128)}, u32[]{:S(2)}) copy-start(f32[1,96,384]{2,1,0:T(8,128)} %right_edge.1) | copy-start | bytes 442372
  132.1 53.7 %copy-start.7 = (f32[4,16]{1,0:T(4,128)S(1)}, f32[4,16]{1,0:T(4,128)}, u32[]{:S(2)}) copy-start(f32[4,16]{1,0:T(4,128)} %operators.1) | copy-start | bytes 772
  132.1 53.7 %copy-start.8 = (s32[16]{0:T(128)S(1)}, s32[16]{0:T(128)}, u32[]{:S(2)}) copy-start(s32[16]{0:T(128)} %term_rows.1) | copy-start | bytes 196
  132.1 53.7 %copy-start.9 = (s32[16]{0:T(128)S(1)}, s32[16]{0:T(128)}, u32[]{:S(2)}) copy-start(s32[16]{0:T(128)} %term_bonds.1) | copy-start | bytes 196
  132.1 53.7 %copy-start.10 = (s32[16]{0:T(128)S(1)}, s32[16]{0:T(128)}, u32[]{:S(2)}) copy-start(s32[16]{0:T(128)} %term_ops.1) | copy-start | bytes 196
  186.6 0.6 copy-start.6

commit v3 on v2

v3 whole, which is shorter than its diff:
```python
import functools

import jax
import jax.numpy as jnp
from jax import lax
from jax.experimental import pallas as pl
from jax.experimental.pallas import tpu as pltpu
from jax.sharding import Mesh
from jax.sharding import PartitionSpec as P

D = 2
D2 = 4
PHYS = 2
CHI = 96
WIDE = D2 * CHI
OPS = 4
TERMS = 16
GROUP = 4
ROWS = ("rows_0", "rows_1", "rows_2")
COLS = ("cols_0", "cols_1")
ROWS_COLS = ("rows_0", "rows_1", "rows_2", "cols_0", "cols_1")
MESH = pl.DeviceIdType.MESH

EPSILON = 1e-06
PRECISION_HIGH = lax.Precision.HIGHEST
F32 = jnp.float32
BF16 = jnp.bfloat16


def iota(shape, dim):
    return lax.broadcasted_iota(jnp.int32, shape, dim)


def halves(value):
    high = value.astype(BF16)
    low = (value - high.astype(F32)).astype(BF16)
    return high, low


def dot(left, right):
    return jnp.dot(left, right, preferred_element_type=F32)


def dot_nt(left, right):
    return lax.dot_general(left, right, (((1,), (1,)), ((), ())), preferred_element_type=F32)


def unpack(wide):
    one, two, three = wide[:, 0:128], wide[:, 128:256], wide[:, 256:384]
    lane = iota((CHI, 128), 1)
    parts = (
        one,
        pltpu.roll(jnp.where(lane >= 96, one, two), 32, 1),
        pltpu.roll(jnp.where(lane >= 64, two, three), 64, 1),
        pltpu.roll(three, 96, 1),
    )
    return [jnp.where(lane < CHI, part, 0.0) for part in parts]


def pack(tiles):
    lane = iota((CHI, 128), 1)
    first = tiles[0]
    second = pltpu.roll(tiles[1], 96, 1)
    third = pltpu.roll(tiles[2], 64, 1)
    fourth = pltpu.roll(tiles[3], 32, 1)
    return jnp.concatenate(
        [
            jnp.where(lane < 96, first, second),
            jnp.where(lane < 64, second, third),
            jnp.where(lane < 32, third, fourth),
        ],
        axis=1,
    )


def pick(mode, *choices):
    value = choices[-1]
    for index in range(len(choices) - 1):
        value = jnp.where(mode == index, choices[index], value)
    return value


def layer_rows(ket, legs):
    shape = (PHYS * 256, 32)
    row, col = iota(shape, 0), iota(shape, 1)
    digits = ((row >> 6) & 3, (row >> 4) & 3, (row >> 2) & 3, row & 3)
    up, left, down, right = legs(*digits)
    base = (row >> 8) * 16
    ket_at = base + (up >> 1) * 8 + (left >> 1) * 4 + (down >> 1) * 2 + (right >> 1)
    bra_at = base + (up & 1) * 8 + (left & 1) * 4 + (down & 1) * 2 + (right & 1)
    take = functools.partial(jnp.dot, precision=PRECISION_HIGH, preferred_element_type=F32)
    kets = take(jnp.where(col == ket_at, 1.0, 0.0), ket)
    bras = take(jnp.where(col == bra_at, 1.0, 0.0), ket)
    both = kets * bras
    full = both[0:256] + both[256:512]
    lane = iota((64, 128), 1)
    at = [full[64 * m : 64 * (m + 1)] for m in range(4)]
    return jnp.concatenate(
        [
            jnp.where(lane < 96, at[0], at[1]),
            jnp.where(lane < 64, at[1], at[2]),
            jnp.where(lane < 32, at[2], at[3]),
        ],
        axis=1,
    )


def thirds(value):
    high = value.astype(BF16)
    rest = value - high.astype(F32)
    middle = rest.astype(BF16)
    low = (rest - middle.astype(F32)).astype(BF16)
    return high, middle, low


def fold_first(spread, coeffs, folded, slot):
    def body(index, carried):
        total = None
        for leg in range(4):
            term = coeffs[pl.ds(index * 4 + leg, 1), :] * spread[leg]
            total = term if total is None else total + term
        high, middle, low = thirds(total)
        rows = pl.ds(pl.multiple_of(index * CHI, CHI), CHI)
        folded[slot, rows, 0:WIDE] = low
        folded[slot, rows, WIDE : 2 * WIDE] = high
        folded[slot, rows, 2 * WIDE : 3 * WIDE] = middle
        return carried

    lax.fori_loop(0, 16, body, 0)


def padded(parts):
    blank = jnp.zeros((32, parts[0].shape[1]), BF16)
    return jnp.concatenate([piece for part in parts for piece in (part, blank)], axis=0)


def apply_layer(state, scale, folded, second, third, slot, middle):
    high, mid, low = thirds(state)
    once = jnp.concatenate([high, mid], axis=1)
    main = jnp.concatenate([once, once], axis=0)
    fine = jnp.concatenate([high, low], axis=0)
    for leg in range(4):
        rows = slice(leg * WIDE, (leg + 1) * WIDE)
        wide = dot(folded[slot, rows, WIDE : 3 * WIDE], main)
        rest = dot(folded[slot, rows, 0 : 2 * WIDE], fine)
        high, mid, low = thirds(wide[:, 0:128] + (wide[:, 128:256] + rest))
        for index, part in enumerate((high, mid)):
            middle[:, leg * 256 + index * 128 : leg * 256 + index * 128 + 128] = part
        for index, part in enumerate((high, low)):
            begin = 1024 + leg * 256 + index * 128
            middle[:, begin : begin + 128] = part
    wide = dot(middle[:, 0:1024], second[slot])
    rest = dot(middle[:, 1024:2048], third[slot])
    return (wide[:, 0:128] + (wide[:, 128:256] + rest)) * scale


def nrm_scale(state):
    total = jnp.sum(jnp.sum(state * state, axis=0, keepdims=True), axis=1, keepdims=True)
    return lax.rsqrt(total * (1.0 / (CHI * WIDE)) + EPSILON)


def fold_pair(spread, coeffs, folded, slot):
    def body(index, carried):
        total = None
        for leg in range(4):
            term = coeffs[pl.ds(index * 4 + leg, 1), :] * spread[leg]
            total = term if total is None else total + term
        high, low = halves(total)
        rows = pl.ds(pl.multiple_of(index * CHI, CHI), CHI)
        folded[slot, rows, 0:WIDE] = high
        folded[slot, rows, WIDE : 2 * WIDE] = low
        return carried

    lax.fori_loop(0, 16, body, 0)


def apply_pair(state, scale, folded, second, slot, middle):
    high, low = halves(state)
    once = jnp.concatenate([high, low], axis=1)
    twice = jnp.concatenate([once, once], axis=0)
    for leg in range(4):
        wide = dot(folded[slot, leg * WIDE : (leg + 1) * WIDE, :], twice)
        high, low = halves(wide[:, 0:128] + wide[:, 128:256])
        middle[:, leg * 256 : leg * 256 + 128] = high
        middle[:, leg * 256 + 128 : leg * 256 + 256] = low
    wide = dot(middle[:, 0:1024], second[slot])
    return (wide[:, 0:128] + wide[:, 128:256]) * scale


def sweep_kernel(
    kets,
    left_maps,
    right_maps,
    top_edge,
    bottom_edge,
    left_edge,
    right_edge,
    outs,
    sides,
    row_kets,
    from_left,
    from_right,
    lefts,
    rights,
    ketses,
    select_one,
    select_two,
    spread,
    coeffs,
    folded,
    second,
    third,
    env_folded,
    env_second,
    middle,
    entered,
    leaving,
    state,
    normed,
    last_in,
    env_entered,
    env_leaving,
    env_normed,
    map_send,
    map_recv,
    hop_send,
    hop_recv,
    row_send,
    out_recv,
    side_recv,
    ket_send,
    ket_recv,
    env_send,
    env_recv,
    over_send,
    over_recv,
):
    z = lax.axis_index("rows_0")
    xl = lax.axis_index("rows_1")
    core = lax.axis_index("rows_2")
    y = lax.axis_index("cols_0")
    xh = lax.axis_index("cols_1")
    planes = lax.axis_size("rows_0")
    stations = lax.axis_size("cols_0")
    end = planes - 1
    at_edge = (z == 0) | (z == end)
    low = jnp.where(at_edge, z, 1 + 2 * (jnp.maximum(z - 1, 0) // 2))
    count = jnp.where(at_edge, GROUP, 2 * GROUP)
    col = xl
    is_worker = at_edge | (core == 1)
    way = jnp.where(z == 0, 1 - core, jnp.where(z == end, core, (z + 1) % 2))
    starts = ((way == 0) & (z == 0)) | ((way == 1) & (z == end))
    is_first = at_edge & starts
    is_last = at_edge & jnp.logical_not(starts)
    has_next = is_worker & jnp.logical_not(is_last)
    has_prev = is_worker & jnp.logical_not(is_first)
    mine = (z - low) * GROUP + xl * 2 + core
    place = xh * 2 + col
    ahead = jnp.where(way == 0, jnp.where(z == 0, 1, z + 2), jnp.where(z == end, end - 1, z - 2))
    ahead = jnp.clip(ahead, 0, end)
    after = (ahead, xl, jnp.where((ahead == 0) | (ahead == end), 0, 1), y, xh)
    behind = jnp.where(way == 0, jnp.where(z == 1, 0, z - 2), jnp.where(z == end - 1, end, z + 2))
    before = (jnp.clip(behind, 0, end), xl, 1, y, xh)
    mirror = jnp.where(z >= planes // 2, 1, 0)
    is_late = is_worker & (way != mirror)
    station_first = ((xh == 0) & (y == 0)) | ((xh == 1) & (y == stations - 1))
    station_last = ((xh == 0) & (y == stations - 1)) | ((xh == 1) & (y == 0))

    def member(slot, y_to, xh_to):
        return (low + slot // GROUP, (slot % GROUP) // 2, slot % 2, y_to, xh_to)

    def remote(source, target, send_sem, recv_sem, device):
        return pltpu.make_async_remote_copy(
            src_ref=source,
            dst_ref=target,
            send_sem=send_sem,
            recv_sem=recv_sem,
            device_id=device,
            device_id_type=MESH,
        )

    def arrived(target, sem):
        pltpu.make_async_copy(target, target, sem).wait()

    barrier = pltpu.get_barrier_semaphore()

    def greet(device):
        pl.semaphore_signal(barrier, inc=1, device_id=device, device_id_type=MESH)

    def greet_slot(slot, carried):
        @pl.when(slot != mine)
        def _():
            greet(member(slot, y, xh))

        greet(member(slot, y, 1 - xh))
        for step in (1, stations - 1):
            for xh_to in range(2):
                greet(member(slot, (y + step) % stations, xh_to))
        return carried

    lax.fori_loop(0, count, greet_slot, 0)

    @pl.when(has_next)
    def _():
        greet(after)

    @pl.when(has_prev)
    def _():
        greet(before)

    pl.semaphore_wait(
        barrier, 6 * count - 1 + jnp.where(has_next, 1, 0) + jnp.where(has_prev, 1, 0)
    )

    def chain(index):
        to_way = (index // 2 + jnp.where(z == end, 1, 0)) % 2
        to_col = index % 2
        to_start = ((to_way == 0) & (z == 0)) | ((to_way == 1) & (z == end))
        to_core = jnp.where(at_edge, jnp.where(to_start, 1, 0), 1)
        to_z = jnp.where(at_edge, z, low + to_way)
        own = (to_z == z) & (to_col == xl) & (to_core == core)
        return to_way, to_col, (to_z, to_col, to_core, y, xh), own

    def map_pairs(to_way, to_col):
        return (
            (left_maps.at[to_way, 0, to_col], lefts.at[mine]),
            (right_maps.at[to_way, 0, to_col], rights.at[mine]),
            (kets.at[to_col], ketses.at[mine]),
        )

    def send_map(index, carried):
        to_way, to_col, device, own = chain(index)

        @pl.when(own)
        def _():
            for kind, (source, target) in enumerate(map_pairs(to_way, to_col)):
                pltpu.make_async_copy(source, target, map_recv.at[mine, kind]).start()

        @pl.when(jnp.logical_not(own))
        def _():
            for kind, (source, target) in enumerate(map_pairs(to_way, to_col)):
                remote(
                    source, target, map_send.at[index, kind], map_recv.at[mine, kind], device
                ).start()

        return carried

    def map_sent(index, carried):
        to_way, to_col, device, own = chain(index)

        @pl.when(jnp.logical_not(own))
        def _():
            for kind, (source, target) in enumerate(map_pairs(to_way, to_col)):
                remote(
                    source, target, map_send.at[index, kind], map_recv.at[mine, kind], device
                ).wait_send()

        return carried

    lax.fori_loop(0, 4, send_map, 0)

    half = pl.ds(2 * xh, 2)

    def ket_across():
        device = (z, xl, core, y, 1 - xh)
        return remote(kets, row_kets.at[half], ket_send.at[0], ket_recv.at[xh], device)

    def ket_back():
        device = (z, xl, core, jnp.maximum(y - 1, 0), xh)
        return remote(kets.at[0], row_kets.at[4], ket_send.at[1], ket_recv.at[2], device)

    sends_back = (xh == 0) & (y > 0)
    extra = sends_back & (col == 0)
    gets_back = (xh == 0) & (y < stations - 1)
    ket_across().start()
    pltpu.make_async_copy(kets, row_kets.at[half], ket_recv.at[xh]).start()

    @pl.when(sends_back)
    def _():
        ket_back().start()

    @pl.when(is_worker)
    def _():
        for leg in range(4):
            row, lane = iota((WIDE, WIDE), 0), iota((WIDE, WIDE), 1)
            for _ in range(3):
                lane = jnp.where(lane >= CHI, lane - CHI, lane)
            select_one[:, leg * WIDE : (leg + 1) * WIDE] = jnp.where(
                row == 4 * lane + leg, 1.0, 0.0
            ).astype(BF16)
            row, lane = iota((256, WIDE), 0), iota((256, WIDE), 1)
            inner = row & 127
            select_two[leg * 256 : (leg + 1) * 256, :] = jnp.where(
                (lane == 4 * inner + leg) & (inner < CHI), 1.0, 0.0
            ).astype(BF16)

    @pl.when(is_first & (way == 0))
    def _():
        entered[...] = top_edge[col]

    @pl.when(is_first & (way == 1))
    def _():
        entered[...] = bottom_edge[col]


    def slot_at(number):
        return number + way * (count - 1 - 2 * number)

    def legs(m, g, o, f):
        return pick(way, m, o), f, pick(way, o, m), g

    def prepare(number):
        j = slot_at(number)
        for kind, target in enumerate((lefts, rights, ketses)):
            arrived(target.at[j], map_recv.at[j, kind])
        coeffs[...] = layer_rows(ketses[j], legs)
        apart = dot(jnp.concatenate(thirds(lefts[j]), axis=0), select_one[...])
        for leg in range(4):
            lanes = slice(leg * WIDE, (leg + 1) * WIDE)
            spread[leg] = apart[0:CHI, lanes] + (
                apart[CHI : 2 * CHI, lanes] + apart[2 * CHI : 3 * CHI, lanes]
            )
        high, mid, lowest = thirds(rights[j])
        main = dot_nt(select_two[...], padded((high, mid)))
        fine = dot_nt(select_two[...], padded((lowest,)))
        second[number] = main.astype(BF16)
        even = (iota((1024, 128), 0) & 128) == 0
        third[number] = jnp.where(even, fine, main[:, 0:128]).astype(BF16)
        fold_first(spread, coeffs, folded, number)

    def side_copy(number, source, xh_to, kind):
        return remote(
            source,
            sides.at[way, place],
            row_send.at[number, kind],
            side_recv.at[way, place],
            member(slot_at(number), y, xh_to),
        )

    def back_copy(number, source):
        return remote(
            source,
            sides.at[way, 4],
            row_send.at[number, 3],
            side_recv.at[way, 4],
            member(slot_at(number), jnp.maximum(y - 1, 0), xh),
        )

    def out_copy(number):
        return remote(
            normed.at[number + 1],
            outs.at[way, col],
            row_send.at[number, 2],
            out_recv.at[way, col],
            member(slot_at(number), y, xh),
        )

    def send_sides(number, source):
        own = slot_at(number) == mine

        @pl.when(own)
        def _():
            pltpu.make_async_copy(
                source, sides.at[way, place], side_recv.at[way, place]
            ).start()

        @pl.when(jnp.logical_not(own))
        def _():
            side_copy(number, source, xh, 0).start()

        side_copy(number, source, 1 - xh, 1).start()

        @pl.when(extra)
        def _():
            back_copy(number, source).start()

    def send_out(number, carried):
        own = slot_at(number) == mine

        @pl.when(own)
        def _():
            pltpu.make_async_copy(
                normed.at[number + 1], outs.at[way, col], out_recv.at[way, col]
            ).start()

        @pl.when(jnp.logical_not(own))
        def _():
            out_copy(number).start()

        return carried

    def hop():
        return remote(leaving, entered, hop_send, hop_recv, after)

    def tiles_of(value):
        return [value[leg * CHI : (leg + 1) * CHI] for leg in range(4)]

    def advance(number):
        @pl.when(number == 0)
        def _():
            @pl.when(has_prev)
            def _():
                arrived(entered, hop_recv)

            for leg, tile in enumerate(unpack(entered[...])):
                state[leg * CHI : (leg + 1) * CHI, :] = tile

        raw = is_first & (number == 0)
        closes = is_last & (number == count - 1)

        @pl.when(closes)
        def _():
            held = state[...]
            last_in[...] = pack(tiles_of(held)) * nrm_scale(held)
            send_sides(number, last_in)

        current = state[...]
        scale = jnp.where(raw, 1.0, nrm_scale(current))
        renewed = apply_layer(current, scale, folded, second, third, number, middle)
        normed[number] = pack(tiles_of(current)) * scale
        state[...] = renewed

        @pl.when(number == count - 1)
        def _():
            final = state[...]
            leaving[...] = pack(tiles_of(final))

            @pl.when(has_next)
            def _():
                hop().start()

            normed[count] = leaving[...] * nrm_scale(final)

        @pl.when(jnp.logical_not(closes))
        def _():
            send_sides(number, normed.at[number])

        @pl.when(number == count - 1)
        def _():
            lax.fori_loop(0, count, send_out, 0)


    def column_at(number):
        return number + xh * (3 - 2 * number)

    def env_legs(m, g, o, f):
        return pick(mirror, f, g), pick(xh, m, o), pick(mirror, g, f), pick(xh, o, m)

    def env_selects():
        for part in range(2):
            arrived(row_kets.at[pl.ds(2 * part, 2)], ket_recv.at[part])

        @pl.when(xh == 0)
        def _():
            row, lane = iota((2 * CHI, WIDE), 0), iota((2 * CHI, WIDE), 1)
            row = jnp.where(row >= CHI, row - CHI, row)
            for _ in range(3):
                lane = jnp.where(lane >= CHI, lane - CHI, lane)
            select_one[0 : 2 * CHI, 0:WIDE] = jnp.where(row == lane, 1.0, 0.0).astype(BF16)

        @pl.when(xh == 1)
        def _():
            for leg in range(4):
                row, lane = iota((WIDE, WIDE), 0), iota((WIDE, WIDE), 1)
                for _ in range(3):
                    lane = jnp.where(lane >= CHI, lane - CHI, lane)
                select_one[:, leg * WIDE : (leg + 1) * WIDE] = jnp.where(
                    row == leg * CHI + lane, 1.0, 0.0
                ).astype(BF16)
                row, lane = iota((256, WIDE), 0), iota((256, WIDE), 1)
                inner = row & 127
                select_two[leg * 256 : (leg + 1) * 256, :] = jnp.where(
                    (lane == leg * CHI + inner) & (inner < CHI), 1.0, 0.0
                ).astype(BF16)

    def env_fold(number):
        @pl.when(number == 0)
        def _():
            env_selects()

        column = column_at(number)
        arrived(sides.at[mirror, column], side_recv.at[mirror, column])
        coeffs[...] = layer_rows(row_kets[column], env_legs)
        early = jnp.concatenate(halves(sides[mirror, column]), axis=0)

        @pl.when(xh == 0)
        def _():
            turned = lax.dot_general(
                early,
                select_one[0 : 2 * CHI, 0:WIDE],
                (((0,), (0,)), ((), ())),
                preferred_element_type=F32,
            )
            for leg in range(4):
                spread[leg] = turned[leg * CHI : (leg + 1) * CHI]

        @pl.when(xh == 1)
        def _():
            apart = dot(early, select_one[...])
            for leg in range(4):
                lanes = slice(leg * WIDE, (leg + 1) * WIDE)
                spread[leg] = apart[0:CHI, lanes] + apart[CHI : 2 * CHI, lanes]

        fold_pair(spread, coeffs, env_folded, number)

    def env_prepare(number):
        column = column_at(number)
        arrived(sides.at[1 - mirror, column], side_recv.at[1 - mirror, column])

        @pl.when(xh == 0)
        def _():
            for leg, tile in enumerate(unpack(sides[1 - mirror, column])):
                high, lowest = halves(tile)
                both = jnp.concatenate(
                    [jnp.concatenate([high, lowest], axis=1), jnp.zeros((32, 256), BF16)], axis=0
                )
                env_second[number, leg * 256 : leg * 256 + 128, :] = both
                env_second[number, leg * 256 + 128 : leg * 256 + 256, :] = both

        @pl.when(xh == 1)
        def _():
            late = padded(halves(sides[1 - mirror, column]))
            env_second[number] = dot_nt(select_two[...], late).astype(BF16)

    def env_hop():
        device = (z, xl, core, jnp.clip(y + 1 - 2 * xh, 0, stations - 1), xh)
        return remote(env_leaving, env_entered, env_send, env_recv, device)

    def over(number):
        column = column_at(number)
        wraps = column == 0
        slot = jnp.where(wraps, 3, jnp.maximum(column - 1, 0))
        y_to = jnp.where(wraps, jnp.maximum(y - 1, 0), y)
        return remote(
            env_normed.at[number],
            from_right.at[slot],
            over_send.at[number],
            over_recv.at[slot],
            (z, xl, core, y_to, 0),
        )

    def sends_over(number):
        return (xh == 1) & ((y > 0) | (column_at(number) > 0))

    def flipped(tile):
        square = jnp.concatenate([tile, jnp.zeros((32, 128), F32)], axis=0)
        return square.T[0:CHI, :]

    def env_advance(number):
        @pl.when(number == 0)
        def _():
            @pl.when(jnp.logical_not(station_first))
            def _():
                arrived(env_entered, env_recv)
                for leg, tile in enumerate(unpack(env_entered[...])):
                    state[leg * CHI : (leg + 1) * CHI, :] = tile

            @pl.when(station_first)
            def _():
                edge = jnp.where(xh == 0, left_edge[0], right_edge[0])
                for leg, tile in enumerate(unpack(edge)):
                    state[leg * CHI : (leg + 1) * CHI, :] = jnp.where(
                        mirror == 1, flipped(tile), tile
                    )

        raw = station_first & (number == 0)

        @pl.when(jnp.logical_not(station_last & (number >= 2)))
        def _():
            current = state[...]
            scale = jnp.where(raw, 1.0, nrm_scale(current))
            renewed = apply_pair(current, scale, env_folded, env_second, number, middle)
            env_normed[number] = pack(tiles_of(current)) * scale
            state[...] = renewed

        @pl.when(station_last & (number >= 2))
        def _():
            current = state[...]
            env_normed[number] = pack(tiles_of(current)) * nrm_scale(current)

        @pl.when(jnp.logical_not(station_last) & (number == 3))
        def _():
            env_leaving[...] = pack(tiles_of(state[...]))
            env_hop().start()

        @pl.when(xh == 0)
        def _():
            from_left[number] = env_normed[number]

        @pl.when(sends_over(number))
        def _():
            over(number).start()


    total = jnp.where(is_worker, 2 * count, 0)
    before_fold = jnp.where(is_late, count, total)

    def task(index, carried):
        folds = (index >= before_fold) & (index < before_fold + 4)
        on_env = index >= total + 4
        on_boundary = jnp.logical_not(folds) & jnp.logical_not(on_env)
        step = jnp.where(index < before_fold, index, index - 4)
        prepares = (is_first & (step % 2 == 0)) | (jnp.logical_not(is_first) & (step < count))

        @pl.when(on_boundary & prepares)
        def _():
            prepare(jnp.where(is_first, step // 2, jnp.clip(step, 0, count - 1)))

        @pl.when(on_boundary & jnp.logical_not(prepares))
        def _():
            advance(jnp.where(is_first, step // 2, jnp.clip(step - count, 0, count - 1)))

        @pl.when(folds)
        def _():
            env_fold(jnp.clip(index - before_fold, 0, 3))

        late = index - (total + 4)
        readies = (station_first & (late % 2 == 0)) | (
            jnp.logical_not(station_first) & (late < 4)
        )

        @pl.when(on_env & readies)
        def _():
            env_prepare(jnp.where(station_first, late // 2, jnp.clip(late, 0, 3)))

        @pl.when(on_env & jnp.logical_not(readies))
        def _():
            env_advance(jnp.where(station_first, late // 2, jnp.clip(late - 4, 0, 3)))

        return carried

    lax.fori_loop(0, total + 12, task, 0)


    lax.fori_loop(0, 4, map_sent, 0)

    @pl.when(has_next)
    def _():
        hop().wait_send()

    def row_sent(number, carried):
        source = normed.at[number]
        side_copy(number, source, 1 - xh, 1).wait_send()

        @pl.when(extra)
        def _():
            back_copy(number, source).wait_send()

        @pl.when(slot_at(number) != mine)
        def _():
            side_copy(number, source, xh, 0).wait_send()
            out_copy(number).wait_send()

        return carried

    lax.fori_loop(0, total // 2, row_sent, 0)
    ket_across().wait_send()

    @pl.when(sends_back)
    def _():
        ket_back().wait_send()

    @pl.when(jnp.logical_not(station_last))
    def _():
        env_hop().wait_send()

    for number in range(4):

        @pl.when(sends_over(number))
        def _():
            over(number).wait_send()

    for direction in range(2):
        for column in range(2):
            arrived(outs.at[direction, column], out_recv.at[direction, column])

    @pl.when(gets_back)
    def _():
        for direction in range(2):
            arrived(sides.at[direction, 4], side_recv.at[direction, 4])
        arrived(row_kets.at[4], ket_recv.at[2])

    @pl.when(xh == 0)
    def _():
        for slot in range(3):
            arrived(from_right.at[slot], over_recv.at[slot])

    @pl.when(gets_back)
    def _():
        arrived(from_right.at[3], over_recv.at[3])


def run_sweep(kets, left_maps, right_maps, top_edge, bottom_edge, left_edge, right_edge):
    vmem = pl.BlockSpec(memory_space=pltpu.VMEM)
    anywhere = pl.BlockSpec(memory_space=pl.ANY)
    column = (CHI, WIDE)
    most = 2 * GROUP
    dma = pltpu.SemaphoreType.DMA
    return pl.pallas_call(
        sweep_kernel,
        out_shape=(
            jax.ShapeDtypeStruct((2, 2) + column, F32),
            jax.ShapeDtypeStruct((2, 5) + column, F32),
            jax.ShapeDtypeStruct((5, 32, 128), F32),
            jax.ShapeDtypeStruct((4,) + column, F32),
            jax.ShapeDtypeStruct((4,) + column, F32),
        ),
        in_specs=[vmem, anywhere, anywhere] + [vmem] * 4,
        out_specs=(vmem,) * 5,
        scratch_shapes=[
            pltpu.VMEM((most,) + column, F32),
            pltpu.VMEM((most,) + column, F32),
            pltpu.VMEM((most, 32, 128), F32),
            pltpu.VMEM((WIDE, 4 * WIDE), BF16),
            pltpu.VMEM((1024, WIDE), BF16),
            pltpu.VMEM((4,) + column, F32),
            pltpu.VMEM((64, WIDE), F32),
            pltpu.VMEM((most, 16 * CHI, 3 * WIDE), BF16),
            pltpu.VMEM((most, 1024, 256), BF16),
            pltpu.VMEM((most, 1024, 128), BF16),
            pltpu.VMEM((4, 16 * CHI, 2 * WIDE), BF16),
            pltpu.VMEM((4, 1024, 256), BF16),
            pltpu.VMEM((WIDE, 2048), BF16),
            pltpu.VMEM(column, F32),
            pltpu.VMEM(column, F32),
            pltpu.VMEM((WIDE, 128), F32),
            pltpu.VMEM((most + 1,) + column, F32),
            pltpu.VMEM(column, F32),
            pltpu.VMEM(column, F32),
            pltpu.VMEM(column, F32),
            pltpu.VMEM((4,) + column, F32),
            dma((4, 3)),
            dma((most, 3)),
            dma,
            dma,
            dma((most, 4)),
            dma((2, 2)),
            dma((2, 5)),
            dma((2,)),
            dma((3,)),
            dma,
            dma,
            dma((4,)),
            dma((4,)),
        ],
        compiler_params=pltpu.CompilerParams(
            collective_id=0, has_side_effects=True, vmem_limit_bytes=67043328
        ),
        name="sweep",
    )(kets, left_maps, right_maps, top_edge, bottom_edge, left_edge, right_edge)


def dot_general(left, right, dims):
    return lax.dot_general(left, right, (dims, ((), ())), preferred_element_type=F32)


def pad_rows(value):
    return jnp.concatenate([value, jnp.zeros((32, value.shape[1]), value.dtype)], axis=0)


def swap_legs(entry):
    return (entry & 0b10101) | ((entry >> 3) & 1) << 1 | ((entry >> 1) & 1) << 3


def open_site(ket, legs_at, wide, opened):
    def body(block, carried):
        begin = pl.multiple_of(block * 8, 8)
        half_done = {}
        for bra in range(8):
            u2, m2, d2 = bra >> 2, (bra >> 1) & 1, bra & 1
            tiles = []
            for top in range(8):
                u, m, d = top >> 2, (top >> 1) & 1, top & 1
                row = (2 * m + m2) * 4 + 2 * u + u2
                lane = (2 * d + d2) * 128
                tiles.append(wide[pl.ds(row * CHI + begin, 8), lane : lane + 128])
            for state in range(2):
                for out in range(2):
                    total = None
                    for top in range(8):
                        at = state * 16 + legs_at(top >> 2, (top >> 1) & 1, top & 1, out)
                        term = ket[at : at + 1, :] * tiles[top]
                        total = term if total is None else total + term
                    half_done[state, out, bra] = total
        for state in range(2):
            for out in range(2):
                for other in range(2):
                    for out2 in range(2):
                        total = None
                        for bra in range(8):
                            at = other * 16 + legs_at(bra >> 2, (bra >> 1) & 1, bra & 1, out2)
                            term = ket[at : at + 1, :] * half_done[state, out, bra]
                            total = term if total is None else total + term
                        row = (2 * out + out2) * CHI
                        opened[state * 2 + other, pl.ds(row + begin, 8), :] = total
        return carried

    lax.fori_loop(0, CHI // 8, body, 0)


def energy_kernel(
    term_rows,
    term_bonds,
    term_ops,
    operators,
    sides,
    row_kets,
    from_left,
    from_right,
    shares,
    wide,
    opened,
    closing,
    density,
    ket,
):
    way = lax.axis_index("cols_1")
    row_here = (
        lax.axis_index("rows_0") * GROUP + lax.axis_index("rows_1") * 2 + lax.axis_index("rows_2")
    )
    first = lax.axis_index("cols_0") * 4
    planes = lax.axis_size("rows_0")
    mirror = jnp.where(lax.axis_index("rows_0") >= planes // 2, 1, 0)

    def take_ket(column):
        for entry in range(32):
            ket[entry : entry + 1, :] = jnp.where(
                mirror == 1,
                row_kets[column, swap_legs(entry) : swap_legs(entry) + 1, :],
                row_kets[column, entry : entry + 1, :],
            )

    shares[...] = jnp.zeros((8, 128), F32)

    def hits(term, column):
        here = (term_rows[term] == row_here) & (term_bonds[term] == first + column)
        return here & (way == 0)

    def column_body(column, carried):
        count = 0
        for term in range(TERMS):
            count = count + jnp.where(hits(term, column), 1, 0)

        @pl.when(count > 0)
        def _():
            high, low = halves(sides[mirror, column])
            both = jnp.concatenate([high, low], axis=0)
            state_high, state_low = halves(jnp.concatenate(unpack(from_left[column]), axis=1))
            tn = ((0,), (0,))
            joined = dot_general(
                both, jnp.concatenate([state_high, state_high], axis=0), tn
            ) + dot_general(both, jnp.concatenate([state_low, state_low], axis=0), tn)
            below_high, below_low = halves(jnp.concatenate(unpack(sides[1 - mirror, column]), axis=1))
            main = jnp.concatenate([pad_rows(below_high), pad_rows(below_high)], axis=0)
            fine = jnp.concatenate([pad_rows(below_low), pad_rows(below_low)], axis=0)
            for leg in range(4):
                part = jnp.concatenate(halves(joined[:, leg * 128 : (leg + 1) * 128]), axis=1)
                wide[leg * WIDE : (leg + 1) * WIDE, :] = dot(part, main) + dot(part, fine)
            take_ket(column)
            open_site(
                ket,
                lambda u, m, d, out: u * 8 + m * 4 + d * 2 + out,
                wide,
                opened,
            )

            right = column + 1
            above = jnp.concatenate(unpack(sides[mirror, right]), axis=0)
            both = jnp.concatenate(halves(above), axis=1)
            state_high, state_low = halves(jnp.concatenate(unpack(from_right[column]), axis=1))
            state_high, state_low = pad_rows(state_high), pad_rows(state_low)
            joined = dot(both, jnp.concatenate([state_high, state_high], axis=0)) + dot(
                both, jnp.concatenate([state_low, state_low], axis=0)
            )
            below_high, below_low = halves(
                jnp.concatenate([pad_rows(tile) for tile in unpack(sides[1 - mirror, right])], axis=0)
            )
            main = jnp.concatenate([below_high, below_high], axis=1)
            fine = jnp.concatenate([below_low, below_low], axis=1)
            for leg in range(4):
                part = jnp.concatenate(halves(joined[:, leg * 128 : (leg + 1) * 128]), axis=1)
                wide[leg * WIDE : (leg + 1) * WIDE, :] = dot_nt(part, main) + dot_nt(part, fine)
            take_ket(right)
            open_site(
                ket,
                lambda u, m, d, out: u * 8 + out * 4 + d * 2 + m,
                wide,
                closing,
            )

            for pair in range(4):
                for other in range(4):
                    product = opened[pair] * closing[other]
                    at = pair * 4 + other
                    density[at : at + 1, :] = jnp.sum(product, axis=0, keepdims=True)
            rho = jnp.sum(density[...], axis=1, keepdims=True)
            index = iota((16, 1), 0)
            diagonal = (index == 0) | (index == 3) | (index == 12) | (index == 15)
            trace = jnp.sum(jnp.where(diagonal, rho, 0.0), axis=0, keepdims=True)
            spread = jnp.sqrt(jnp.sum(rho * rho, axis=0, keepdims=True))
            bottom = jnp.maximum(jnp.abs(trace), 0.25 * spread)

            def term_body(term, kept):
                @pl.when(hits(term, column))
                def _():
                    chosen = jnp.zeros((16, 1), F32)
                    for entry in range(16):
                        chosen = jnp.where(
                            index == entry, operators[term_ops[term], entry], chosen
                        )
                    value = jnp.sum(chosen * rho, axis=0, keepdims=True) / bottom
                    lane = iota((8, 128), 1)
                    shares[...] = jnp.where(lane == term, value, shares[...])

                return kept

            lax.fori_loop(0, TERMS, term_body, 0)

        return carried

    lax.fori_loop(0, 4, column_body, 0)


def run_energies(term_rows, term_bonds, term_ops, operators, sides, row_kets, lefts, rights):
    vmem = pl.BlockSpec(memory_space=pltpu.VMEM)
    smem = pl.BlockSpec(memory_space=pltpu.SMEM)
    return pl.pallas_call(
        energy_kernel,
        out_shape=jax.ShapeDtypeStruct((8, 128), F32),
        in_specs=[smem] * 4 + [vmem] * 4,
        out_specs=vmem,
        scratch_shapes=[
            pltpu.VMEM((16 * CHI, 512), F32),
            pltpu.VMEM((4, WIDE, 128), F32),
            pltpu.VMEM((4, WIDE, 128), F32),
            pltpu.VMEM((16, 128), F32),
            pltpu.VMEM((32, 128), F32),
        ],
        compiler_params=pltpu.CompilerParams(vmem_limit_bytes=32 * 1024 * 1024),
        name="energies",
    )(term_rows, term_bonds, term_ops, operators, sides, row_kets, lefts, rights)


def sum_kernel(shares, total, planes_in, plane_in, partial, send_one, recv_one, send_two, recv_two):
    z = lax.axis_index("rows_0")
    xl = lax.axis_index("rows_1")
    core = lax.axis_index("rows_2")
    y = lax.axis_index("cols_0")
    way = lax.axis_index("cols_1")
    place = y * 4 + xl * 2 + core
    barrier = pltpu.get_barrier_semaphore()

    def greet(device):
        pl.semaphore_signal(barrier, inc=1, device_id=device, device_id_type=MESH)

    def along(step):
        return ((z + step) % 8, xl, core, y, way)

    def within(step):
        other = (place * 2 + way + step) % 32
        return (z, (other // 4) % 2, (other // 2) % 2, other // 8, other % 2)

    for step in range(1, 8):
        greet(along(step))
    for step in range(1, 32):
        greet(within(step))
    pl.semaphore_wait(barrier, 38)

    def first(step):
        return pltpu.make_async_remote_copy(
            src_ref=shares,
            dst_ref=planes_in.at[z],
            send_sem=send_one.at[step],
            recv_sem=recv_one.at[z],
            device_id=along(step),
            device_id_type=MESH,
        )

    def second(step):
        return pltpu.make_async_remote_copy(
            src_ref=partial,
            dst_ref=plane_in.at[place],
            send_sem=send_two.at[step],
            recv_sem=recv_two.at[place],
            device_id=within(step),
            device_id_type=MESH,
        )

    @pl.when(way == 0)
    def _():
        for step in range(1, 8):
            first(step).start()
        pltpu.make_async_copy(shares, planes_in.at[z], recv_one.at[z]).start()
        added = None
        for plane in range(8):
            target = planes_in.at[plane]
            pltpu.make_async_copy(target, target, recv_one.at[plane]).wait()
        for plane in range(8):
            added = planes_in[plane] if added is None else added + planes_in[plane]
        partial[...] = added
        for step in range(1, 32):
            second(step).start()
        pltpu.make_async_copy(partial, plane_in.at[place], recv_two.at[place]).start()

    for other in range(16):
        target = plane_in.at[other]
        pltpu.make_async_copy(target, target, recv_two.at[other]).wait()
    added = None
    for other in range(16):
        added = plane_in[other] if added is None else added + plane_in[other]
    total[...] = added

    @pl.when(way == 0)
    def _():
        for step in range(1, 8):
            first(step).wait_send()
        for step in range(1, 32):
            second(step).wait_send()


def run_sum(shares):
    vmem = pl.BlockSpec(memory_space=pltpu.VMEM)
    return pl.pallas_call(
        sum_kernel,
        out_shape=jax.ShapeDtypeStruct((8, 128), F32),
        in_specs=[vmem],
        out_specs=vmem,
        scratch_shapes=[
            pltpu.VMEM((8, 8, 128), F32),
            pltpu.VMEM((16, 8, 128), F32),
            pltpu.VMEM((8, 128), F32),
            pltpu.SemaphoreType.DMA((8,)),
            pltpu.SemaphoreType.DMA((8,)),
            pltpu.SemaphoreType.DMA((32,)),
            pltpu.SemaphoreType.DMA((16,)),
        ],
        compiler_params=pltpu.CompilerParams(collective_id=2, has_side_effects=True),
        name="shares_sum",
    )(shares)


def shards(
    kets,
    left_maps,
    right_maps,
    top_edge,
    bottom_edge,
    left_edge,
    right_edge,
    term_rows,
    term_bonds,
    term_ops,
    operators,
):
    spread_kets = jnp.broadcast_to(kets[0][:, :, None], (kets.shape[1], 32, 128))
    outs, sides, row_kets, lefts, rights = run_sweep(
        spread_kets, left_maps, right_maps, top_edge, bottom_edge, left_edge, right_edge
    )
    shares = run_energies(
        term_rows, term_bonds, term_ops, operators, sides, row_kets, lefts, rights
    )
    energies = run_sum(shares)[0, :TERMS]
    return (outs[0][None], outs[1][None], energies)


def solution(mesh):
    torus = Mesh(
        mesh.devices.reshape(8, 2, 2, 4, 2), ("rows_0", "rows_1", "rows_2", "cols_0", "cols_1")
    )
    placed = (
        P(ROWS, COLS, None),
        P(None, ROWS, COLS, None, None),
        P(None, ROWS, COLS, None, None),
        P(COLS, None, None),
        P(COLS, None, None),
        P(ROWS, None, None),
        P(ROWS, None, None),
        P(),
        P(),
        P(),
        P(),
    )
    return jax.shard_map(
        shards,
        mesh=torus,
        in_specs=placed,
        out_specs=(P(ROWS, COLS, None, None), P(ROWS, COLS, None, None), P()),
        check_vma=False,
    )
```

time: 210 us -> 213 us (1.014); the launches traced: 207 us -> 213 us
  local copies, waits for them, and re-layouts: 7.46 us -> 11 us
    pallas_call x2 -> x1, Pallas kernels: 179 us -> 183 us  [run_sweep(): pl.pallas_call(sweep_kernel, out_shape=(jax.ShapeDtypeStruct((2, 2) + col...]
    unnamed x22 -> x20, local copies, waits for them, and re-layouts: 4.67 us -> 7.62 us
where the time goes in v3:
time: 213 us
  Pallas kernels  201 us (94%)
  local copies, waits for them, and re-layouts  11 us (5%)
    pallas_call x1, Pallas kernels, run_sweep(): pl.pallas_call(sweep_kernel, out_shape=(jax.ShapeDtypeStruct((2, 2) + col...  183 us
    pallas_call x1, Pallas kernels, run_sum(): pl.pallas_call(sum_kernel, out_shape=jax.ShapeDtypeStruct((8, 128), F32),...  17.7 us
    unnamed x20, local copies, waits for them, and re-layouts  7.62 us

profile of v3, /device:TPU:1, one launch (start us, length us, event | category | flops | bytes accessed | tf_op | source)
XLA Modules:
  0.0 212.8 jit_solution(12646743379431836105)
XLA Ops:
  0.6 1.4 broadcast_in_dim.8.kets
  2.0 182.5 %sweep.1 = (f32[2,2,96,384]{3,2,1,0:T(8,128)}, f32[2,5,96,384]{3,2,1,0:T(8,128)}, f32[5,32,128]{2,1,0:T(8,128)}, f32[4,96,384]{2,1,0:T(8,128)}, f32[4,96,384]{2,1,0:T(8,128)}) custom-call(f32[2,32,128]{2,1,0:T(8,128)} %broadcast_in_dim.8.kets, f32[2,1,2,96,384]{4,3,2,1,0:T(8,128)} %left_maps.1, f32[2,1,2,96,384]{4,3,2,1,0:T(8,128)} %right_maps.1, ...), custom_call_target="tpu_custom_call" | custom-call | tf_op jit(solution)/shard_map/sweep/pallas_call | solution.py:799
  184.5 0.0 copy-start
  184.5 1.4 copy-done
  185.9 0.0 copy-start.1
  185.9 1.1 copy-done.1
  187.0 0.0 copy-start.2
  187.0 1.1 copy-done.2
  188.0 0.0 copy-start.3
  188.0 0.9 copy-done.3
  188.9 0.0 copy-start.5
  188.9 0.7 copy-done.5
  189.6 0.7 copy-done.6
  190.2 0.0 copy-start.7
  190.2 0.7 copy-done.7
  190.9 0.0 copy-start.8
  190.9 0.7 copy-done.8
  191.6 0.8 energies.1.shares
  192.4 0.0 copy-start.4
  192.4 0.6 copy-done.4
  193.0 17.7 %shares_sum.1 = f32[8,128]{1,0:T(8,128)} custom-call(f32[8,128]{1,0:T(8,128)} %copy-done.4), custom_call_target="tpu_custom_call" | custom-call | tf_op jit(solution)/shard_map/shares_sum/pallas_call | solution.py:1123
  210.7 1.2 slice_bitcast_fusion
  211.9 0.0 copy-done.9
  211.9 0.9 fusion
  (2 shorter events, 0.0 us)
Async XLA Ops:
  184.5 1.4 copy-start
  185.9 1.1 copy-start.1
  187.0 1.1 copy-start.2
  188.0 0.9 copy-start.3
  188.9 0.7 copy-start.5
  189.6 0.7 copy-start.6
  190.2 0.7 copy-start.7
  190.9 0.7 copy-start.8
  191.6 20.3 %copy-start.9 = (f32[2,2,96,384]{3,2,1,0:T(8,128)S(1)}, f32[2,2,96,384]{3,2,1,0:T(8,128)}, u32[]{:S(2)}) copy-start(f32[2,2,96,384]{3,2,1,0:T(8,128)} %get-tuple-element.8) | copy-start | bytes 1769476
  192.4 0.6 copy-start.4

commit v4 on v3

--- a/solution.py
+++ b/solution.py
@@ -80,7 +80,7 @@
     return value
 
 
-def layer_rows(ket, legs):
+def layer_picks(legs):
     shape = (PHYS * 256, 32)
     row, col = iota(shape, 0), iota(shape, 1)
     digits = ((row >> 6) & 3, (row >> 4) & 3, (row >> 2) & 3, row & 3)
@@ -88,10 +88,15 @@
     base = (row >> 8) * 16
     ket_at = base + (up >> 1) * 8 + (left >> 1) * 4 + (down >> 1) * 2 + (right >> 1)
     bra_at = base + (up & 1) * 8 + (left & 1) * 4 + (down & 1) * 2 + (right & 1)
-    take = functools.partial(jnp.dot, precision=PRECISION_HIGH, preferred_element_type=F32)
-    kets = take(jnp.where(col == ket_at, 1.0, 0.0), ket)
-    bras = take(jnp.where(col == bra_at, 1.0, 0.0), ket)
-    both = kets * bras
+    return jnp.concatenate(
+        [jnp.where(col == ket_at, 1.0, 0.0), jnp.where(col == bra_at, 1.0, 0.0)], axis=0
+    ).astype(BF16)
+
+
+def layer_rows(ket, picks):
+    parts = dot(picks, jnp.concatenate(thirds(ket), axis=1))
+    taken = parts[:, 0:128] + (parts[:, 128:256] + parts[:, 256:384])
+    both = taken[0:512] * taken[512:1024]
     full = both[0:256] + both[256:512]
     lane = iota((64, 128), 1)
     at = [full[64 * m : 64 * (m + 1)] for m in range(4)]
@@ -207,6 +212,7 @@
     select_two,
     spread,
     coeffs,
+    picks,
     folded,
     second,
     third,
@@ -230,6 +236,9 @@
     side_recv,
     ket_send,
     ket_recv,
+    edge_send,
+    pass_send,
+    back_send,
     env_send,
     env_recv,
     over_send,
@@ -248,7 +257,7 @@
     count = jnp.where(at_edge, GROUP, 2 * GROUP)
     col = xl
     is_worker = at_edge | (core == 1)
-    way = jnp.where(z == 0, 1 - core, jnp.where(z == end, core, (z + 1) % 2))
+    way = jnp.where(z == 0, 1 - core, jnp.where(z == end, core, z % 2))
     starts = ((way == 0) & (z == 0)) | ((way == 1) & (z == end))
     is_first = at_edge & starts
     is_last = at_edge & jnp.logical_not(starts)
@@ -256,18 +265,25 @@
     has_prev = is_worker & jnp.logical_not(is_first)
     mine = (z - low) * GROUP + xl * 2 + core
     place = xh * 2 + col
-    ahead = jnp.where(way == 0, jnp.where(z == 0, 1, z + 2), jnp.where(z == end, end - 1, z - 2))
+    ahead = z + 2 - 4 * way
     ahead = jnp.clip(ahead, 0, end)
     after = (ahead, xl, jnp.where((ahead == 0) | (ahead == end), 0, 1), y, xh)
-    behind = jnp.where(way == 0, jnp.where(z == 1, 0, z - 2), jnp.where(z == end - 1, end, z + 2))
+    behind = jnp.where(
+        way == 0, jnp.where(z == end, end - 1, z - 2), jnp.where(z == 0, 1, z + 2)
+    )
     before = (jnp.clip(behind, 0, end), xl, 1, y, xh)
     mirror = jnp.where(z >= planes // 2, 1, 0)
-    is_late = is_worker & (way != mirror)
-    station_first = ((xh == 0) & (y == 0)) | ((xh == 1) & (y == stations - 1))
-    station_last = ((xh == 0) & (y == stations - 1)) | ((xh == 1) & (y == 0))
+    in_middle = (z == planes // 2) | (z == planes // 2 - 1)
+    is_late = is_worker & (way != mirror) & jnp.logical_not(in_middle)
+    station_first = ((core == 0) & (y == 0)) | ((core == 1) & (y == stations - 1))
+    station_last = ((core == 0) & (y == stations - 1)) | ((core == 1) & (y == 0))
+    leader = jnp.where(y >= stations // 2, 1, 0)
 
     def member(slot, y_to, xh_to):
         return (low + slot // GROUP, (slot % GROUP) // 2, slot % 2, y_to, xh_to)
+
+    def env_member(slot):
+        return (low + slot // GROUP, slot % 2, leader, y, (slot % GROUP) // 2)
 
     def remote(source, target, send_sem, recv_sem, device):
         return pltpu.make_async_remote_copy(
@@ -308,76 +324,8 @@
     def _():
         greet(before)
 
-    pl.semaphore_wait(
-        barrier, 6 * count - 1 + jnp.where(has_next, 1, 0) + jnp.where(has_prev, 1, 0)
-    )
-
-    def chain(index):
-        to_way = (index // 2 + jnp.where(z == end, 1, 0)) % 2
-        to_col = index % 2
-        to_start = ((to_way == 0) & (z == 0)) | ((to_way == 1) & (z == end))
-        to_core = jnp.where(at_edge, jnp.where(to_start, 1, 0), 1)
-        to_z = jnp.where(at_edge, z, low + to_way)
-        own = (to_z == z) & (to_col == xl) & (to_core == core)
-        return to_way, to_col, (to_z, to_col, to_core, y, xh), own
-
-    def map_pairs(to_way, to_col):
-        return (
-            (left_maps.at[to_way, 0, to_col], lefts.at[mine]),
-            (right_maps.at[to_way, 0, to_col], rights.at[mine]),
-            (kets.at[to_col], ketses.at[mine]),
-        )
-
-    def send_map(index, carried):
-        to_way, to_col, device, own = chain(index)
-
-        @pl.when(own)
-        def _():
-            for kind, (source, target) in enumerate(map_pairs(to_way, to_col)):
-                pltpu.make_async_copy(source, target, map_recv.at[mine, kind]).start()
-
-        @pl.when(jnp.logical_not(own))
-        def _():
-            for kind, (source, target) in enumerate(map_pairs(to_way, to_col)):
-                remote(
-                    source, target, map_send.at[index, kind], map_recv.at[mine, kind], device
-                ).start()
-
-        return carried
-
-    def map_sent(index, carried):
-        to_way, to_col, device, own = chain(index)
-
-        @pl.when(jnp.logical_not(own))
-        def _():
-            for kind, (source, target) in enumerate(map_pairs(to_way, to_col)):
-                remote(
-                    source, target, map_send.at[index, kind], map_recv.at[mine, kind], device
-                ).wait_send()
-
-        return carried
-
-    lax.fori_loop(0, 4, send_map, 0)
-
-    half = pl.ds(2 * xh, 2)
-
-    def ket_across():
-        device = (z, xl, core, y, 1 - xh)
-        return remote(kets, row_kets.at[half], ket_send.at[0], ket_recv.at[xh], device)
-
-    def ket_back():
-        device = (z, xl, core, jnp.maximum(y - 1, 0), xh)
-        return remote(kets.at[0], row_kets.at[4], ket_send.at[1], ket_recv.at[2], device)
-
-    sends_back = (xh == 0) & (y > 0)
-    extra = sends_back & (col == 0)
-    gets_back = (xh == 0) & (y < stations - 1)
-    ket_across().start()
-    pltpu.make_async_copy(kets, row_kets.at[half], ket_recv.at[xh]).start()
-
-    @pl.when(sends_back)
-    def _():
-        ket_back().start()
+    def legs(m, g, o, f):
+        return pick(way, m, o), f, pick(way, o, m), g
 
     @pl.when(is_worker)
     def _():
@@ -388,11 +336,105 @@
             select_one[:, leg * WIDE : (leg + 1) * WIDE] = jnp.where(
                 row == 4 * lane + leg, 1.0, 0.0
             ).astype(BF16)
-            row, lane = iota((256, WIDE), 0), iota((256, WIDE), 1)
-            inner = row & 127
-            select_two[leg * 256 : (leg + 1) * 256, :] = jnp.where(
-                (lane == 4 * inner + leg) & (inner < CHI), 1.0, 0.0
+            row, lane = iota((128, WIDE), 0), iota((128, WIDE), 1)
+            select_two[leg * 128 : (leg + 1) * 128, :] = jnp.where(
+                (lane == 4 * row + leg) & (row < CHI), 1.0, 0.0
             ).astype(BF16)
+        picks[...] = layer_picks(legs)
+
+    pl.semaphore_wait(
+        barrier, 6 * count - 1 + jnp.where(has_next, 1, 0) + jnp.where(has_prev, 1, 0)
+    )
+
+    def chain(index):
+        to_way = (index // 2 + jnp.where(z == end, 1, 0)) % 2
+        to_col = index % 2
+        to_start = ((to_way == 0) & (z == 0)) | ((to_way == 1) & (z == end))
+        to_core = jnp.where(at_edge, jnp.where(to_start, 1, 0), 1)
+        to_z = jnp.where(at_edge, z, low + 1 - to_way)
+        own = (to_z == z) & (to_col == xl) & (to_core == core)
+        return to_way, to_col, (to_z, to_col, to_core, y, xh), own
+
+    def map_pairs(to_way, to_col):
+        return (
+            (left_maps.at[to_way, 0, to_col], lefts.at[mine]),
+            (right_maps.at[to_way, 0, to_col], rights.at[mine]),
+            (kets.at[to_col], ketses.at[mine]),
+        )
+
+    def send_map(index, carried):
+        to_way, to_col, device, own = chain(index)
+
+        @pl.when(own)
+        def _():
+            for kind, (source, target) in enumerate(map_pairs(to_way, to_col)):
+                pltpu.make_async_copy(source, target, map_recv.at[mine, kind]).start()
+
+        @pl.when(jnp.logical_not(own))
+        def _():
+            for kind, (source, target) in enumerate(map_pairs(to_way, to_col)):
+                remote(
+                    source, target, map_send.at[index, kind], map_recv.at[mine, kind], device
+                ).start()
+
+        return carried
+
+    def map_sent(index, carried):
+        to_way, to_col, device, own = chain(index)
+
+        @pl.when(jnp.logical_not(own))
+        def _():
+            for kind, (source, target) in enumerate(map_pairs(to_way, to_col)):
+                remote(
+                    source, target, map_send.at[index, kind], map_recv.at[mine, kind], device
+                ).wait_send()
+
+        return carried
+
+    lax.fori_loop(0, 4, send_map, 0)
+
+    half = pl.ds(2 * xh, 2)
+    at_home = (core == xl) & (xl == xh)
+
+    def ket_copy(to_core):
+        device = (z, core, to_core, y, xl)
+        return remote(kets, row_kets.at[half], ket_send.at[to_core], ket_recv.at[xh], device)
+
+    def ket_back():
+        device = (z, core, 0, jnp.maximum(y - 1, 0), xl)
+        return remote(kets.at[0], row_kets.at[4], ket_send.at[2], ket_recv.at[2], device)
+
+    def edge_copy(edge, to_core):
+        return remote(edge.at[0], env_entered, edge_send, env_recv, (z, core, to_core, y, xl))
+
+    for to_core in range(2):
+
+        @pl.when(at_home & (core == to_core))
+        def _():
+            pltpu.make_async_copy(kets, row_kets.at[half], ket_recv.at[xh]).start()
+
+        @pl.when(jnp.logical_not(at_home & (core == to_core)))
+        def _():
+            ket_copy(to_core).start()
+
+    sends_back = (core == 0) & (y > 0)
+    gets_back = (core == 0) & (y < stations - 1)
+    kets_back = (xh == 0) & (y > 0)
+
+    @pl.when(kets_back)
+    def _():
+        ket_back().start()
+
+    edges = ((left_edge, 0, 0), (right_edge, 1, stations - 1))
+    for edge, to_core, y_of in edges:
+
+        @pl.when((y == y_of) & (xh == xl) & at_home & (core == to_core))
+        def _():
+            pltpu.make_async_copy(edge.at[0], env_entered, env_recv).start()
+
+        @pl.when((y == y_of) & (xh == xl) & jnp.logical_not(at_home & (core == to_core)))
+        def _():
+            edge_copy(edge, to_core).start()
 
     @pl.when(is_first & (way == 0))
     def _():
@@ -406,14 +448,13 @@
     def slot_at(number):
         return number + way * (count - 1 - 2 * number)
 
-    def legs(m, g, o, f):
-        return pick(way, m, o), f, pick(way, o, m), g
-
-    def prepare(number):
-        j = slot_at(number)
+    def prepare(step):
+        ordered = slot_at(step)
+        j = jnp.where(is_first, ordered, (mine + step) % count)
+        number = j + way * (count - 1 - 2 * j)
         for kind, target in enumerate((lefts, rights, ketses)):
             arrived(target.at[j], map_recv.at[j, kind])
-        coeffs[...] = layer_rows(ketses[j], legs)
+        coeffs[...] = layer_rows(ketses[j], picks[...])
         apart = dot(jnp.concatenate(thirds(lefts[j]), axis=0), select_one[...])
         for leg in range(4):
             lanes = slice(leg * WIDE, (leg + 1) * WIDE)
@@ -423,56 +464,49 @@
         high, mid, lowest = thirds(rights[j])
         main = dot_nt(select_two[...], padded((high, mid)))
         fine = dot_nt(select_two[...], padded((lowest,)))
-        second[number] = main.astype(BF16)
-        even = (iota((1024, 128), 0) & 128) == 0
-        third[number] = jnp.where(even, fine, main[:, 0:128]).astype(BF16)
+        main, fine = main.astype(BF16), fine.astype(BF16)
+        for leg in range(4):
+            rows = slice(leg * 128, (leg + 1) * 128)
+            for copy in range(2):
+                begin = leg * 256 + copy * 128
+                second[number, begin : begin + 128, :] = main[rows]
+            third[number, leg * 256 : leg * 256 + 128, :] = fine[rows]
+            third[number, leg * 256 + 128 : leg * 256 + 256, :] = main[rows, 0:128]
         fold_first(spread, coeffs, folded, number)
 
-    def side_copy(number, source, xh_to, kind):
+    def side_copy(number, source):
         return remote(
             source,
             sides.at[way, place],
-            row_send.at[number, kind],
+            row_send.at[number, 0],
             side_recv.at[way, place],
-            member(slot_at(number), y, xh_to),
+            env_member(slot_at(number)),
         )
 
-    def back_copy(number, source):
-        return remote(
-            source,
-            sides.at[way, 4],
-            row_send.at[number, 3],
-            side_recv.at[way, 4],
-            member(slot_at(number), jnp.maximum(y - 1, 0), xh),
-        )
+    def side_own(number):
+        slot = slot_at(number)
+        same_core = (slot % 2 == xl) & (leader == core)
+        return (low + slot // GROUP == z) & same_core & ((slot % GROUP) // 2 == xh)
 
     def out_copy(number):
         return remote(
             normed.at[number + 1],
             outs.at[way, col],
-            row_send.at[number, 2],
+            row_send.at[number, 1],
             out_recv.at[way, col],
             member(slot_at(number), y, xh),
         )
 
     def send_sides(number, source):
-        own = slot_at(number) == mine
-
-        @pl.when(own)
+        @pl.when(side_own(number))
         def _():
             pltpu.make_async_copy(
                 source, sides.at[way, place], side_recv.at[way, place]
             ).start()
 
-        @pl.when(jnp.logical_not(own))
-        def _():
-            side_copy(number, source, xh, 0).start()
-
-        side_copy(number, source, 1 - xh, 1).start()
-
-        @pl.when(extra)
-        def _():
-            back_copy(number, source).start()
+        @pl.when(jnp.logical_not(side_own(number)))
+        def _():
+            side_copy(number, source).start()
 
     def send_out(number, carried):
         own = slot_at(number) == mine
@@ -541,16 +575,17 @@
 
 
     def column_at(number):
-        return number + xh * (3 - 2 * number)
+        return number + core * (3 - 2 * number)
 
     def env_legs(m, g, o, f):
-        return pick(mirror, f, g), pick(xh, m, o), pick(mirror, g, f), pick(xh, o, m)
+        return pick(mirror, f, g), pick(core, m, o), pick(mirror, g, f), pick(core, o, m)
 
     def env_selects():
         for part in range(2):
             arrived(row_kets.at[pl.ds(2 * part, 2)], ket_recv.at[part])
-
-        @pl.when(xh == 0)
+        picks[...] = layer_picks(env_legs)
+
+        @pl.when(core == 0)
         def _():
             row, lane = iota((2 * CHI, WIDE), 0), iota((2 * CHI, WIDE), 1)
             row = jnp.where(row >= CHI, row - CHI, row)
@@ -558,7 +593,7 @@
                 lane = jnp.where(lane >= CHI, lane - CHI, lane)
             select_one[0 : 2 * CHI, 0:WIDE] = jnp.where(row == lane, 1.0, 0.0).astype(BF16)
 
-        @pl.when(xh == 1)
+        @pl.when(core == 1)
         def _():
             for leg in range(4):
                 row, lane = iota((WIDE, WIDE), 0), iota((WIDE, WIDE), 1)
@@ -567,11 +602,34 @@
                 select_one[:, leg * WIDE : (leg + 1) * WIDE] = jnp.where(
                     row == leg * CHI + lane, 1.0, 0.0
                 ).astype(BF16)
-                row, lane = iota((256, WIDE), 0), iota((256, WIDE), 1)
-                inner = row & 127
-                select_two[leg * 256 : (leg + 1) * 256, :] = jnp.where(
-                    (lane == leg * CHI + inner) & (inner < CHI), 1.0, 0.0
+                row, lane = iota((128, WIDE), 0), iota((128, WIDE), 1)
+                select_two[leg * 128 : (leg + 1) * 128, :] = jnp.where(
+                    (lane == leg * CHI + row) & (row < CHI), 1.0, 0.0
                 ).astype(BF16)
+
+    def forward(side, column):
+        target = sides.at[side, column]
+        device = (z, xl, 1 - core, y, xh)
+        return remote(
+            target, target, pass_send.at[side, column], side_recv.at[side, column], device
+        )
+
+    def back(side):
+        device = (z, xl, core, jnp.maximum(y - 1, 0), xh)
+        return remote(
+            sides.at[side, 0], sides.at[side, 4], back_send.at[side], side_recv.at[side, 4], device
+        )
+
+    def take_side(side, column):
+        arrived(sides.at[side, column], side_recv.at[side, column])
+
+        @pl.when(core == leader)
+        def _():
+            forward(side, column).start()
+
+        @pl.when(sends_back & (column == 0))
+        def _():
+            back(side).start()
 
     def env_fold(number):
         @pl.when(number == 0)
@@ -579,11 +637,11 @@
             env_selects()
 
         column = column_at(number)
-        arrived(sides.at[mirror, column], side_recv.at[mirror, column])
-        coeffs[...] = layer_rows(row_kets[column], env_legs)
+        take_side(mirror, column)
+        coeffs[...] = layer_rows(row_kets[column], picks[...])
         early = jnp.concatenate(halves(sides[mirror, column]), axis=0)
 
-        @pl.when(xh == 0)
+        @pl.when(core == 0)
         def _():
             turned = lax.dot_general(
                 early,
@@ -594,7 +652,7 @@
             for leg in range(4):
                 spread[leg] = turned[leg * CHI : (leg + 1) * CHI]
 
-        @pl.when(xh == 1)
+        @pl.when(core == 1)
         def _():
             apart = dot(early, select_one[...])
             for leg in range(4):
@@ -605,9 +663,9 @@
 
     def env_prepare(number):
         column = column_at(number)
-        arrived(sides.at[1 - mirror, column], side_recv.at[1 - mirror, column])
-
-        @pl.when(xh == 0)
+        take_side(1 - mirror, column)
+
+        @pl.when(core == 0)
         def _():
             for leg, tile in enumerate(unpack(sides[1 - mirror, column])):
                 high, lowest = halves(tile)
@@ -617,13 +675,17 @@
                 env_second[number, leg * 256 : leg * 256 + 128, :] = both
                 env_second[number, leg * 256 + 128 : leg * 256 + 256, :] = both
 
-        @pl.when(xh == 1)
+        @pl.when(core == 1)
         def _():
             late = padded(halves(sides[1 - mirror, column]))
-            env_second[number] = dot_nt(select_two[...], late).astype(BF16)
+            turned = dot_nt(select_two[...], late).astype(BF16)
+            for leg in range(4):
+                for copy in range(2):
+                    begin = leg * 256 + copy * 128
+                    env_second[number, begin : begin + 128, :] = turned[leg * 128 : leg * 128 + 128]
 
     def env_hop():
-        device = (z, xl, core, jnp.clip(y + 1 - 2 * xh, 0, stations - 1), xh)
+        device = (z, xl, core, jnp.clip(y + 1 - 2 * core, 0, stations - 1), xh)
         return remote(env_leaving, env_entered, env_send, env_recv, device)
 
     def over(number):
@@ -636,11 +698,11 @@
             from_right.at[slot],
             over_send.at[number],
             over_recv.at[slot],
-            (z, xl, core, y_to, 0),
+            (z, xl, 0, y_to, xh),
         )
 
     def sends_over(number):
-        return (xh == 1) & ((y > 0) | (column_at(number) > 0))
+        return (core == 1) & ((y > 0) | (column_at(number) > 0))
 
     def flipped(tile):
         square = jnp.concatenate([tile, jnp.zeros((32, 128), F32)], axis=0)
@@ -649,19 +711,18 @@
     def env_advance(number):
         @pl.when(number == 0)
         def _():
-            @pl.when(jnp.logical_not(station_first))
+            arrived(env_entered, env_recv)
+            flips = station_first & (mirror == 1)
+
+            @pl.when(jnp.logical_not(flips))
             def _():
-                arrived(env_entered, env_recv)
                 for leg, tile in enumerate(unpack(env_entered[...])):
                     state[leg * CHI : (leg + 1) * CHI, :] = tile
 
-            @pl.when(station_first)
+            @pl.when(flips)
             def _():
-                edge = jnp.where(xh == 0, left_edge[0], right_edge[0])
-                for leg, tile in enumerate(unpack(edge)):
-                    state[leg * CHI : (leg + 1) * CHI, :] = jnp.where(
-                        mirror == 1, flipped(tile), tile
-                    )
+                for leg, tile in enumerate(unpack(env_entered[...])):
+                    state[leg * CHI : (leg + 1) * CHI, :] = flipped(tile)
 
         raw = station_first & (number == 0)
 
@@ -683,7 +744,7 @@
             env_leaving[...] = pack(tiles_of(state[...]))
             env_hop().start()
 
-        @pl.when(xh == 0)
+        @pl.when(core == 0)
         def _():
             from_left[number] = env_normed[number]
 
@@ -739,26 +800,44 @@
         hop().wait_send()
 
     def row_sent(number, carried):
-        source = normed.at[number]
-        side_copy(number, source, 1 - xh, 1).wait_send()
-
-        @pl.when(extra)
-        def _():
-            back_copy(number, source).wait_send()
+        @pl.when(jnp.logical_not(side_own(number)))
+        def _():
+            side_copy(number, normed.at[number]).wait_send()
 
         @pl.when(slot_at(number) != mine)
         def _():
-            side_copy(number, source, xh, 0).wait_send()
             out_copy(number).wait_send()
 
         return carried
 
     lax.fori_loop(0, total // 2, row_sent, 0)
-    ket_across().wait_send()
-
-    @pl.when(sends_back)
+
+    for to_core in range(2):
+
+        @pl.when(jnp.logical_not(at_home & (core == to_core)))
+        def _():
+            ket_copy(to_core).wait_send()
+
+    @pl.when(kets_back)
     def _():
         ket_back().wait_send()
+
+    for edge, to_core, y_of in edges:
+
+        @pl.when((y == y_of) & (xh == xl) & jnp.logical_not(at_home & (core == to_core)))
+        def _():
+            edge_copy(edge, to_core).wait_send()
+
+    for side in range(2):
+
+        @pl.when(core == leader)
+        def _():
+            for column in range(4):
+                forward(side, column).wait_send()
+
+        @pl.when(sends_back)
+        def _():
+            back(side).wait_send()
 
     @pl.when(jnp.logical_not(station_last))
     def _():
@@ -780,7 +859,7 @@
             arrived(sides.at[direction, 4], side_recv.at[direction, 4])
         arrived(row_kets.at[4], ket_recv.at[2])
 
-    @pl.when(xh == 0)
+    @pl.when(core == 0)
     def _():
         for slot in range(3):
             arrived(from_right.at[slot], over_recv.at[slot])
@@ -812,9 +891,10 @@
             pltpu.VMEM((most,) + column, F32),
             pltpu.VMEM((most, 32, 128), F32),
             pltpu.VMEM((WIDE, 4 * WIDE), BF16),
-            pltpu.VMEM((1024, WIDE), BF16),
+            pltpu.VMEM((512, WIDE), BF16),
             pltpu.VMEM((4,) + column, F32),
             pltpu.VMEM((64, WIDE), F32),
+            pltpu.VMEM((1024, 32), BF16),
             pltpu.VMEM((most, 16 * CHI, 3 * WIDE), BF16),
             pltpu.VMEM((most, 1024, 256), BF16),
             pltpu.VMEM((most, 1024, 128), BF16),
@@ -833,11 +913,14 @@
             dma((most, 3)),
             dma,
             dma,
-            dma((most, 4)),
+            dma((most, 2)),
             dma((2, 2)),
             dma((2, 5)),
+            dma((3,)),
+            dma((3,)),
+            dma,
+            dma((2, 4)),
             dma((2,)),
-            dma((3,)),
             dma,
             dma,
             dma((4,)),
@@ -903,20 +986,25 @@
     term_bonds,
     term_ops,
     operators,
-    sides,
-    row_kets,
-    from_left,
-    from_right,
+    all_sides,
+    all_kets,
+    all_left,
+    all_right,
     shares,
     wide,
     opened,
     closing,
     density,
     ket,
+    sides,
+    row_kets,
+    from_left,
+    from_right,
+    fetch,
 ):
-    way = lax.axis_index("cols_1")
+    way = lax.axis_index("rows_2")
     row_here = (
-        lax.axis_index("rows_0") * GROUP + lax.axis_index("rows_1") * 2 + lax.axis_index("rows_2")
+        lax.axis_index("rows_0") * GROUP + lax.axis_index("cols_1") * 2 + lax.axis_index("rows_1")
     )
     first = lax.axis_index("cols_0") * 4
     planes = lax.axis_size("rows_0")
@@ -943,20 +1031,33 @@
 
         @pl.when(count > 0)
         def _():
-            high, low = halves(sides[mirror, column])
+            copies = [
+                pltpu.make_async_copy(
+                    all_sides.at[:, pl.ds(column, 2)], sides, fetch.at[0]
+                ),
+                pltpu.make_async_copy(all_kets.at[pl.ds(column, 2)], row_kets, fetch.at[1]),
+                pltpu.make_async_copy(all_left.at[column], from_left, fetch.at[2]),
+                pltpu.make_async_copy(all_right.at[column], from_right, fetch.at[3]),
+            ]
+            for copy in copies:
+                copy.start()
+            for copy in copies:
+                copy.wait()
+
+            high, low = halves(sides[mirror, 0])
             both = jnp.concatenate([high, low], axis=0)
-            state_high, state_low = halves(jnp.concatenate(unpack(from_left[column]), axis=1))
+            state_high, state_low = halves(jnp.concatenate(unpack(from_left[...]), axis=1))
             tn = ((0,), (0,))
             joined = dot_general(
                 both, jnp.concatenate([state_high, state_high], axis=0), tn
             ) + dot_general(both, jnp.concatenate([state_low, state_low], axis=0), tn)
-            below_high, below_low = halves(jnp.concatenate(unpack(sides[1 - mirror, column]), axis=1))
+            below_high, below_low = halves(jnp.concatenate(unpack(sides[1 - mirror, 0]), axis=1))
             main = jnp.concatenate([pad_rows(below_high), pad_rows(below_high)], axis=0)
             fine = jnp.concatenate([pad_rows(below_low), pad_rows(below_low)], axis=0)
             for leg in range(4):
                 part = jnp.concatenate(halves(joined[:, leg * 128 : (leg + 1) * 128]), axis=1)
                 wide[leg * WIDE : (leg + 1) * WIDE, :] = dot(part, main) + dot(part, fine)
-            take_ket(column)
+            take_ket(0)
             open_site(
                 ket,
                 lambda u, m, d, out: u * 8 + m * 4 + d * 2 + out,
@@ -964,23 +1065,22 @@
                 opened,
             )
 
-            right = column + 1
-            above = jnp.concatenate(unpack(sides[mirror, right]), axis=0)
+            above = jnp.concatenate(unpack(sides[mirror, 1]), axis=0)
             both = jnp.concatenate(halves(above), axis=1)
-            state_high, state_low = halves(jnp.concatenate(unpack(from_right[column]), axis=1))
+            state_high, state_low = halves(jnp.concatenate(unpack(from_right[...]), axis=1))
             state_high, state_low = pad_rows(state_high), pad_rows(state_low)
             joined = dot(both, jnp.concatenate([state_high, state_high], axis=0)) + dot(
                 both, jnp.concatenate([state_low, state_low], axis=0)
             )
             below_high, below_low = halves(
-                jnp.concatenate([pad_rows(tile) for tile in unpack(sides[1 - mirror, right])], axis=0)
+                jnp.concatenate([pad_rows(tile) for tile in unpack(sides[1 - mirror, 1])], axis=0)
             )
             main = jnp.concatenate([below_high, below_high], axis=1)
             fine = jnp.concatenate([below_low, below_low], axis=1)
             for leg in range(4):
                 part = jnp.concatenate(halves(joined[:, leg * 128 : (leg + 1) * 128]), axis=1)
                 wide[leg * WIDE : (leg + 1) * WIDE, :] = dot_nt(part, main) + dot_nt(part, fine)
-            take_ket(right)
+            take_ket(1)
             open_site(
                 ket,
                 lambda u, m, d, out: u * 8 + out * 4 + d * 2 + m,
@@ -1027,7 +1127,7 @@
     return pl.pallas_call(
         energy_kernel,
         out_shape=jax.ShapeDtypeStruct((8, 128), F32),
-        in_specs=[smem] * 4 + [vmem] * 4,
+        in_specs=[smem] * 4 + [pl.BlockSpec(memory_space=pl.ANY)] * 4,
         out_specs=vmem,
         scratch_shapes=[
             pltpu.VMEM((16 * CHI, 512), F32),
@@ -1035,6 +1135,11 @@
             pltpu.VMEM((4, WIDE, 128), F32),
             pltpu.VMEM((16, 128), F32),
             pltpu.VMEM((32, 128), F32),
+            pltpu.VMEM((2, 2, CHI, WIDE), F32),
+            pltpu.VMEM((2, 32, 128), F32),
+            pltpu.VMEM((CHI, WIDE), F32),
+            pltpu.VMEM((CHI, WIDE), F32),
+            pltpu.SemaphoreType.DMA((4,)),
         ],
         compiler_params=pltpu.CompilerParams(vmem_limit_bytes=32 * 1024 * 1024),
         name="energies",
@@ -1046,19 +1151,20 @@
     xl = lax.axis_index("rows_1")
     core = lax.axis_index("rows_2")
     y = lax.axis_index("cols_0")
-    way = lax.axis_index("cols_1")
-    place = y * 4 + xl * 2 + core
+    xh = lax.axis_index("cols_1")
+    way = core
+    place = y * 4 + xl * 2 + xh
     barrier = pltpu.get_barrier_semaphore()
 
     def greet(device):
         pl.semaphore_signal(barrier, inc=1, device_id=device, device_id_type=MESH)
 
     def along(step):
-        return ((z + step) % 8, xl, core, y, way)
+        return ((z + step) % 8, xl, core, y, xh)
 
     def within(step):
         other = (place * 2 + way + step) % 32
-        return (z, (other // 4) % 2, (other // 2) % 2, other // 8, other % 2)
+        return (z, (other // 4) % 2, other % 2, other // 8, (other // 2) % 2)
 
     for step in range(1, 8):
         greet(along(step))

time: 213 us -> 180 us (0.85)
  Pallas kernels: 201 us -> 168 us
    pallas_call x1, Pallas kernels: 183 us -> 150 us  [run_sweep(): pl.pallas_call(sweep_kernel, out_shape=(jax.ShapeDtypeStruct((2, 2) + col...]
where the time goes in v4:
time: 180 us; the launch traced here: 179 us
  Pallas kernels  168 us (93%)
  local copies, waits for them, and re-layouts  11 us (6%)
    pallas_call x1, Pallas kernels, run_sweep(): pl.pallas_call(sweep_kernel, out_shape=(jax.ShapeDtypeStruct((2, 2) + col...  150 us
    pallas_call x1, Pallas kernels, run_sum(): pl.pallas_call(sum_kernel, out_shape=jax.ShapeDtypeStruct((8, 128), F32),...  17.2 us
    unnamed x20, local copies, waits for them, and re-layouts  7.62 us

profile of v4, /device:TPU:1, one launch (start us, length us, event | category | flops | bytes accessed | tf_op | source)
XLA Modules:
  0.0 179.3 jit_solution(12006479342349505807)
XLA Ops:
  0.6 1.4 broadcast_in_dim.8.kets
  2.0 149.6 %sweep.1 = (f32[2,2,96,384]{3,2,1,0:T(8,128)}, f32[2,5,96,384]{3,2,1,0:T(8,128)}, f32[5,32,128]{2,1,0:T(8,128)}, f32[4,96,384]{2,1,0:T(8,128)}, f32[4,96,384]{2,1,0:T(8,128)}) custom-call(f32[2,32,128]{2,1,0:T(8,128)} %broadcast_in_dim.8.kets, f32[2,1,2,96,384]{4,3,2,1,0:T(8,128)} %left_maps.1, f32[2,1,2,96,384]{4,3,2,1,0:T(8,128)} %right_maps.1, ...), custom_call_target="tpu_custom_call" | custom-call | tf_op jit(solution)/shard_map/sweep/pallas_call | solution.py:878
  151.6 0.0 copy-start
  151.6 1.4 copy-done
  152.9 0.0 copy-start.1
  152.9 1.1 copy-done.1
  154.0 0.0 copy-start.2
  154.0 1.1 copy-done.2
  155.1 0.0 copy-start.3
  155.1 0.9 copy-done.3
  155.9 0.0 copy-start.5
  156.0 0.7 copy-done.5
  156.6 0.0 copy-start.6
  156.6 0.7 copy-done.6
  157.3 0.0 copy-start.7
  157.3 0.7 copy-done.7
  157.9 0.7 copy-done.8
  158.6 0.9 energies.1.shares
  159.5 0.0 copy-start.4
  159.5 0.6 copy-done.4
  160.1 17.2 %shares_sum.1 = f32[8,128]{1,0:T(8,128)} custom-call(f32[8,128]{1,0:T(8,128)} %copy-done.4), custom_call_target="tpu_custom_call" | custom-call | tf_op jit(solution)/shard_map/shares_sum/pallas_call | solution.py:1229
  177.2 1.2 slice_bitcast_fusion
  178.4 0.0 copy-done.9
  178.4 0.9 fusion
  (2 shorter events, 0.0 us)
Async XLA Ops:
  151.6 1.4 copy-start
  152.9 1.1 copy-start.1
  154.0 1.1 copy-start.2
  155.1 0.9 copy-start.3
  155.9 0.7 copy-start.5
  156.6 0.7 copy-start.6
  157.3 0.7 copy-start.7
  157.9 0.7 copy-start.8
  158.6 19.8 %copy-start.9 = (f32[2,2,96,384]{3,2,1,0:T(8,128)S(1)}, f32[2,2,96,384]{3,2,1,0:T(8,128)}, u32[]{:S(2)}) copy-start(f32[2,2,96,384]{3,2,1,0:T(8,128)} %get-tuple-element.8) | copy-start | bytes 1769476
  159.5 0.6 copy-start.4

commit v5 on v4

--- a/solution.py
+++ b/solution.py
@@ -93,11 +93,15 @@
     ).astype(BF16)
 
 
-def layer_rows(ket, picks):
+def pair_values(ket, picks):
     parts = dot(picks, jnp.concatenate(thirds(ket), axis=1))
     taken = parts[:, 0:128] + (parts[:, 128:256] + parts[:, 256:384])
     both = taken[0:512] * taken[512:1024]
-    full = both[0:256] + both[256:512]
+    return both[0:256] + both[256:512]
+
+
+def layer_rows(ket, picks):
+    full = pair_values(ket, picks)
     lane = iota((64, 128), 1)
     at = [full[64 * m : 64 * (m + 1)] for m in range(4)]
     return jnp.concatenate(
@@ -118,20 +122,42 @@
     return high, middle, low
 
 
-def fold_first(spread, coeffs, folded, slot):
-    def body(index, carried):
-        total = None
-        for leg in range(4):
-            term = coeffs[pl.ds(index * 4 + leg, 1), :] * spread[leg]
-            total = term if total is None else total + term
-        high, middle, low = thirds(total)
-        rows = pl.ds(pl.multiple_of(index * CHI, CHI), CHI)
-        folded[slot, rows, 0:WIDE] = low
-        folded[slot, rows, WIDE : 2 * WIDE] = high
-        folded[slot, rows, 2 * WIDE : 3 * WIDE] = middle
-        return carried
-
-    lax.fori_loop(0, 16, body, 0)
+ROOT = 0.7071067811865476
+
+
+def symmetric(tiles):
+    return [tiles[0], (tiles[1] + tiles[2]) * ROOT, tiles[3], (tiles[1] - tiles[2]) * ROOT]
+
+
+def plain(tiles):
+    return [tiles[0], (tiles[1] + tiles[3]) * ROOT, (tiles[1] - tiles[3]) * ROOT, tiles[2]]
+
+
+def is_even(*legs):
+    return sum(leg == 3 for leg in legs) % 2 == 0
+
+
+def basis_turn():
+    row, col = iota((256, 256), 0), iota((256, 256), 1)
+    value = jnp.ones((256, 256), F32)
+    for to_shift, from_shift in ((6, 4), (4, 2), (2, 0), (0, 6)):
+        new, old = (row >> to_shift) & 3, (col >> from_shift) & 3
+        one = jnp.where(old == 1, 1.0, 0.0)
+        two = jnp.where(old == 2, 1.0, 0.0)
+        ends = jnp.where(new == 0, jnp.where(old == 0, 1.0, 0.0), jnp.where(old == 3, 1.0, 0.0))
+        middle = jnp.where(new == 1, one + two, one - two)
+        value = value * jnp.where((new & 1) == 0, ends, middle)
+    return value.astype(BF16)
+
+
+def even_rows(full, turn):
+    parts = dot(turn, jnp.concatenate(thirds(full), axis=1))
+    row = iota((256, 128), 0)
+    halved = (row & 1) + ((row >> 2) & 1) + ((row >> 4) & 1) + ((row >> 6) & 1)
+    factor = jnp.where((halved & 1) == 1, ROOT, 1.0) * jnp.where(
+        halved >= 4, 0.25, jnp.where(halved >= 2, 0.5, 1.0)
+    )
+    return (parts[:, 0:128] + (parts[:, 128:256] + parts[:, 256:384])) * factor
 
 
 def padded(parts):
@@ -139,21 +165,43 @@
     return jnp.concatenate([piece for part in parts for piece in (part, blank)], axis=0)
 
 
-def apply_layer(state, scale, folded, second, third, slot, middle):
-    high, mid, low = thirds(state)
-    once = jnp.concatenate([high, mid], axis=1)
-    main = jnp.concatenate([once, once], axis=0)
-    fine = jnp.concatenate([high, low], axis=0)
-    for leg in range(4):
-        rows = slice(leg * WIDE, (leg + 1) * WIDE)
-        wide = dot(folded[slot, rows, WIDE : 3 * WIDE], main)
-        rest = dot(folded[slot, rows, 0 : 2 * WIDE], fine)
-        high, mid, low = thirds(wide[:, 0:128] + (wide[:, 128:256] + rest))
-        for index, part in enumerate((high, mid)):
-            middle[:, leg * 256 + index * 128 : leg * 256 + index * 128 + 128] = part
-        for index, part in enumerate((high, low)):
-            begin = 1024 + leg * 256 + index * 128
-            middle[:, begin : begin + 128] = part
+def apply_layer(state, scale, first, layers, second, third, slot, joined, middle):
+    def side_by_side(part):
+        blank = jnp.zeros((32, 128), BF16)
+        return jnp.concatenate(
+            [
+                jnp.concatenate([part[leg * CHI : (leg + 1) * CHI], blank], axis=0)
+                for leg in range(4)
+            ],
+            axis=1,
+        )
+
+    high, mid, low = (side_by_side(part) for part in thirds(state))
+    joined[...] = dot(first[slot], jnp.concatenate([high, high, mid, mid, high, low], axis=0))
+    block = 16
+    for begin in range(0, CHI, block):
+        tiles = {}
+        for f in range(4):
+            for m in range(4):
+                rows = slice(f * CHI + begin, f * CHI + begin + block)
+                tiles[f, m] = joined[rows, m * 128 : (m + 1) * 128]
+        for g in range(4):
+            for o in range(4):
+                total = None
+                for f in range(4):
+                    for m in range(4):
+                        if is_even(g, o, f, m):
+                            at = ((g * 4 + o) * 4 + f) * 4 + m
+                            term = layers[slot, at : at + 1, :] * tiles[f, m]
+                            total = term if total is None else total + term
+                high, mid, low = thirds(total)
+                rows = slice(o * CHI + begin, o * CHI + begin + block)
+                for index, part in enumerate((high, mid)):
+                    lane = g * 256 + index * 128
+                    middle[rows, lane : lane + 128] = part
+                for index, part in enumerate((high, low)):
+                    lane = 1024 + g * 256 + index * 128
+                    middle[rows, lane : lane + 128] = part
     wide = dot(middle[:, 0:1024], second[slot])
     rest = dot(middle[:, 1024:2048], third[slot])
     return (wide[:, 0:128] + (wide[:, 128:256] + rest)) * scale
@@ -213,7 +261,10 @@
     spread,
     coeffs,
     picks,
-    folded,
+    turn,
+    layers,
+    first,
+    joined,
     second,
     third,
     env_folded,
@@ -330,17 +381,16 @@
     @pl.when(is_worker)
     def _():
         for leg in range(4):
-            row, lane = iota((WIDE, WIDE), 0), iota((WIDE, WIDE), 1)
-            for _ in range(3):
-                lane = jnp.where(lane >= CHI, lane - CHI, lane)
-            select_one[:, leg * WIDE : (leg + 1) * WIDE] = jnp.where(
-                row == 4 * lane + leg, 1.0, 0.0
+            row, lane = iota((WIDE, 128), 0), iota((WIDE, 128), 1)
+            select_one[:, leg * 128 : (leg + 1) * 128] = jnp.where(
+                (row == 4 * lane + leg) & (lane < CHI), 1.0, 0.0
             ).astype(BF16)
             row, lane = iota((128, WIDE), 0), iota((128, WIDE), 1)
             select_two[leg * 128 : (leg + 1) * 128, :] = jnp.where(
                 (lane == 4 * row + leg) & (row < CHI), 1.0, 0.0
             ).astype(BF16)
         picks[...] = layer_picks(legs)
+        turn[...] = basis_turn()
 
     pl.semaphore_wait(
         barrier, 6 * count - 1 + jnp.where(has_next, 1, 0) + jnp.where(has_prev, 1, 0)
@@ -454,25 +504,28 @@
         number = j + way * (count - 1 - 2 * j)
         for kind, target in enumerate((lefts, rights, ketses)):
             arrived(target.at[j], map_recv.at[j, kind])
-        coeffs[...] = layer_rows(ketses[j], picks[...])
-        apart = dot(jnp.concatenate(thirds(lefts[j]), axis=0), select_one[...])
-        for leg in range(4):
-            lanes = slice(leg * WIDE, (leg + 1) * WIDE)
-            spread[leg] = apart[0:CHI, lanes] + (
-                apart[CHI : 2 * CHI, lanes] + apart[2 * CHI : 3 * CHI, lanes]
-            )
+        layers[number] = even_rows(pair_values(ketses[j], picks[...]), turn[...])
+        apart = dot(jnp.concatenate(thirds(lefts[j]), axis=0), select_one[:, 0:512])
+        apart = apart[0:CHI] + (apart[CHI : 2 * CHI] + apart[2 * CHI : 3 * CHI])
+        legs_of = symmetric([apart[:, leg * 128 : (leg + 1) * 128] for leg in range(4)])
+        for leg, tile in enumerate(legs_of):
+            high, mid, lowest = thirds(tile)
+            for index, part in enumerate((high, mid, high, mid, lowest, high)):
+                lanes = slice(index * 128, (index + 1) * 128)
+                first[number, leg * CHI : (leg + 1) * CHI, lanes] = part
         high, mid, lowest = thirds(rights[j])
         main = dot_nt(select_two[...], padded((high, mid)))
         fine = dot_nt(select_two[...], padded((lowest,)))
-        main, fine = main.astype(BF16), fine.astype(BF16)
-        for leg in range(4):
-            rows = slice(leg * 128, (leg + 1) * 128)
+        apart = main[:, 0:128] + (main[:, 128:256] + fine)
+        legs_of = symmetric([apart[leg * 128 : (leg + 1) * 128] for leg in range(4)])
+        for leg, tile in enumerate(legs_of):
+            high, mid, lowest = thirds(tile)
             for copy in range(2):
                 begin = leg * 256 + copy * 128
-                second[number, begin : begin + 128, :] = main[rows]
-            third[number, leg * 256 : leg * 256 + 128, :] = fine[rows]
-            third[number, leg * 256 + 128 : leg * 256 + 256, :] = main[rows, 0:128]
-        fold_first(spread, coeffs, folded, number)
+                second[number, begin : begin + 128, 0:128] = high
+                second[number, begin : begin + 128, 128:256] = mid
+            third[number, leg * 256 : leg * 256 + 128, :] = lowest
+            third[number, leg * 256 + 128 : leg * 256 + 256, :] = high
 
     def side_copy(number, source):
         return remote(
@@ -536,8 +589,9 @@
             def _():
                 arrived(entered, hop_recv)
 
-            for leg, tile in enumerate(unpack(entered[...])):
-                state[leg * CHI : (leg + 1) * CHI, :] = tile
+            came = unpack(entered[...])
+            for leg, (tile, turned) in enumerate(zip(came, symmetric(came))):
+                state[leg * CHI : (leg + 1) * CHI, :] = jnp.where(is_first, turned, tile)
 
         raw = is_first & (number == 0)
         closes = is_last & (number == count - 1)
@@ -545,13 +599,15 @@
         @pl.when(closes)
         def _():
             held = state[...]
-            last_in[...] = pack(tiles_of(held)) * nrm_scale(held)
+            last_in[...] = pack(plain(tiles_of(held))) * nrm_scale(held)
             send_sides(number, last_in)
 
         current = state[...]
         scale = jnp.where(raw, 1.0, nrm_scale(current))
-        renewed = apply_layer(current, scale, folded, second, third, number, middle)
-        normed[number] = pack(tiles_of(current)) * scale
+        renewed = apply_layer(
+            current, scale, first, layers, second, third, number, joined, middle
+        )
+        normed[number] = pack(plain(tiles_of(current))) * scale
         state[...] = renewed
 
         @pl.when(number == count - 1)
@@ -563,7 +619,7 @@
             def _():
                 hop().start()
 
-            normed[count] = leaving[...] * nrm_scale(final)
+            normed[count] = pack(plain(tiles_of(final))) * nrm_scale(final)
 
         @pl.when(jnp.logical_not(closes))
         def _():
@@ -895,7 +951,10 @@
             pltpu.VMEM((4,) + column, F32),
             pltpu.VMEM((64, WIDE), F32),
             pltpu.VMEM((1024, 32), BF16),
-            pltpu.VMEM((most, 16 * CHI, 3 * WIDE), BF16),
+            pltpu.VMEM((256, 256), BF16),
+            pltpu.VMEM((most, 256, 128), F32),
+            pltpu.VMEM((most, WIDE, 768), BF16),
+            pltpu.VMEM((WIDE, 512), F32),
             pltpu.VMEM((most, 1024, 256), BF16),
             pltpu.VMEM((most, 1024, 128), BF16),
             pltpu.VMEM((4, 16 * CHI, 2 * WIDE), BF16),

time: 180 us -> 163 us (0.906)
  Pallas kernels: 168 us -> 152 us
    pallas_call x1, Pallas kernels: 150 us -> 133 us  [run_sweep(): pl.pallas_call(sweep_kernel, out_shape=(jax.ShapeDtypeStruct((2, 2) + col...]
where the time goes in v5:
time: 163 us
  Pallas kernels  152 us (93%)
  local copies, waits for them, and re-layouts  11 us (7%)
    pallas_call x1, Pallas kernels, run_sweep(): pl.pallas_call(sweep_kernel, out_shape=(jax.ShapeDtypeStruct((2, 2) + col...  133 us
    pallas_call x1, Pallas kernels, run_sum(): pl.pallas_call(sum_kernel, out_shape=jax.ShapeDtypeStruct((8, 128), F32),...  17.4 us
    unnamed x20, local copies, waits for them, and re-layouts  7.62 us

profile of v5, /device:TPU:1, one launch (start us, length us, event | category | flops | bytes accessed | tf_op | source)
XLA Modules:
  0.0 163.3 jit_solution(3884627419125422374)
XLA Ops:
  0.6 1.4 broadcast_in_dim.8.kets
  2.0 133.3 %sweep.1 = (f32[2,2,96,384]{3,2,1,0:T(8,128)}, f32[2,5,96,384]{3,2,1,0:T(8,128)}, f32[5,32,128]{2,1,0:T(8,128)}, f32[4,96,384]{2,1,0:T(8,128)}, f32[4,96,384]{2,1,0:T(8,128)}) custom-call(f32[2,32,128]{2,1,0:T(8,128)} %broadcast_in_dim.8.kets, f32[2,1,2,96,384]{4,3,2,1,0:T(8,128)} %left_maps.1, f32[2,1,2,96,384]{4,3,2,1,0:T(8,128)} %right_maps.1, ...), custom_call_target="tpu_custom_call" | custom-call | tf_op jit(solution)/shard_map/sweep/pallas_call | solution.py:934
  135.4 0.0 copy-start
  135.4 1.4 copy-done
  136.7 0.0 copy-start.1
  136.7 1.1 copy-done.1
  137.8 0.0 copy-start.2
  137.8 1.1 copy-done.2
  138.9 0.0 copy-start.3
  138.9 0.9 copy-done.3
  139.7 0.0 copy-start.5
  139.7 0.7 copy-done.5
  140.4 0.0 copy-start.6
  140.4 0.7 copy-done.6
  141.1 0.0 copy-start.7
  141.1 0.7 copy-done.7
  141.7 0.7 copy-done.8
  142.4 0.9 energies.1.shares
  143.3 0.0 copy-start.4
  143.3 0.6 copy-done.4
  143.9 17.4 %shares_sum.1 = f32[8,128]{1,0:T(8,128)} custom-call(f32[8,128]{1,0:T(8,128)} %copy-done.4), custom_call_target="tpu_custom_call" | custom-call | tf_op jit(solution)/shard_map/shares_sum/pallas_call | solution.py:1288
  161.3 1.2 slice_bitcast_fusion
  162.5 0.0 copy-done.9
  162.5 0.9 fusion
  (2 shorter events, 0.0 us)
Async XLA Ops:
  135.4 1.4 copy-start
  136.7 1.1 copy-start.1
  137.8 1.1 copy-start.2
  138.9 0.9 copy-start.3
  139.7 0.7 copy-start.5
  140.4 0.7 copy-start.6
  141.1 0.7 copy-start.7
  141.7 0.7 copy-start.8
  142.4 20.1 %copy-start.9 = (f32[2,2,96,384]{3,2,1,0:T(8,128)S(1)}, f32[2,2,96,384]{3,2,1,0:T(8,128)}, u32[]{:S(2)}) copy-start(f32[2,2,96,384]{3,2,1,0:T(8,128)} %get-tuple-element.8) | copy-start | bytes 1769476
  143.3 0.6 copy-start.4

commit v6 on v5

--- a/solution.py
+++ b/solution.py
@@ -397,7 +397,7 @@
     )
 
     def chain(index):
-        to_way = (index // 2 + jnp.where(z == end, 1, 0)) % 2
+        to_way = (index // 2 + mirror) % 2
         to_col = index % 2
         to_start = ((to_way == 0) & (z == 0)) | ((to_way == 1) & (z == end))
         to_core = jnp.where(at_edge, jnp.where(to_start, 1, 0), 1)
@@ -441,7 +441,12 @@
 
         return carried
 
-    lax.fori_loop(0, 4, send_map, 0)
+    def send_rest():
+        lax.fori_loop(0, 2, map_sent, 0)
+        lax.fori_loop(2, 4, send_map, 0)
+
+    on_early = is_worker & (way == mirror)
+    lax.fori_loop(0, 2, send_map, 0)
 
     half = pl.ds(2 * xh, 2)
     at_home = (core == xl) & (xl == xh)
@@ -809,10 +814,19 @@
             over(number).start()
 
 
+    @pl.when(jnp.logical_not(on_early))
+    def _():
+        send_rest()
+
+    turn_at = jnp.where(at_edge, 4, 1)
     total = jnp.where(is_worker, 2 * count, 0)
     before_fold = jnp.where(is_late, count, total)
 
     def task(index, carried):
+        @pl.when(on_early & (index == turn_at))
+        def _():
+            send_rest()
+
         folds = (index >= before_fold) & (index < before_fold + 4)
         on_env = index >= total + 4
         on_boundary = jnp.logical_not(folds) & jnp.logical_not(on_env)
@@ -849,7 +863,7 @@
     lax.fori_loop(0, total + 12, task, 0)
 
 
-    lax.fori_loop(0, 4, map_sent, 0)
+    lax.fori_loop(2, 4, map_sent, 0)
 
     @pl.when(has_next)
     def _():
@@ -1200,7 +1214,7 @@
             pltpu.VMEM((CHI, WIDE), F32),
             pltpu.SemaphoreType.DMA((4,)),
         ],
-        compiler_params=pltpu.CompilerParams(vmem_limit_bytes=32 * 1024 * 1024),
+        compiler_params=pltpu.CompilerParams(vmem_limit_bytes=67043328),
         name="energies",
     )(term_rows, term_bonds, term_ops, operators, sides, row_kets, lefts, rights)
 
@@ -1273,7 +1287,7 @@
     added = None
     for other in range(16):
         added = plane_in[other] if added is None else added + plane_in[other]
-    total[...] = added
+    total[...] = added[0:1, 0:TERMS]
 
     @pl.when(way == 0)
     def _():
@@ -1287,7 +1301,7 @@
     vmem = pl.BlockSpec(memory_space=pltpu.VMEM)
     return pl.pallas_call(
         sum_kernel,
-        out_shape=jax.ShapeDtypeStruct((8, 128), F32),
+        out_shape=jax.ShapeDtypeStruct((1, TERMS), F32),
         in_specs=[vmem],
         out_specs=vmem,
         scratch_shapes=[
@@ -1299,7 +1313,9 @@
             pltpu.SemaphoreType.DMA((32,)),
             pltpu.SemaphoreType.DMA((16,)),
         ],
-        compiler_params=pltpu.CompilerParams(collective_id=2, has_side_effects=True),
+        compiler_params=pltpu.CompilerParams(
+            collective_id=2, has_side_effects=True, vmem_limit_bytes=67043328
+        ),
         name="shares_sum",
     )(shares)
 
@@ -1324,7 +1340,7 @@
     shares = run_energies(
         term_rows, term_bonds, term_ops, operators, sides, row_kets, lefts, rights
     )
-    energies = run_sum(shares)[0, :TERMS]
+    energies = run_sum(shares).reshape(TERMS)
     return (outs[0][None], outs[1][None], energies)
 
 

time: 163 us -> 162 us (level); the launches traced: 163 us -> 159 us
  local copies, waits for them, and re-layouts: 11 us -> 4.41 us
  Pallas kernels: 152 us -> 154 us
    unnamed x20 -> x1, local copies, waits for them, and re-layouts: 7.62 us -> 1.14 us
where the time goes in v6:
time: 162 us; the launch traced here: 159 us
  Pallas kernels  154 us (95%)
  local copies, waits for them, and re-layouts  4.41 us (3%)
    pallas_call x1, Pallas kernels, run_sweep(): pl.pallas_call(sweep_kernel, out_shape=(jax.ShapeDtypeStruct((2, 2) + col...  134 us
    pallas_call x1, Pallas kernels, run_sum(): pl.pallas_call(sum_kernel, out_shape=jax.ShapeDtypeStruct((1, TERMS), F32...  18.6 us

profile of v6, /device:TPU:1, one launch (start us, length us, event | category | flops | bytes accessed | tf_op | source)
XLA Modules:
  0.0 159.0 jit_solution(13872611940065712826)
XLA Ops:
  0.6 1.4 broadcast_in_dim.8.kets
  2.0 133.7 %sweep.1 = (f32[2,2,96,384]{3,2,1,0:T(8,128)}, f32[2,5,96,384]{3,2,1,0:T(8,128)}, f32[5,32,128]{2,1,0:T(8,128)}, f32[4,96,384]{2,1,0:T(8,128)}, f32[4,96,384]{2,1,0:T(8,128)}) custom-call(f32[2,32,128]{2,1,0:T(8,128)} %broadcast_in_dim.8.kets, f32[2,1,2,96,384]{4,3,2,1,0:T(8,128)} %left_maps.1, f32[2,1,2,96,384]{4,3,2,1,0:T(8,128)} %right_maps.1, ...), custom_call_target="tpu_custom_call" | custom-call | tf_op jit(solution)/shard_map/sweep/pallas_call | solution.py:948
  135.7 1.6 energies.1.shares
  137.3 18.6 %shares_sum.1 = f32[1,16]{1,0:T(1,128)} custom-call(f32[8,128]{1,0:T(8,128)} %energies.1.shares), custom_call_target="tpu_custom_call" | custom-call | tf_op jit(solution)/shard_map/shares_sum/pallas_call | solution.py:1302
  155.9 1.9 %fusion = (f32[1,2,96,384]{3,2,1,0:T(8,128)}, f32[1,2,96,384]{3,2,1,0:T(8,128)}) fusion(f32[2,2,96,384]{3,2,1,0:T(8,128)} %get-tuple-element.8), kind=kLoop, calls=%fused_computation | loop fusion | bytes 1179648 | tf_op jit(solution)/shard_map/slice | solution.py:1344
  157.8 1.1 copy.15

commit v7 on v6

--- a/solution.py
+++ b/solution.py
@@ -241,7 +241,7 @@
 
 
 def sweep_kernel(
-    kets,
+    own_kets,
     left_maps,
     right_maps,
     top_edge,
@@ -253,6 +253,7 @@
     row_kets,
     from_left,
     from_right,
+    kets,
     lefts,
     rights,
     ketses,
@@ -375,6 +376,13 @@
     def _():
         greet(before)
 
+    for local in range(2):
+        chosen = iota((32, 32), 0) == iota((32, 32), 1)
+        spaced = jnp.where(chosen, own_kets[local : local + 1, :], 0.0)
+        ones = jnp.ones((32, 128), BF16)
+        high, mid, lowest = (dot(part, ones) for part in thirds(spaced))
+        kets[local] = high + (mid + lowest)
+
     def legs(m, g, o, f):
         return pick(way, m, o), f, pick(way, o, m), g
 
@@ -587,7 +595,7 @@
     def tiles_of(value):
         return [value[leg * CHI : (leg + 1) * CHI] for leg in range(4)]
 
-    def advance(number):
+    def advance(number, carried):
         @pl.when(number == 0)
         def _():
             @pl.when(has_prev)
@@ -633,6 +641,8 @@
         @pl.when(number == count - 1)
         def _():
             lax.fori_loop(0, count, send_out, 0)
+
+        return carried
 
 
     def column_at(number):
@@ -839,7 +849,9 @@
 
         @pl.when(on_boundary & jnp.logical_not(prepares))
         def _():
-            advance(jnp.where(is_first, step // 2, jnp.clip(step - count, 0, count - 1)))
+            begin = jnp.where(is_first, step // 2, 0)
+            stop = jnp.where(is_first, begin + 1, jnp.where(step == count, count, 0))
+            lax.fori_loop(begin, stop, advance, 0)
 
         @pl.when(folds)
         def _():
@@ -957,6 +969,7 @@
         in_specs=[vmem, anywhere, anywhere] + [vmem] * 4,
         out_specs=(vmem,) * 5,
         scratch_shapes=[
+            pltpu.VMEM((2, 32, 128), F32),
             pltpu.VMEM((most,) + column, F32),
             pltpu.VMEM((most,) + column, F32),
             pltpu.VMEM((most, 32, 128), F32),
@@ -1333,9 +1346,8 @@
     term_ops,
     operators,
 ):
-    spread_kets = jnp.broadcast_to(kets[0][:, :, None], (kets.shape[1], 32, 128))
     outs, sides, row_kets, lefts, rights = run_sweep(
-        spread_kets, left_maps, right_maps, top_edge, bottom_edge, left_edge, right_edge
+        kets[0], left_maps, right_maps, top_edge, bottom_edge, left_edge, right_edge
     )
     shares = run_energies(
         term_rows, term_bonds, term_ops, operators, sides, row_kets, lefts, rights

time: 162 us -> 161 us (level)
  Pallas kernels: 154 us -> 156 us
    pallas_call x1, Pallas kernels: 18.6 us -> 21.9 us  [run_sum(): pl.pallas_call(sum_kernel, out_shape=jax.ShapeDtypeStruct((1, TERMS), F32...]
where the time goes in v7:
time: 161 us; the launch traced here: 159 us
  Pallas kernels  156 us (97%)
  local copies, waits for them, and re-layouts  3.04 us (2%)
    pallas_call x1, Pallas kernels, run_sweep(): pl.pallas_call(sweep_kernel, out_shape=(jax.ShapeDtypeStruct((2, 2) + col...  132 us
    pallas_call x1, Pallas kernels, run_sum(): pl.pallas_call(sum_kernel, out_shape=jax.ShapeDtypeStruct((1, TERMS), F32...  21.9 us

profile of v7, /device:TPU:1, one launch (start us, length us, event | category | flops | bytes accessed | tf_op | source)
XLA Modules:
  0.0 159.3 jit_solution(10412906619316192426)
XLA Ops:
  0.6 132.2 %sweep.1 = (f32[2,2,96,384]{3,2,1,0:T(8,128)}, f32[2,5,96,384]{3,2,1,0:T(8,128)}, f32[5,32,128]{2,1,0:T(8,128)}, f32[4,96,384]{2,1,0:T(8,128)}, f32[4,96,384]{2,1,0:T(8,128)}) custom-call(f32[2,32]{1,0:T(2,128)} %bitcast.2, f32[2,1,2,96,384]{4,3,2,1,0:T(8,128)} %left_maps.1, f32[2,1,2,96,384]{4,3,2,1,0:T(8,128)} %right_maps.1, f32[2,96,384]{2,1,0:T(8,128)} %top_edge.1, ...), custom_call_target="tpu_custom_call" | custom-call | tf_op jit(solution)/shard_map/sweep/pallas_call | solution.py:960
  132.8 1.6 energies.1.shares
  134.4 21.9 %shares_sum.1 = f32[1,16]{1,0:T(1,128)} custom-call(f32[8,128]{1,0:T(8,128)} %energies.1.shares), custom_call_target="tpu_custom_call" | custom-call | tf_op jit(solution)/shard_map/shares_sum/pallas_call | solution.py:1315
  156.3 1.9 %fusion = (f32[1,2,96,384]{3,2,1,0:T(8,128)}, f32[1,2,96,384]{3,2,1,0:T(8,128)}) fusion(f32[2,2,96,384]{3,2,1,0:T(8,128)} %get-tuple-element.8), kind=kLoop, calls=%fused_computation | loop fusion | bytes 1179648 | tf_op jit(solution)/shard_map/slice | solution.py:1356
  158.2 1.1 copy.15
